TPU v7x, 128 devices: a whole 4x4x4 slice. The times are simulated.
128 devices in a mesh: pts: 16 (over y, z_lo, core), freq: 8 (over z_hi, x).
Axes of the slice: x: 4, y: 4, z: 4 (z_hi: 2, z_lo: 2; z = z_hi * 2 + z_lo), core: 2. Of those that a mesh axis runs over, the one named last changes fastest.
Arguments:
- spectra: bfloat16 [128, 2, 32, 32768], P('freq', None, None, 'pts'), may hold values from -6 to 6
- weights: float32 [32768], P('pts'), may hold values from 0.25 to 4
- triads: int32 [128, 2], replicated, may hold values from 0 to 127, as said below
Outputs:
- bispectrum: float32 [128, 2, 32, 32], P('freq')
- density: float32 [128, 2, 32, 32], P('freq')
- vectors: float32 [128, 2, 32], P('freq')
- energy: float32 [128], P('freq')
- mode_fields: float32 [128, 2, 32768], P('freq', None, 'pts')
Inputs may be any that keep to these rules, and one draw needn't show every extreme that they name: Row t holds (k, l) of triad t. The triads of group g, rows g * 16 to (g + 1) * 16 - 1, have k within the group's own frequencies g * 16 to (g + 1) * 16 - 1. The l of exactly 2 triads of each group lie in each group's frequency range. Among the 32 frequencies l and (k + l) mod 128 of one group's triads, at most 6 lie in any one group's range, and in every group some range holds exactly 6.
All inputs are finite; a program needn't handle non-finite values.
Results may differ from a plain program's by a relative error of at most 0.0052.
Values may be sent and summed in bfloat16 or wider, within the bound.
No kernel may reach another device: no remote copies, remote signals or barrier semaphores. Data moves between devices by JAX's collectives and lax.ppermute only.
A program may use at most 128 MiB of HBM per device.

v0:
```python
import math

import jax
import jax.numpy as jnp
from jax import lax
from jax.sharding import PartitionSpec as P

ITERS = 3


highest = lax.Precision.HIGHEST


def cut_along(value, dim, length):
    before, after = (value.shape[:dim], value.shape[dim + 1 :])
    return jnp.moveaxis(value.reshape(*before, length, -1, *after), dim, 0)


def piece_ends(length, count):
    unit = 8 if length >= 8 * count else 1
    return [length // unit * k // count * unit for k in range(1, count)]


def joined_along(pieces, dim):
    dims = list(pieces.shape[1:])
    dims[dim] *= pieces.shape[0]
    return jnp.moveaxis(pieces, 0, dim).reshape(dims)


def cut_exchange(value, axis, pieces, split_dim, concat_dim):
    blocks = cut_along(value, split_dim, lax.axis_size(axis))
    cut = max(range(1, max(2, blocks.ndim - 1)), key=lambda d: blocks.shape[d])
    gathered = []
    for slab in jnp.split(blocks, piece_ends(blocks.shape[cut], pieces), axis=cut):
        if slab.size:
            gathered.append(lax.all_to_all(slab, axis, split_axis=0, concat_axis=0, tiled=True))
    return joined_along(jnp.concatenate(gathered, axis=cut), concat_dim)


def sent_to_all(value, axis):
    length = lax.axis_size(axis)
    return lax.all_to_all(
        jnp.broadcast_to(value[None], (length, *value.shape)), axis, 0, 0, tiled=True
    )


def of_everyone(value, axis):
    everything = sent_to_all(value, axis)
    return jnp.sum(everything, axis=0)


def packed_total(arrays, axis):
    ends = [0]
    for a in arrays:
        ends.append(ends[-1] + a.size)
    total = of_everyone(jnp.concatenate([a.ravel() for a in arrays]), axis)
    return tuple((total[b:e].reshape(a.shape) for a, b, e in zip(arrays, ends, ends[1:])))


def block_gram(left, right):
    half_rows = left.shape[2]
    lead_dims = left.shape[:1]
    flat_left = left.reshape(lead_dims + (2 * half_rows, left.shape[3]))
    flat_right = right.reshape(lead_dims + (2 * half_rows, right.shape[3]))
    joined = jnp.einsum("tap,tbp->tab", flat_left, flat_right, preferred_element_type=jnp.float32)
    real_part = joined[:, :half_rows, :half_rows] + joined[:, half_rows:, half_rows:]
    imag_part = joined[:, :half_rows, half_rows:] - joined[:, half_rows:, :half_rows]
    return jnp.stack([real_part, imag_part], axis=1)


def weighted_product(first_rows, second_rows, weights):
    first_real = first_rows[:, 0].astype(jnp.float32)
    first_imag = first_rows[:, 1].astype(jnp.float32)
    second_real = second_rows[:, 0].astype(jnp.float32)
    second_imag = second_rows[:, 1].astype(jnp.float32)
    prod_real = first_real * second_real - first_imag * second_imag
    prod_imag = first_real * second_imag + first_imag * second_real
    return (jnp.stack([prod_real, prod_imag], axis=1) * weights).astype(jnp.bfloat16)


def apply_matrix(matrix, vector):
    return jnp.einsum("...ab,...b->...a", matrix, vector, precision=highest)


def apply_adjoint(matrix, vector):
    return jnp.einsum("...ba,...b->...a", matrix, vector, precision=highest)


def power_iteration(bispec):
    real_mat = bispec[..., 0, :, :]
    imag_mat = bispec[..., 1, :, :]
    order = real_mat.shape[-1]
    vec_real = jnp.full(real_mat.shape[:-1], 1.0 / math.sqrt(order), jnp.float32)
    vec_imag = jnp.zeros(real_mat.shape[:-1], jnp.float32)
    for sweep_index in range(ITERS):
        out_real = apply_matrix(real_mat, vec_real) - apply_matrix(imag_mat, vec_imag)
        out_imag = apply_matrix(real_mat, vec_imag) + apply_matrix(imag_mat, vec_real)
        back_real = apply_adjoint(real_mat, out_real) + apply_adjoint(imag_mat, out_imag)
        back_imag = apply_adjoint(real_mat, out_imag) - apply_adjoint(imag_mat, out_real)
        factor = 1.0 / jnp.sqrt(
            jnp.sum(back_real * back_real + back_imag * back_imag, axis=-1) + 1.0
        )
        vec_real = back_real * factor[..., None]
        vec_imag = back_imag * factor[..., None]
    out_real = apply_matrix(real_mat, vec_real) - apply_matrix(imag_mat, vec_imag)
    out_imag = apply_matrix(real_mat, vec_imag) + apply_matrix(imag_mat, vec_real)
    top_part = jnp.sum(out_real * out_real + out_imag * out_imag, axis=-1)
    bottom_part = order * (jnp.sum(vec_real * vec_real + vec_imag * vec_imag, axis=-1) + 1.0)
    return (jnp.stack([vec_real, vec_imag], axis=-2), top_part / bottom_part)


def fetch_slots(spectra, triads, group_index, freq_count, f_dev, per_group):
    freq_total = f_dev * freq_count
    cap_rows = 3 * per_group // freq_count
    need_count = 2 * per_group
    freq_first = triads[:, 0]
    freq_second = triads[:, 1]
    wanted = jnp.stack([freq_second, (freq_first + freq_second) % freq_total], axis=1).reshape(
        freq_count, need_count
    )
    owners = wanted // f_dev
    earlier = lax.broadcasted_iota(jnp.int32, (need_count, need_count), 1) < lax.broadcasted_iota(
        jnp.int32, (need_count, need_count), 0
    )
    same_owner = owners[:, :, None] == owners[:, None, :]
    slot_rank = jnp.sum(jnp.where(same_owner & earlier[None], 1, 0), axis=2).astype(jnp.int32)
    slot_ids = lax.broadcasted_iota(jnp.int32, (1, cap_rows, 1), 1)
    chosen = (owners[:, None, :] == group_index) & (slot_rank[:, None, :] == slot_ids)
    local_row = wanted - group_index * f_dev
    row_index = jnp.sum(jnp.where(chosen, local_row[:, None, :], 0), axis=2)
    outgoing = jnp.take(spectra, row_index.reshape(-1), axis=0).reshape(
        (freq_count, cap_rows) + spectra.shape[1:]
    )
    incoming = cut_exchange(outgoing, "freq", 2, 0, 0)
    flat_rows = incoming.reshape((freq_count * cap_rows,) + spectra.shape[1:])
    own_owner = lax.dynamic_index_in_dim(owners, group_index, 0, keepdims=False)
    own_slot = lax.dynamic_index_in_dim(slot_rank, group_index, 0, keepdims=False)
    picked = jnp.take(flat_rows, own_owner * cap_rows + own_slot, axis=0)
    return (picked[0::2], picked[1::2])


def local(spectra, weights, triads):
    freq_count = lax.axis_size("freq")
    group_index = lax.axis_index("freq")
    f_dev = spectra.shape[0]
    blocks = spectra.shape[2]
    per_group = triads.shape[0] // freq_count
    point_count = spectra.shape[3] * lax.axis_size("pts")
    own_triads = lax.dynamic_slice_in_dim(triads, group_index * per_group, per_group, 0)
    k_mine = own_triads[:, 0]
    first_rows = jnp.take(spectra, k_mine - group_index * f_dev, axis=0)
    second_rows, third_rows = fetch_slots(
        spectra, triads, group_index, freq_count, f_dev, per_group
    )
    weighted_spectra = (spectra.astype(jnp.float32) * weights).astype(jnp.bfloat16)
    density_part = block_gram(weighted_spectra, spectra)
    bis_part = block_gram(weighted_product(first_rows, second_rows, weights), third_rows)
    bis_scale = 1.0 / math.sqrt(blocks * point_count)
    dens_scale = 1.0 / point_count
    bis_total, dens_total = packed_total((bis_part, density_part), "pts")
    bispectrum = bis_total * bis_scale
    density = dens_total * dens_scale
    vectors, energy = power_iteration(bispectrum)
    vector_low = vectors.astype(jnp.bfloat16)
    mixed = jnp.einsum("tcbp,tdb->tcdp", third_rows, vector_low, preferred_element_type=jnp.float32)
    mode_fields = jnp.stack(
        [mixed[:, 0, 0] - mixed[:, 1, 1], mixed[:, 0, 1] + mixed[:, 1, 0]], axis=1
    )
    return (bispectrum, density, vectors, energy, mode_fields)


def solution(mesh):
    in_specs = (P("freq", None, None, "pts"), P("pts"), P())
    out_specs = (
        P("freq", None, None, None),
        P("freq", None, None, None),
        P("freq", None, None),
        P("freq"),
        P("freq", None, "pts"),
    )
    return jax.shard_map(local, mesh=mesh, in_specs=in_specs, out_specs=out_specs, check_vma=False)
```

profile of v0, /device:TPU:6, one launch (start us, length us, event | category | flops | bytes accessed | tf_op | source)
XLA Modules:
  0.0 318.0 jit_solution(12975256829402804548)
XLA Ops:
  0.7 0.8 fusion.52
  1.7 0.3 select_reduce_fusion
  2.0 0.2 select_reduce_fusion.1
  2.4 8.5 %gather_fusion.1 = bf16[48,2,32,2048]{3,2,1,0:T(8,128)(2,1)} fusion(bf16[16,2,32,2048]{3,2,1,0:T(8,128)(2,1)} %param.3, s32[1024]{0:T(1024)S(1)} %pad_clamp_fusion.1), kind=kCustom, calls=%fused_computation.1 | custom fusion | bytes 25166016 | tf_op jit(solution)/shard_map/jit(_take)/gather | solution.py:131
  10.9 6.5 %broadcast_select_fusion = bf16[8,1,6,2,32,2048]{5,4,3,2,1,0:T(8,128)(2,1)S(1)} fusion(bf16[8,1,6,2,32,2048]{5,4,3,2,1,0:T(8,128)(2,1)} %bitcast.216, pred[8,6]{1,0:T(8,128)(4,1)S(1)} %copy.32), kind=kLoop, calls=%fused_computation.4 | loop fusion | flops 6291456 | bytes 25165872 | tf_op jit(solution)/shard_map/jit(_take)/select_n | solution.py:131
  17.5 3.8 %fusion.50 = (bf16[8,1,6,2,16,2048]{5,4,3,2,1,0:T(8,128)(2,1)S(1)}, bf16[8,1,6,2,16,2048]{5,4,3,2,1,0:T(8,128)(2,1)}) fusion(bf16[8,1,6,2,32,2048]{5,4,3,2,1,0:T(8,128)(2,1)S(1)} %broadcast_select_fusion), kind=kLoop, calls=%fused_computation.124 | loop fusion | bytes 25165824 | tf_op jit(solution)/shard_map/split | solution.py:34
  21.3 80.1 %all_to_all.16 = bf16[8,1,6,2,16,2048]{5,4,3,2,1,0:T(8,128)(2,1)} all-to-all(bf16[8,1,6,2,16,2048]{5,4,3,2,1,0:T(8,128)(2,1)S(1)} %get-tuple-element.23), channel_id=1, replica_groups=mesh['pts'=16,'freq'=8] {'freq'}, dimensions={0} | all-to-all | bytes 12582912 | tf_op jit(solution)/shard_map/all_to_all | solution.py:36
  101.5 6.5 %all-to-all-start.1 = ((bf16[8,1,6,2,16,2048]{5,4,3,2,1,0:T(8,128)(2,1)}), bf16[8,1,6,2,16,2048]{5,4,3,2,1,0:T(8,128)(2,1)}, u32[]{:S(2)}, u32[]{:S(2)}) async-start(bf16[8,1,6,2,16,2048]{5,4,3,2,1,0:T(8,128)(2,1)} %get-tuple-element.24), calls=%async_computation.1 | async-start | bytes 12582912 | tf_op jit(solution)/shard_map/all_to_all | solution.py:36
  108.1 5.0 %gather_fusion = bf16[16,2,32,2048]{3,2,1,0:T(8,128)(2,1)} fusion(bf16[16,2,32,2048]{3,2,1,0:T(8,128)(2,1)} %param.3, s32[1024]{0:T(1024)S(1)} %pad_clamp_fusion.2), kind=kCustom, calls=%fused_computation | custom fusion | bytes 8388672 | tf_op jit(solution)/shard_map/jit(_take)/gather | solution.py:151
  113.1 3.4 %multiply_convert_fusion = bf16[16,2,32,2048]{3,2,1,0:T(8,128)(2,1)S(1)} fusion(bf16[16,2,32,2048]{3,2,1,0:T(8,128)(2,1)} %param.3, f32[2048]{0:T(1024)S(1)} %copy-done.4), kind=kLoop, calls=%fused_computation.8 | loop fusion | flops 6291456 | bytes 8396800 | tf_op jit(solution)/shard_map/convert_element_type | solution.py:155
  116.5 1.2 fusion.54
  117.8 0.2 fusion.4
  118.1 0.2 reshape.290
  118.3 4.6 %broadcast_select_fusion.2 = bf16[16,2,32,2048]{3,2,1,0:T(8,128)(2,1)} fusion(bf16[16,2,32,2048]{3,2,1,0:T(8,128)(2,1)} %gather_fusion, pred[16]{0:T(512)(128)(4,1)S(1)} %get-tuple-element.17), kind=kLoop, calls=%fused_computation.16 | loop fusion | flops 2097152 | bytes 8388624 | tf_op jit(solution)/shard_map/jit(_take)/select_n | solution.py:151
  122.9 74.1 %all-to-all-done.1 = bf16[8,1,6,2,16,2048]{5,4,3,2,1,0:T(8,128)(2,1)} async-done(((bf16[8,1,6,2,16,2048]{5,4,3,2,1,0:T(8,128)(2,1)}), bf16[8,1,6,2,16,2048]{5,4,3,2,1,0:T(8,128)(2,1)}, u32[]{:S(2)}, u32[]{:S(2)}) %all-to-all-start.1) | async-done | bytes 6291488 | tf_op jit(solution)/shard_map/all_to_all | solution.py:36
  197.0 10.7 %pad_maximum_fusion = bf16[8,1,6,2,32,2048]{5,4,3,2,1,0:T(8,128)(2,1)} fusion(bf16[8,1,6,2,16,2048]{5,4,3,2,1,0:T(8,128)(2,1)} %all-to-all-done.1, bf16[8,1,6,2,16,2048]{5,4,3,2,1,0:T(8,128)(2,1)} %all_to_all.16), kind=kLoop, calls=%fused_computation.3 | loop fusion | flops 25165824 | bytes 25165824 | tf_op jit(solution)/shard_map/concatenate | solution.py:37
  207.7 9.6 %gather_fusion.2 = bf16[32,2,32,2048]{3,2,1,0:T(8,128)(2,1)} fusion(bf16[48,2,32,2048]{3,2,1,0:T(8,128)(2,1)} %bitcast.217, s32[1024]{0:T(1024)S(1)} %pad_clamp_fusion), kind=kCustom, calls=%fused_computation.2 | custom fusion | bytes 16777344 | tf_op jit(solution)/shard_map/jit(_take)/gather | solution.py:138
  217.3 7.5 %broadcast_select_fusion.1 = bf16[32,2,32,2048]{3,2,1,0:T(8,128)(2,1)} fusion(bf16[32,2,32,2048]{3,2,1,0:T(8,128)(2,1)} %gather_fusion.2, pred[32]{0:T(512)(128)(4,1)S(1)} %get-tuple-element.19), kind=kLoop, calls=%fused_computation.9 | loop fusion | flops 4194304 | bytes 16777248 | tf_op jit(solution)/shard_map/jit(_take)/select_n | solution.py:138
  224.7 4.0 %fusion.51 = (bf16[16,2,32,2048]{3,2,1,0:T(8,128)(2,1)S(1)}, bf16[16,2,32,2048]{3,2,1,0:T(8,128)(2,1)S(1)}) fusion(bf16[32,2,32,2048]{3,2,1,0:T(8,128)(2,1)} %broadcast_select_fusion.1), kind=kLoop, calls=%fused_computation.125 | loop fusion | bytes 16777216 | tf_op jit(solution)/shard_map/slice | solution.py:139
  228.8 0.6 copy-done.2
  229.4 1.7 fusion.1
  231.1 1.1 pad_maximum_fusion.1
  232.2 1.3 fusion
  233.5 1.2 fusion.53
  234.7 0.2 fusion.6
  235.2 3.2 %broadcast_in_dim.86 = f32[16,1,65536]{2,1,0:T(1,128)S(1)} broadcast(f32[65536]{0:T(1024)S(1)} %pad_maximum_fusion.4), dimensions={2} | broadcast | bytes 4456448 | tf_op jit(solution)/shard_map/broadcast_in_dim | solution.py:43
  238.5 55.1 %all_to_all.17 = f32[16,1,65536]{2,1,0:T(1,128)} all-to-all(f32[16,1,65536]{2,1,0:T(1,128)S(1)} %broadcast_in_dim.86), channel_id=1, replica_groups=mesh['pts'=16,'freq'=8] {'pts'}, dimensions={0} | all-to-all | bytes 8388608 | tf_op jit(solution)/shard_map/all_to_all | solution.py:42
  293.5 4.9 %reduce_sum.74 = f32[65536]{0:T(1024)S(1)} reduce(f32[16,1,65536]{2,1,0:T(1,128)} %all_to_all.17, f32[]{:T(128)} %constant.92.clone.1), dimensions={0,1}, to_apply=%region_2.3 | reduce | flops 983040 | bytes 4456452 | tf_op jit(solution)/shard_map/reduce_sum | solution.py:49
  298.5 0.2 mul.161
  298.7 0.5 fusion.37
  299.2 0.5 fusion.21
  299.7 0.5 fusion.23
  300.3 0.5 fusion.36
  300.8 0.4 fusion.20
  301.1 0.3 fusion.35
  301.5 0.3 fusion.34
  301.9 0.3 fusion.22
  302.4 0.5 fusion.19
  302.9 0.5 fusion.32
  303.5 0.5 fusion.33
  304.0 0.5 fusion.17
  304.5 0.4 fusion.16
  304.9 0.3 fusion.31
  305.2 0.3 fusion.30
  305.6 0.3 fusion.18
  306.1 0.5 fusion.15
  306.7 0.5 fusion.28
  307.2 0.5 fusion.29
  307.7 0.5 fusion.13
  308.3 0.4 fusion.12
  308.6 0.3 fusion.27
  309.0 0.3 fusion.26
  309.3 0.3 fusion.14
  309.8 0.2 add_reduce_fusion
  310.0 2.9 convolution_bitcast_fusion
  312.9 0.2 fusion.7
  313.1 0.2 fusion.9
  313.3 0.5 fusion.11
  313.8 0.5 fusion.24
  314.4 0.5 fusion.25
  314.9 0.5 fusion.10
  315.4 1.0 mul.164
  316.4 0.9 pad_maximum_fusion.5
  317.5 0.5 multiply_divide_fusion
  (54 shorter events, 1.7 us)
Async XLA Ops:
  101.5 6.5 %copy-start.5 = (s32[128,2]{0,1:T(2,128)S(1)}, s32[128,2]{0,1:T(2,128)}, u32[]{:S(2)}) copy-start(s32[128,2]{0,1:T(2,128)} %param.5) | copy-start | bytes 3076
  101.5 95.6 %all-to-all-start.1 = ((bf16[8,1,6,2,16,2048]{5,4,3,2,1,0:T(8,128)(2,1)}), bf16[8,1,6,2,16,2048]{5,4,3,2,1,0:T(8,128)(2,1)}, u32[]{:S(2)}, u32[]{:S(2)}) async-start(bf16[8,1,6,2,16,2048]{5,4,3,2,1,0:T(8,128)(2,1)} %get-tuple-element.24), calls=%async_computation.1 | async-start | bytes 12582912 | tf_op jit(solution)/shard_map/all_to_all | solution.py:36
  108.1 5.0 %copy-start.4 = (f32[2048]{0:T(1024)S(1)}, f32[2048]{0:T(1024)}, u32[]{:S(2)}) copy-start(f32[2048]{0:T(1024)} %param.4) | copy-start | bytes 24580
  113.1 3.5 %copy-start = (bf16[16,2,32,2048]{3,2,1,0:T(8,128)(2,1)S(1)}, bf16[16,2,32,2048]{3,2,1,0:T(8,128)(2,1)}, u32[]{:S(2)}) copy-start(bf16[16,2,32,2048]{3,2,1,0:T(8,128)(2,1)} %param.3) | copy-start | bytes 12582916
  224.7 4.7 %copy-start.2 = (bf16[16,2,32,2048]{3,2,1,0:T(8,128)(2,1)S(1)}, bf16[16,2,32,2048]{3,2,1,0:T(8,128)(2,1)}, u32[]{:S(2)}) copy-start(bf16[16,2,32,2048]{3,2,1,0:T(8,128)(2,1)} %broadcast_select_fusion.2) | copy-start | bytes 12582916
  298.6 16.2 %copy-start.1 = (f32[16,2,32,32]{3,2,1,0:T(8,128)}, f32[16,2,32,32]{3,2,1,0:T(8,128)S(1)}, u32[]{:S(2)}) copy-start(f32[16,2,32,32]{3,2,1,0:T(8,128)S(1)} %mul.161) | copy-start | bytes 393220
  310.0 8.0 %copy-start.3 = (f32[16,2,32]{2,1,0:T(2,128)}, f32[16,2,32]{2,1,0:T(2,128)S(1)}, u32[]{:S(2)}) copy-start(f32[16,2,32]{2,1,0:T(2,128)S(1)} %pad_maximum_fusion.6) | copy-start | bytes 12292
where the time goes:
time: 319 us; the launch traced here: 318 us
  blocking collectives  135 us (42%)
  waiting for transfers between devices  74.1 us (23%)
  other arithmetic  46.3 us (15%)
  local copies, waits for them, and re-layouts  36.9 us (12%)
  matrix products  17.9 us (6%)
  starting transfers between devices  6.53 us (2%)
    all_to_all x1, blocking collectives, cut_exchange(): lax.all_to_all(slab, axis, split_axis=0, concat_axis=0, tiled=True)  80.1 us
    all_to_all x1, waiting for transfers between devices, cut_exchange(): lax.all_to_all(slab, axis, split_axis=0, concat_axis=0, tiled=True)  74.1 us
    all_to_all x1, blocking collectives, sent_to_all(): lax.all_to_all(jnp.broadcast_to(value[None], (length, *value.shape)), axi...  55.1 us
    concatenate x1, other arithmetic, cut_exchange(): return joined_along(jnp.concatenate(gathered, axis=cut), concat_dim)  10.7 us
    gather x1, local copies, waits for them, and re-layouts, fetch_slots(): picked = jnp.take(flat_rows, own_owner * cap_rows + own_slot, axis=0)  9.57 us
    gather x1, local copies, waits for them, and re-layouts, fetch_slots(): jnp.take(spectra, row_index.reshape(-1), axis=0)  8.49 us
    dot_general x16, matrix products, apply_matrix(): return jnp.einsum('...ab,...b->...a', matrix, vector, precision=highest)  8.43 us
    select_n x2, other arithmetic, fetch_slots(): picked = jnp.take(flat_rows, own_owner * cap_rows + own_slot, axis=0)  7.46 us
  transfers between devices with their start and end apart: 1, of which 1 were waited for; matrix products, arithmetic and copies ran while one was open for 5% of the time, Pallas kernels for 0%

commit v1 on v0

v1 whole, which is shorter than its diff:
```python
import math

import jax
import jax.numpy as jnp
from jax import lax
from jax.experimental import pallas as pl
from jax.experimental.pallas import tpu as pltpu
from jax.sharding import PartitionSpec as P

ITERS = 3
EVERYONE = ("pts", "freq")
NT = (((1,), (1,)), ((), ()))
VMEM = pl.BlockSpec(memory_space=pltpu.VMEM)
SMEM = pl.BlockSpec(memory_space=pltpu.SMEM)


def gram(left_re, left_im, right):
    half = right.shape[0] // 2
    right_re, right_im = right[:half], right[half:]
    turned = jnp.concatenate([right_im, -right_re], axis=0)
    return lax.dot_general(
        left_re, right, NT, preferred_element_type=jnp.float32
    ) + lax.dot_general(left_im, turned, NT, preferred_element_type=jnp.float32)


def folded(matrix):
    half = matrix.shape[0] // 2
    return jnp.concatenate([matrix[:half], matrix[half:]], axis=1)


def density_kernel(spectra_ref, weights_ref, out_ref):
    rows = spectra_ref[0]
    half = rows.shape[0] // 2
    weighted = (rows.astype(jnp.float32) * weights_ref[...]).astype(jnp.bfloat16)
    out_ref[0] = folded(gram(weighted[:half], weighted[half:], rows))


def density_parts(spectra, weights):
    freqs, _, blocks, points = spectra.shape
    return pl.pallas_call(
        density_kernel,
        grid=(freqs,),
        in_specs=[
            pl.BlockSpec((1, 2 * blocks, points), lambda f: (f, 0, 0)),
            pl.BlockSpec((1, points), lambda f: (0, 0)),
        ],
        out_specs=pl.BlockSpec((1, blocks // 2, 4 * blocks), lambda f: (f, 0, 0)),
        out_shape=jax.ShapeDtypeStruct((freqs, blocks // 2, 4 * blocks), jnp.float32),
        cost_estimate=pl.CostEstimate(
            flops=freqs * 4 * blocks * blocks * points * 2,
            bytes_accessed=spectra.size * 2,
            transcendentals=0,
        ),
        name="density",
    )(spectra.reshape(freqs, 2 * blocks, points), weights.reshape(1, points))


def triad_kernel(groups, triads_ref, spectra_ref, weights_ref, out_ref):
    total = spectra_ref.shape[0]
    half = spectra_ref.shape[1] // 2
    count = out_ref.shape[0]
    per_group = count // groups

    def step(j, carry):
        t = lax.rem(j, groups) * per_group + lax.div(j, groups)
        k = triads_ref[2 * t]
        l = triads_ref[2 * t + 1]
        m = lax.rem(k + l, total)
        first = spectra_ref[k].astype(jnp.float32)
        second = spectra_ref[l].astype(jnp.float32)
        weights = weights_ref[...]
        ar, ai, br, bi = first[:half], first[half:], second[:half], second[half:]
        re = ((ar * br - ai * bi) * weights).astype(jnp.bfloat16)
        im = ((ar * bi + ai * br) * weights).astype(jnp.bfloat16)
        out_ref[j] = folded(gram(re, im, spectra_ref[m]))
        return carry

    lax.fori_loop(0, count, step, 0, unroll=4)


def triad_parts(triads, spectra, weights, groups):
    count = triads.shape[0]
    total, rows, points = spectra.shape
    return pl.pallas_call(
        lambda *refs: triad_kernel(groups, *refs),
        in_specs=[SMEM, VMEM, VMEM],
        out_specs=VMEM,
        out_shape=jax.ShapeDtypeStruct((count, rows // 4, 2 * rows), jnp.float32),
        cost_estimate=pl.CostEstimate(
            flops=count * rows * rows * points * 2,
            bytes_accessed=spectra.size * 2,
            transcendentals=0,
        ),
        name="triads",
    )(triads.reshape(-1), spectra, weights)


def power_kernel(scale, parts_ref, matrix_ref, vector_ref):
    total = jnp.sum(parts_ref[...], axis=0) * scale
    matrix_ref[...] = total
    blocks = 2 * total.shape[0]
    lane = lax.broadcasted_iota(jnp.int32, (1, 4 * blocks), 1)
    lower = lane < 2 * blocks
    other = pltpu.roll(total, 2 * blocks, 1)
    both = jnp.concatenate(
        [jnp.where(lower, total, other), jnp.where(lower, other, total)], axis=0
    )
    sign = jnp.where(lax.rem(lax.div(lane, blocks), 2) == 0, 1.0, -1.0)

    def forward(one, two):
        re = jnp.sum(both * jnp.where(lower, one, 0.0), axis=1, keepdims=True)
        im = jnp.sum(both * jnp.where(lower, two, 0.0), axis=1, keepdims=True)
        return re, im

    def square(one):
        return jnp.sum(jnp.where(lower, one * one, 0.0), axis=1, keepdims=True)

    start = 1.0 / math.sqrt(blocks)
    one = jnp.where(sign > 0, start, 0.0)
    two = jnp.where(sign > 0, 0.0, start)
    for _ in range(ITERS):
        re, im = forward(one, two)
        with_re = jnp.sum(both * re, axis=0, keepdims=True)
        with_im = jnp.sum(both * im, axis=0, keepdims=True)
        one = with_re + sign * pltpu.roll(with_im, blocks, 1)
        two = with_im - sign * pltpu.roll(with_re, blocks, 1)
        factor = 1.0 / jnp.sqrt(square(one) + 1.0)
        one = one * factor
        two = two * factor
    re, im = forward(one, two)
    top = jnp.sum(re * re + im * im, axis=0, keepdims=True)
    energy = top / (blocks * (square(one) + 1.0))
    row = jnp.where(lower, one * sign, energy)
    vector_ref[...] = jnp.broadcast_to(row[None], vector_ref.shape)


def power(parts, scale):
    count, rows, lanes = parts.shape
    return pl.pallas_call(
        lambda *refs: power_kernel(scale, *refs),
        in_specs=[VMEM],
        out_specs=[VMEM, VMEM],
        out_shape=[
            jax.ShapeDtypeStruct((rows, lanes), jnp.float32),
            jax.ShapeDtypeStruct((count, 1, lanes), jnp.float32),
        ],
        name="power",
    )(parts)


def modes_kernel(triads_ref, spectra_ref, vectors_ref, out_ref):
    total = spectra_ref.shape[0]
    steps = vectors_ref.shape[0]
    rows = vectors_ref.shape[1]
    each = rows // 2

    def step(s, carry):
        picked = []
        for q in range(each):
            t = s * each + q
            m = lax.rem(triads_ref[2 * t] + triads_ref[2 * t + 1], total)
            picked.append(spectra_ref[m])
        right = jnp.concatenate(picked, axis=0)
        out_ref[s] = jnp.dot(vectors_ref[s], right, preferred_element_type=jnp.float32)
        return carry

    lax.fori_loop(0, steps, step, 0, unroll=2)


def modes(triads, spectra, vectors):
    count, width = vectors.shape
    total, rows, points = spectra.shape
    half = width // 2
    each = 4
    re, im = vectors[:, :half], vectors[:, half:]
    pair = jnp.stack([re, -im, im, re], axis=1).reshape(count // each, each, 2, 1, width)
    own = jnp.eye(each, dtype=jnp.bfloat16).reshape(1, each, 1, each, 1)
    left = (pair * own).reshape(count // each, 2 * each, each * width)
    return pl.pallas_call(
        modes_kernel,
        in_specs=[SMEM, VMEM, VMEM],
        out_specs=VMEM,
        out_shape=jax.ShapeDtypeStruct((count // each, 2 * each, points), jnp.float32),
        cost_estimate=pl.CostEstimate(
            flops=count * rows * points * 4,
            bytes_accessed=spectra.size * 2,
            transcendentals=0,
        ),
        name="modes",
    )(triads.reshape(-1), spectra, left)


def to_all(value, axis):
    length = lax.axis_size(axis)
    return lax.all_to_all(
        jnp.broadcast_to(value[None], (length, *value.shape)), axis, 0, 0, tiled=True
    )


def unfolded(packed):
    n, half, lanes = packed.shape
    blocks = 2 * half
    parted = packed.reshape(n, half, 2, 2, blocks)
    return parted.transpose(0, 3, 2, 1, 4).reshape(n, 2, blocks, blocks)


def local(spectra, weights, triads):
    groups = lax.axis_size("freq")
    lines = lax.axis_size("pts")
    group = lax.axis_index("freq")
    f_dev, _, blocks, points = spectra.shape
    per_group = triads.shape[0] // groups
    point_count = points * lines
    share = points // groups

    send = spectra.reshape(f_dev, 2, blocks, groups, share).transpose(3, 0, 1, 2, 4)
    turned = lax.all_to_all(send, "freq", 0, 0, tiled=True)
    turned = turned.reshape(groups * f_dev, 2 * blocks, share)
    own_weights = lax.dynamic_slice_in_dim(weights, group * share, share, 0).reshape(1, share)

    dens_parts = density_parts(spectra, weights)
    dens_own = jnp.sum(lax.all_to_all(dens_parts, "pts", 0, 0, tiled=True), axis=0)
    dens_own = dens_own * (1.0 / point_count)

    parts = triad_parts(triads, turned, own_weights, groups)
    parts = lax.all_to_all(parts, EVERYONE, 0, 0, tiled=True)
    matrix, vector = power(parts, 1.0 / math.sqrt(blocks * point_count))

    rows = lax.all_to_all(vector, EVERYONE, 0, 0, tiled=True)
    rows = rows.reshape(lines, groups, -1).swapaxes(0, 1)
    vectors = rows[:, :, : 2 * blocks].reshape(groups * per_group, 2 * blocks)
    fields = modes(triads, turned, vectors.astype(jnp.bfloat16))
    fields = fields.reshape(groups, 2 * per_group, share)
    fields = lax.all_to_all(fields, "freq", 0, 0, tiled=True)
    mode_fields = fields.swapaxes(0, 1).reshape(per_group, 2, points)

    both = to_all(jnp.concatenate([matrix, dens_own], axis=0), "pts")
    bispectrum = unfolded(both[:, : blocks // 2])
    density = unfolded(both[:, blocks // 2 :])

    own = lax.dynamic_index_in_dim(rows, group, 0, keepdims=False)
    out_vectors = own[:, : 2 * blocks].reshape(per_group, 2, blocks)
    energy = own[:, 2 * blocks]
    return (bispectrum, density, out_vectors, energy, mode_fields)


def solution(mesh):
    in_specs = (P("freq", None, None, "pts"), P("pts"), P())
    out_specs = (
        P("freq", None, None, None),
        P("freq", None, None, None),
        P("freq", None, None),
        P("freq"),
        P("freq", None, "pts"),
    )
    return jax.shard_map(local, mesh=mesh, in_specs=in_specs, out_specs=out_specs, check_vma=False)
```

time: 319 us -> 170 us (0.53)
  blocking collectives: 135 us -> 0 us
  other arithmetic: 46.3 us -> 1.52 us
  starting transfers between devices: 6.53 us -> 38.9 us
  Pallas kernels: 0 us -> 31.9 us
  local copies, waits for them, and re-layouts: 36.9 us -> 14.2 us
  matrix products: 17.9 us -> 0 us
  waiting for transfers between devices: 74.1 us -> 78.9 us
    all_to_all x2 -> x0, blocking collectives: 135 us -> none  [the longest x1 80.1 us: cut_exchange(): lax.all_to_all(slab, axis, split_axis=0, concat_axis=0, tiled=True)]
    all_to_all x1 -> x6, starting transfers between devices: 6.53 us -> 38.9 us  [the longest x1 9.97 us: local(): parts = lax.all_to_all(parts, EVERYONE, 0, 0, tiled=True)]
    pallas_call x0 -> x4, Pallas kernels: none -> 31.9 us  [the longest x1 11.9 us: triad_parts(): pl.pallas_call(lambda *refs: triad_kernel(groups, *refs), in_specs=[SMEM,...]
    gather x3 -> x0, local copies, waits for them, and re-layouts: 23 us -> none  [the longest x1 9.57 us: fetch_slots(): picked = jnp.take(flat_rows, own_owner * cap_rows + own_slot, axis=0)]
    select_n x5 -> x0, other arithmetic: 18.6 us -> none  [the longest x2 7.46 us: fetch_slots(): picked = jnp.take(flat_rows, own_owner * cap_rows + own_slot, axis=0)]
    dot_general x31 -> x0, matrix products: 17.9 us -> none  [the longest x16 8.43 us: apply_matrix(): return jnp.einsum('...ab,...b->...a', matrix, vector, precision=highest)]
    concatenate x2 -> x1, other arithmetic: 10.7 us -> 0.7 us  [local(): both = to_all(jnp.concatenate([matrix, dens_own], axis=0), 'pts')]
    reshape x4 -> x7, local copies, waits for them, and re-layouts: 0.5 us -> 7.89 us  [the longest x1 4.75 us: local(): spectra.reshape(f_dev, 2, blocks, groups, share).transpose(3, 0, 1, 2, 4)]
  transfers between devices with their start and end apart: 1 -> 6, of which waited for: 1 -> 4; matrix products, arithmetic and copies ran while one was open for 5% -> 5% of each run, Pallas kernels for 0% -> 17%
where the time goes in v1:
time: 170 us; the launch traced here: 166 us
  waiting for transfers between devices  78.9 us (46%)
  starting transfers between devices  38.9 us (23%)
  Pallas kernels  31.9 us (19%)
  local copies, waits for them, and re-layouts  14.2 us (8%)
    all_to_all x1, waiting for transfers between devices, local(): turned = lax.all_to_all(send, 'freq', 0, 0, tiled=True)  49.5 us
    all_to_all x1, waiting for transfers between devices, local(): parts = lax.all_to_all(parts, EVERYONE, 0, 0, tiled=True)  17.2 us
    pallas_call x1, Pallas kernels, triad_parts(): pl.pallas_call(lambda *refs: triad_kernel(groups, *refs), in_specs=[SMEM,...  11.9 us
    pallas_call x1, Pallas kernels, density_parts(): pl.pallas_call(density_kernel, grid=(freqs,), in_specs=[pl.BlockSpec((1,...  11.7 us
    all_to_all x1, starting transfers between devices, local(): parts = lax.all_to_all(parts, EVERYONE, 0, 0, tiled=True)  9.97 us
    all_to_all x1, starting transfers between devices, local(): turned = lax.all_to_all(send, 'freq', 0, 0, tiled=True)  8.09 us
    all_to_all x1, waiting for transfers between devices, local(): rows = lax.all_to_all(vector, EVERYONE, 0, 0, tiled=True)  7.44 us
    all_to_all x1, starting transfers between devices, local(): rows = lax.all_to_all(vector, EVERYONE, 0, 0, tiled=True)  6.47 us
  transfers between devices with their start and end apart: 6, of which 4 were waited for; matrix products, arithmetic and copies ran while one was open for 5% of the time, Pallas kernels for 17%

profile of v1, /device:TPU:6, one launch (start us, length us, event | category | flops | bytes accessed | tf_op | source)
XLA Modules:
  0.0 166.2 jit_solution(13452729947683311946)
XLA Ops:
  0.6 4.8 %copy.67 = bf16[16,2,4,8,8,256]{5,4,2,1,0,3:T(8,128)(2,1)} copy(bf16[16,2,4,8,8,256]{5,4,3,2,1,0:T(8,128)(2,1)} %bitcast.33) | data formatting | bytes 8388608 | tf_op jit(solution)/shard_map/reshape | solution.py:216
  5.4 8.1 %all-to-all-start = ((bf16[8,16,2,32,256]{4,3,2,1,0:T(8,128)(2,1)}), bf16[8,16,2,32,256]{4,3,2,1,0:T(8,128)(2,1)}, u32[]{:S(2)}, u32[]{:S(2)}) async-start(bf16[8,16,2,32,256]{4,3,2,1,0:T(8,128)(2,1)} %bitcast.35), calls=%async_computation | async-start | bytes 8388608 | tf_op jit(solution)/shard_map/all_to_all | solution.py:217
  13.5 0.0 copy-start.1
  13.5 11.7 %density.1 = f32[16,16,128]{2,1,0:T(8,128)} custom-call(bf16[16,64,2048]{2,1,0:T(8,128)(2,1)} %bitcast.34, f32[1,2048]{1,0:T(1,128)} %bitcast.48), custom_call_target="tpu_custom_call" | custom-call | flops 268435456 | bytes 4194304 | tf_op jit(solution)/shard_map/density/pallas_call | solution.py:40
  25.2 49.5 %all-to-all-done = bf16[8,16,2,32,256]{4,3,2,1,0:T(8,128)(2,1)} async-done(((bf16[8,16,2,32,256]{4,3,2,1,0:T(8,128)(2,1)}), bf16[8,16,2,32,256]{4,3,2,1,0:T(8,128)(2,1)}, u32[]{:S(2)}, u32[]{:S(2)}) %all-to-all-start) | async-done | bytes 4194336 | tf_op jit(solution)/shard_map/all_to_all | solution.py:217
  74.7 5.0 %all-to-all-start.2 = ((f32[16,16,128]{2,1,0:T(8,128)}), f32[16,16,128]{2,1,0:T(8,128)S(1)}, u32[]{:S(2)}, u32[]{:S(2)}) async-start(f32[16,16,128]{2,1,0:T(8,128)} %density.1), calls=%async_computation.2 | async-start | bytes 262144 | tf_op jit(solution)/shard_map/all_to_all | solution.py:222
  79.7 1.3 dynamic_slice.5
  81.1 0.0 copy-done.1
  81.1 0.1 copy.48
  81.2 0.7 reshape.72.refs_0_.triads_ref
  81.9 11.9 %triads.1 = f32[128,16,128]{2,1,0:T(8,128)} custom-call(s32[256]{0:T(256)} %reshape.72.refs_0_.triads_ref, bf16[128,64,256]{2,1,0:T(8,128)(2,1)} %bitcast.1.refs_1_.spectra_ref, f32[1,256]{1,0:T(1,128)} %bitcast.49), custom_call_target="tpu_custom_call" | custom-call | flops 268435456 | bytes 4194304 | tf_op jit(solution)/shard_map/triads/pallas_call | solution.py:84
  93.8 0.0 all-to-all-done.2
  93.8 10.0 %all-to-all-start.1 = ((f32[128,16,128]{2,1,0:T(8,128)}), f32[128,16,128]{2,1,0:T(8,128)S(1)}, u32[]{:S(2)}, u32[]{:S(2)}) async-start(f32[128,16,128]{2,1,0:T(8,128)} %triads.1), calls=%async_computation.1 | async-start | bytes 2097152 | tf_op jit(solution)/shard_map/all_to_all | solution.py:226
  103.8 0.1 mul.37
  103.9 0.1 mul.38
  104.0 17.2 %all-to-all-done.1.refs_0_ = f32[128,16,128]{2,1,0:T(8,128)S(1)} async-done(((f32[128,16,128]{2,1,0:T(8,128)}), f32[128,16,128]{2,1,0:T(8,128)S(1)}, u32[]{:S(2)}, u32[]{:S(2)}) %all-to-all-start.1) | async-done | bytes 1048608 | tf_op jit(solution)/shard_map/all_to_all | solution.py:226
  121.1 0.0 copy-start
  121.1 1.0 copy-done
  122.1 2.9 %power.1 = (f32[16,128]{1,0:T(8,128)}, f32[128,1,128]{2,1,0:T(1,128)}) custom-call(f32[128,16,128]{2,1,0:T(8,128)} %copy-done), custom_call_target="tpu_custom_call" | custom-call | tf_op jit(solution)/shard_map/power/pallas_call | solution.py:139
  125.1 6.5 %all-to-all-start.4 = ((f32[128,1,128]{2,1,0:T(1,128)}), f32[128,1,128]{2,1,0:T(1,128)S(1)}, u32[]{:S(2)}, u32[]{:S(2)}) async-start(f32[128,1,128]{2,1,0:T(1,128)} %get-tuple-element.8), calls=%async_computation.4 | async-start | bytes 131072 | tf_op jit(solution)/shard_map/all_to_all | solution.py:229
  131.5 0.7 pad_maximum_fusion.1
  132.2 7.4 %all-to-all-done.4 = f32[128,1,128]{2,1,0:T(1,128)S(1)} async-done(((f32[128,1,128]{2,1,0:T(1,128)}), f32[128,1,128]{2,1,0:T(1,128)S(1)}, u32[]{:S(2)}, u32[]{:S(2)}) %all-to-all-start.4) | async-done | bytes 65568 | tf_op jit(solution)/shard_map/all_to_all | solution.py:229
  139.7 0.7 broadcast_in_dim.2
  140.4 3.5 %all-to-all-start.3 = ((f32[16,32,128]{2,1,0:T(8,128)}), f32[16,32,128]{2,1,0:T(8,128)S(1)}, u32[]{:S(2)}, u32[]{:S(2)}) async-start(f32[16,32,128]{2,1,0:T(8,128)} %broadcast_in_dim.2), calls=%async_computation.3 | async-start | bytes 524288 | tf_op jit(solution)/shard_map/all_to_all | solution.py:195
  144.0 0.1 negate_bitcast_fusion
  144.1 0.1 copy.58
  144.2 0.1 mul.34
  144.3 0.1 mul.35
  144.4 0.2 mul.36
  144.7 0.7 broadcast_multiply_fusion.vectors_ref
  145.3 0.1 copy.52
  145.4 0.7 copy.60
  146.1 5.3 %modes.1 = f32[32,8,256]{2,1,0:T(8,128)} custom-call(s32[256]{0:T(256)} %reshape.72.refs_0_.triads_ref, bf16[128,64,256]{2,1,0:T(8,128)(2,1)} %bitcast.1.refs_1_.spectra_ref, bf16[32,8,256]{2,1,0:T(8,128)(2,1)} %broadcast_multiply_fusion.vectors_ref), custom_call_target="tpu_custom_call" | custom-call | flops 8388608 | bytes 4194304 | tf_op jit(solution)/shard_map/modes/pallas_call | solution.py:179
  151.5 0.5 slice_bitcast_fusion.2
  152.0 0.0 all-to-all-done.3
  152.0 5.8 %all-to-all-start.5 = ((f32[8,32,256]{2,1,0:T(8,128)}), f32[8,32,256]{2,1,0:T(8,128)S(1)}, u32[]{:S(2)}, u32[]{:S(2)}) async-start(f32[8,32,256]{2,1,0:T(8,128)} %bitcast.38), calls=%async_computation.5 | async-start | bytes 524288 | tf_op jit(solution)/shard_map/all_to_all | solution.py:234
  157.8 0.4 reshape.78
  158.3 0.9 copy.50
  159.1 0.4 reshape.80
  159.6 0.9 copy.51
  160.4 4.8 %all-to-all-done.5 = f32[8,32,256]{2,1,0:T(8,128)S(1)} async-done(((f32[8,32,256]{2,1,0:T(8,128)}), f32[8,32,256]{2,1,0:T(8,128)S(1)}, u32[]{:S(2)}, u32[]{:S(2)}) %all-to-all-start.5) | async-done | bytes 262176 | tf_op jit(solution)/shard_map/all_to_all | solution.py:234
  165.2 0.2 copy.59
  165.3 0.9 reshape.85
  (8 shorter events, 0.1 us)
Async XLA Ops:
  5.4 69.3 %all-to-all-start = ((bf16[8,16,2,32,256]{4,3,2,1,0:T(8,128)(2,1)}), bf16[8,16,2,32,256]{4,3,2,1,0:T(8,128)(2,1)}, u32[]{:S(2)}, u32[]{:S(2)}) async-start(bf16[8,16,2,32,256]{4,3,2,1,0:T(8,128)(2,1)} %bitcast.35), calls=%async_computation | async-start | bytes 8388608 | tf_op jit(solution)/shard_map/all_to_all | solution.py:217
  13.5 67.6 %copy-start.1 = (s32[128,2]{0,1:T(2,128)S(1)}, s32[128,2]{0,1:T(2,128)}, u32[]{:S(2)}) copy-start(s32[128,2]{0,1:T(2,128)} %param.5) | copy-start | bytes 3076
  74.7 19.1 %all-to-all-start.2 = ((f32[16,16,128]{2,1,0:T(8,128)}), f32[16,16,128]{2,1,0:T(8,128)S(1)}, u32[]{:S(2)}, u32[]{:S(2)}) async-start(f32[16,16,128]{2,1,0:T(8,128)} %density.1), calls=%async_computation.2 | async-start | bytes 262144 | tf_op jit(solution)/shard_map/all_to_all | solution.py:222
  93.8 27.3 %all-to-all-start.1 = ((f32[128,16,128]{2,1,0:T(8,128)}), f32[128,16,128]{2,1,0:T(8,128)S(1)}, u32[]{:S(2)}, u32[]{:S(2)}) async-start(f32[128,16,128]{2,1,0:T(8,128)} %triads.1), calls=%async_computation.1 | async-start | bytes 2097152 | tf_op jit(solution)/shard_map/all_to_all | solution.py:226
  121.1 1.0 copy-start
  125.1 14.6 %all-to-all-start.4 = ((f32[128,1,128]{2,1,0:T(1,128)}), f32[128,1,128]{2,1,0:T(1,128)S(1)}, u32[]{:S(2)}, u32[]{:S(2)}) async-start(f32[128,1,128]{2,1,0:T(1,128)} %get-tuple-element.8), calls=%async_computation.4 | async-start | bytes 131072 | tf_op jit(solution)/shard_map/all_to_all | solution.py:229
  140.4 11.6 %all-to-all-start.3 = ((f32[16,32,128]{2,1,0:T(8,128)}), f32[16,32,128]{2,1,0:T(8,128)S(1)}, u32[]{:S(2)}, u32[]{:S(2)}) async-start(f32[16,32,128]{2,1,0:T(8,128)} %broadcast_in_dim.2), calls=%async_computation.3 | async-start | bytes 524288 | tf_op jit(solution)/shard_map/all_to_all | solution.py:195
  152.0 13.2 %all-to-all-start.5 = ((f32[8,32,256]{2,1,0:T(8,128)}), f32[8,32,256]{2,1,0:T(8,128)S(1)}, u32[]{:S(2)}, u32[]{:S(2)}) async-start(f32[8,32,256]{2,1,0:T(8,128)} %bitcast.38), calls=%async_computation.5 | async-start | bytes 524288 | tf_op jit(solution)/shard_map/all_to_all | solution.py:234

commit v2 on v1

v2 whole, which is shorter than its diff:
```python
import math

import jax
import jax.numpy as jnp
from jax import lax
from jax.experimental import pallas as pl
from jax.experimental.pallas import tpu as pltpu
from jax.sharding import Mesh
from jax.sharding import PartitionSpec as P

ITERS = 3
EACH = 4
NT = (((1,), (1,)), ((), ()))
VMEM = pl.BlockSpec(memory_space=pltpu.VMEM)
SMEM = pl.BlockSpec(memory_space=pltpu.SMEM)


def params(mib=12):
    return pltpu.CompilerParams(vmem_limit_bytes=mib << 20)


def gram(left_re, left_im, right):
    half = right.shape[0] // 2
    right_re, right_im = right[:half], right[half:]
    turned = jnp.concatenate([right_im, -right_re], axis=0)
    return lax.dot_general(
        left_re, right, NT, preferred_element_type=jnp.float32
    ) + lax.dot_general(left_im, turned, NT, preferred_element_type=jnp.float32)


def folded(matrix):
    half = matrix.shape[0] // 2
    return jnp.concatenate([matrix[:half], matrix[half:]], axis=1)


def cut_kernel(rows_ref, out_ref, sems):
    count, _, share = out_ref.shape
    copies = [
        pltpu.make_async_copy(
            rows_ref.at[:, pl.ds(d * share, share)], out_ref.at[d], sems.at[d]
        )
        for d in range(count)
    ]
    for copy in copies:
        copy.start()
    for copy in copies:
        copy.wait()


def cut(rows, count):
    length, points = rows.shape
    return pl.pallas_call(
        cut_kernel,
        in_specs=[pl.BlockSpec(memory_space=pl.ANY)],
        out_specs=VMEM,
        out_shape=pltpu.VMEM((count, length, points // count), rows.dtype),
        scratch_shapes=[pltpu.SemaphoreType.DMA((count,))],
        compiler_params=params(),
        name="cut",
    )(rows)


def density_kernel(spectra_ref, weights_ref, out_ref):
    half = spectra_ref.shape[1] // 2
    for f in range(spectra_ref.shape[0]):
        rows = spectra_ref[f]
        weighted = (rows.astype(jnp.float32) * weights_ref[...]).astype(jnp.bfloat16)
        out_ref[f] = folded(gram(weighted[:half], weighted[half:], rows))


def density_parts(spectra, weights):
    freqs, rows, points = spectra.shape
    return pl.pallas_call(
        density_kernel,
        grid=(freqs // EACH,),
        in_specs=[
            pl.BlockSpec((EACH, rows, points), lambda f: (f, 0, 0)),
            pl.BlockSpec((1, points), lambda f: (0, 0)),
        ],
        out_specs=pl.BlockSpec((EACH, rows // 4, 2 * rows), lambda f: (f, 0, 0)),
        out_shape=jax.ShapeDtypeStruct((freqs, rows // 4, 2 * rows), jnp.float32),
        cost_estimate=pl.CostEstimate(
            flops=freqs * rows * rows * points * 2,
            bytes_accessed=spectra.size * 2,
            transcendentals=0,
        ),
        compiler_params=params(24),
        name="density",
    )(spectra, weights)


def triad_kernel(groups, mine, triads_ref, spectra_ref, weights_ref, out_ref):
    total, rows, share = spectra_ref.shape
    half = rows // 2
    count = out_ref.shape[0]
    per_group = 2 * count // groups
    core = lax.axis_index("core")
    core = core if mine else 1 - core
    offset = pl.multiple_of(lax.axis_index("freq") * share, share)

    def step(j, carry):
        t = lax.rem(j, groups) * per_group + 2 * lax.div(j, groups) + core
        k = triads_ref[0, t]
        l = triads_ref[1, t]
        m = lax.rem(k + l, total)
        first = spectra_ref[k].astype(jnp.float32)
        second = spectra_ref[l].astype(jnp.float32)
        weights = weights_ref[:, pl.ds(offset, share)]
        ar, ai, br, bi = first[:half], first[half:], second[:half], second[half:]
        re = ((ar * br - ai * bi) * weights).astype(jnp.bfloat16)
        im = ((ar * bi + ai * br) * weights).astype(jnp.bfloat16)
        out_ref[j] = folded(gram(re, im, spectra_ref[m]))
        return carry

    lax.fori_loop(0, count, step, 0, unroll=32)


def triad_parts(triads, spectra, weights, groups, mine):
    count = triads.shape[1] // 2
    total, rows, points = spectra.shape
    return pl.pallas_call(
        lambda *refs: triad_kernel(groups, mine, *refs),
        in_specs=[SMEM, VMEM, VMEM],
        out_specs=VMEM,
        out_shape=jax.ShapeDtypeStruct((count, rows // 4, 2 * rows), jnp.float32),
        cost_estimate=pl.CostEstimate(
            flops=count * rows * rows * points * 4,
            bytes_accessed=spectra.size * 2,
            transcendentals=0,
        ),
        compiler_params=params(),
        name="triads_own" if mine else "triads_other",
    )(triads, spectra, weights)


def power_kernel(scale, parts_ref, out_ref):
    total = jnp.sum(parts_ref[...], axis=0) * scale
    half = total.shape[0]
    blocks = 2 * half
    lane = lax.broadcasted_iota(jnp.int32, (1, 4 * blocks), 1)
    lower = lane < 2 * blocks
    other = pltpu.roll(total, 2 * blocks, 1)
    both = jnp.concatenate(
        [jnp.where(lower, total, other), jnp.where(lower, other, total)], axis=0
    )
    sign = jnp.where(lax.rem(lax.div(lane, blocks), 2) == 0, 1.0, -1.0)

    def forward(one, two):
        re = jnp.sum(both * jnp.where(lower, one, 0.0), axis=1, keepdims=True)
        im = jnp.sum(both * jnp.where(lower, two, 0.0), axis=1, keepdims=True)
        return re, im

    def square(one):
        return jnp.sum(jnp.where(lower, one * one, 0.0), axis=1, keepdims=True)

    start = 1.0 / math.sqrt(blocks)
    one = jnp.where(sign > 0, start, 0.0)
    two = jnp.where(sign > 0, 0.0, start)
    for _ in range(ITERS):
        re, im = forward(one, two)
        with_re = jnp.sum(both * re, axis=0, keepdims=True)
        with_im = jnp.sum(both * im, axis=0, keepdims=True)
        one = with_re + sign * pltpu.roll(with_im, blocks, 1)
        two = with_im - sign * pltpu.roll(with_re, blocks, 1)
        factor = 1.0 / jnp.sqrt(square(one) + 1.0)
        one = one * factor
        two = two * factor
    re, im = forward(one, two)
    top = jnp.sum(re * re + im * im, axis=0, keepdims=True)
    energy = top / (blocks * (square(one) + 1.0))
    row = jnp.where(lower, one * sign, energy)
    tail = jnp.broadcast_to(row, (out_ref.shape[1] - half, 4 * blocks))
    for d in range(out_ref.shape[0]):
        out_ref[d, :half] = total
        out_ref[d, half:] = tail


def power(parts, scale, lines):
    _, rows, lanes = parts.shape
    return pl.pallas_call(
        lambda *refs: power_kernel(scale, *refs),
        in_specs=[VMEM],
        out_specs=VMEM,
        out_shape=jax.ShapeDtypeStruct((lines, rows + 8, lanes), jnp.float32),
        compiler_params=params(8),
        name="power",
    )(parts)


def modes_kernel(triads_ref, spectra_ref, vectors_ref, out_ref, pairs_ref):
    total = spectra_ref.shape[0]
    count, lanes = vectors_ref.shape
    blocks = lanes // 4
    lane = lax.broadcasted_iota(jnp.int32, (1, lanes), 1)
    lower = lane < 2 * blocks
    sign = jnp.where(lax.rem(lax.div(lane, blocks), 2) == 0, 1.0, -1.0)
    rows = jnp.where(lower, vectors_ref[...], 0.0)
    rows = rows + pltpu.roll(rows, 2 * blocks, 1)
    swapped = pltpu.roll(rows, blocks, 1)
    odd = lax.rem(lax.broadcasted_iota(jnp.int32, (count, 1), 0), 2) == 1
    keep = lower != odd
    pairs_ref[pl.ds(0, count, stride=2), :] = jnp.where(keep, rows * sign, 0.0)
    pairs_ref[pl.ds(1, count, stride=2), :] = jnp.where(keep, swapped, 0.0)
    early = lax.broadcasted_iota(jnp.int32, (2 * EACH, 1), 0) < EACH

    def step(s, carry):
        picked = []
        for q in range(EACH):
            t = s * EACH + q
            m = lax.rem(triads_ref[0, t] + triads_ref[1, t], total)
            picked.append(spectra_ref[m])
        right = jnp.concatenate(picked, axis=0)
        pair = pairs_ref[pl.ds(pl.multiple_of(s * 2 * EACH, 2 * EACH), 2 * EACH), :]
        left = jnp.concatenate(
            [jnp.where(early, pair, 0.0), jnp.where(early, 0.0, pair)], axis=1
        ).astype(jnp.bfloat16)
        out_ref[s] = jnp.dot(left, right, preferred_element_type=jnp.float32)
        return carry

    lax.fori_loop(0, count // EACH, step, 0, unroll=16)


def modes(triads, spectra, vectors):
    count, lanes = vectors.shape
    total, rows, points = spectra.shape
    return pl.pallas_call(
        modes_kernel,
        in_specs=[SMEM, VMEM, VMEM],
        out_specs=VMEM,
        out_shape=jax.ShapeDtypeStruct((count // EACH, 2 * EACH, points), jnp.float32),
        scratch_shapes=[pltpu.VMEM((2 * count, lanes), jnp.float32)],
        cost_estimate=pl.CostEstimate(
            flops=count * rows * points * 4,
            bytes_accessed=spectra.size * 2,
            transcendentals=0,
        ),
        compiler_params=params(),
        name="modes",
    )(triads, spectra, vectors)


def exchange(value, axis):
    return lax.all_to_all(value, axis, 0, 0, tiled=True)


def swap(value, axis, bit):
    length = lax.axis_size(axis)
    return lax.ppermute(value, axis, [(i, i ^ bit) for i in range(length)])


def unfolded(packed):
    n, half, lanes = packed.shape
    blocks = 2 * half
    parted = packed.reshape(n, half, 2, 2, blocks)
    return parted.transpose(0, 3, 2, 1, 4).reshape(n, 2, blocks, blocks)


def local(spectra, weights, triads):
    groups = lax.axis_size("freq")
    lines = lax.axis_size("line")
    cores = lax.axis_size("core")
    f_dev, _, blocks, points = spectra.shape
    per_group = triads.shape[0] // groups
    point_count = points * lines * cores
    share = points // groups
    weights = weights.reshape(1, points)
    triads = triads.T

    send = cut(spectra.reshape(f_dev * 2 * blocks, points), groups)
    turned = exchange(send, "freq").reshape(groups * f_dev, 2 * blocks, share)

    other = triad_parts(triads, turned, weights, groups, False)
    given = swap(other, "core", 1)
    parts = triad_parts(triads, turned, weights, groups, True) + given
    late_weights, parts = lax.optimization_barrier((weights, parts))
    parts = exchange(parts, ("line", "freq"))

    dens = density_parts(spectra.reshape(f_dev, 2 * blocks, points), late_weights)
    dens = dens + swap(dens, "core", 1)
    for bit in (1, 2, 4):
        dens = dens + swap(dens, "line", bit)
    density = unfolded(dens * (1.0 / point_count))

    payload = power(parts, 1.0 / math.sqrt(blocks * point_count), lines * cores)
    payload = exchange(payload, ("line", "core"))
    bispectrum = unfolded(payload[:, : blocks // 2])
    rows = payload[:, blocks // 2]
    out_vectors = rows[:, : 2 * blocks].reshape(per_group, 2, blocks)
    energy = rows[:, 2 * blocks]

    vectors = exchange(jnp.broadcast_to(rows[None], (groups, *rows.shape)), "freq")
    fields = modes(triads, turned, vectors.reshape(groups * per_group, -1))
    fields = exchange(fields.reshape(groups, 2 * per_group, share), "freq")
    mode_fields = fields.swapaxes(0, 1).reshape(per_group, 2, points)
    return (bispectrum, density, out_vectors, energy, mode_fields)


def solution(mesh):
    pts, freq = mesh.devices.shape
    finer = Mesh(mesh.devices.reshape(pts // 2, 2, freq), ("line", "core", "freq"))
    place = ("line", "core")
    in_specs = (P("freq", None, None, place), P(place), P())
    out_specs = (
        P("freq", None, None, None),
        P("freq", None, None, None),
        P("freq", None, None),
        P("freq"),
        P("freq", None, place),
    )
    return jax.shard_map(local, mesh=finer, in_specs=in_specs, out_specs=out_specs, check_vma=False)
```

time: 170 us -> 135 us (0.79)
  blocking collectives: 0 us -> 69.9 us
  waiting for transfers between devices: 78.9 us -> 11.6 us
  Pallas kernels: 31.9 us -> 12.3 us
  starting transfers between devices: 38.9 us -> 25.5 us
  local copies, waits for them, and re-layouts: 14.2 us -> 11.6 us
    all_to_all x6 -> x3, waiting for transfers between devices: 78.9 us -> 6.18 us  [exchange(): return lax.all_to_all(value, axis, 0, 0, tiled=True)]
    all_to_all x0 -> x2, blocking collectives: none -> 69.9 us  [exchange(): return lax.all_to_all(value, axis, 0, 0, tiled=True)]
    all_to_all x6 -> x3, starting transfers between devices: 38.9 us -> 18.8 us  [exchange(): return lax.all_to_all(value, axis, 0, 0, tiled=True)]
    pallas_call x2 -> x4, Pallas kernels: 23.6 us -> 8.4 us  [the longest x2 4.79 us: triad_parts(): pl.pallas_call(lambda *refs: triad_kernel(groups, mine, *refs), in_specs=...]
    ppermute x0 -> x5, starting transfers between devices: none -> 6.76 us  [swap(): return lax.ppermute(value, axis, [(i, i ^ bit) for i in range(length)])]
    unnamed x5 -> x12, local copies, waits for them, and re-layouts: 1.09 us -> 6.57 us
    reshape x4 -> x1, local copies, waits for them, and re-layouts: 6.15 us -> 0.68 us  [local(): out_vectors = rows[:, :2 * blocks].reshape(per_group, 2, blocks)]
    ppermute x0 -> x5, waiting for transfers between devices: none -> 5.43 us  [swap(): return lax.ppermute(value, axis, [(i, i ^ bit) for i in range(length)])]
  transfers between devices with their start and end apart: 6 -> 8, of which waited for: 4 -> 4; matrix products, arithmetic and copies ran while one was open for 5% -> 3% of each run, Pallas kernels for 17% -> 7%
where the time goes in v2:
time: 135 us; the launch traced here: 133 us
  blocking collectives  69.9 us (52%)
  starting transfers between devices  25.5 us (19%)
  Pallas kernels  12.3 us (9%)
  local copies, waits for them, and re-layouts  11.6 us (9%)
  waiting for transfers between devices  11.6 us (9%)
    all_to_all x2, blocking collectives, exchange(): return lax.all_to_all(value, axis, 0, 0, tiled=True)  69.9 us
    all_to_all x3, starting transfers between devices, exchange(): return lax.all_to_all(value, axis, 0, 0, tiled=True)  18.8 us
    ppermute x5, starting transfers between devices, swap(): return lax.ppermute(value, axis, [(i, i ^ bit) for i in range(length)])  6.76 us
    unnamed x12, local copies, waits for them, and re-layouts  6.57 us
    all_to_all x3, waiting for transfers between devices, exchange(): return lax.all_to_all(value, axis, 0, 0, tiled=True)  6.18 us
    ppermute x5, waiting for transfers between devices, swap(): return lax.ppermute(value, axis, [(i, i ^ bit) for i in range(length)])  5.43 us
    pallas_call x2, Pallas kernels, triad_parts(): pl.pallas_call(lambda *refs: triad_kernel(groups, mine, *refs), in_specs=...  4.79 us
    pallas_call x1, Pallas kernels, density_parts(): pl.pallas_call(density_kernel, grid=(freqs // EACH,), in_specs=[pl.BlockS...  2.93 us
  transfers between devices with their start and end apart: 8, of which 4 were waited for; matrix products, arithmetic and copies ran while one was open for 3% of the time, Pallas kernels for 7%

profile of v2, /device:TPU:6, one launch (start us, length us, event | category | flops | bytes accessed | tf_op | source)
XLA Modules:
  0.0 132.6 jit_solution(5947669626369133135)
XLA Ops:
  0.6 0.0 copy-start.2
  0.6 2.2 %copy-done.2 = bf16[16,2,32,2048]{3,2,1,0:T(8,128)(2,1)S(1)} copy-done((bf16[16,2,32,2048]{3,2,1,0:T(8,128)(2,1)S(1)}, bf16[16,2,32,2048]{3,2,1,0:T(8,128)(2,1)}, u32[]{:S(2)}) %copy-start.2) | copy-done | bytes 4194328
  2.8 0.7 cut.1
  3.5 0.0 copy-start.4
  3.5 0.0 copy-start.5
  3.5 57.3 %all_to_all.25 = bf16[8,1024,256]{2,1,0:T(8,128)(2,1)S(1)} all-to-all(bf16[8,1024,256]{2,1,0:T(8,128)(2,1)S(1)} %cut.1), channel_id=1, replica_groups=mesh['line'=8,'core'=2,'freq'=8] {'freq'}, dimensions={0} | all-to-all | bytes 8388608 | tf_op jit(solution)/shard_map/all_to_all | solution.py:243
  60.8 0.0 copy-start
  60.8 0.0 copy-done.4
  60.8 0.0 copy-done.5
  60.8 2.4 %triads_other.1 = f32[64,16,128]{2,1,0:T(8,128)S(1)} custom-call(s32[2,128]{1,0:T(2,128)S(1)} %bitcast.23, bf16[128,64,256]{2,1,0:T(8,128)(2,1)S(1)} %bitcast.14, f32[1,2048]{1,0:T(1,128)S(1)} %bitcast.20), custom_call_target="tpu_custom_call" | custom-call | flops 268435456 | bytes 4194304 | tf_op jit(solution)/shard_map/triads_other/pallas_call | solution.py:121
  63.2 0.1 collective-permute-start
  63.3 2.4 %triads_own.1 = f32[64,16,128]{2,1,0:T(8,128)S(1)} custom-call(s32[2,128]{1,0:T(2,128)S(1)} %bitcast.24, bf16[128,64,256]{2,1,0:T(8,128)(2,1)S(1)} %bitcast.15, f32[1,2048]{1,0:T(1,128)S(1)} %bitcast.21), custom_call_target="tpu_custom_call" | custom-call | flops 268435456 | bytes 4194304 | tf_op jit(solution)/shard_map/triads_own/pallas_call | solution.py:121
  65.7 0.0 copy-done
  65.7 0.0 collective-permute-done
  65.7 0.9 add.15
  66.6 8.2 %all-to-all-start.1 = ((f32[64,16,128]{2,1,0:T(8,128)}), f32[64,16,128]{2,1,0:T(8,128)S(1)}, u32[]{:S(2)}, u32[]{:S(2)}) async-start(f32[64,16,128]{2,1,0:T(8,128)} %add.15), calls=%async_computation.1 | async-start | bytes 1048576 | tf_op jit(solution)/shard_map/all_to_all | solution.py:243
  74.8 0.0 copy-start.3
  74.8 2.2 %copy-done.3 = bf16[16,2,32,2048]{3,2,1,0:T(8,128)(2,1)S(1)} copy-done((bf16[16,2,32,2048]{3,2,1,0:T(8,128)(2,1)S(1)}, bf16[16,2,32,2048]{3,2,1,0:T(8,128)(2,1)}, u32[]{:S(2)}) %copy-start.3) | copy-done | bytes 4194328
  77.0 2.9 %density.1 = f32[16,16,128]{2,1,0:T(8,128)S(1)} custom-call(bf16[16,64,2048]{2,1,0:T(8,128)(2,1)S(1)} %bitcast.18, f32[1,2048]{1,0:T(1,128)S(1)} %bitcast.22), custom_call_target="tpu_custom_call" | custom-call | flops 268435456 | bytes 4194304 | tf_op jit(solution)/shard_map/density/pallas_call | solution.py:73
  79.9 0.1 collective-permute-start.1
  80.0 1.3 %collective-permute-done.1 = f32[16,16,128]{2,1,0:T(8,128)S(1)} collective-permute-done((f32[16,16,128]{2,1,0:T(8,128)S(1)}, f32[16,16,128]{2,1,0:T(8,128)S(1)}, u32[]{:S(2)}, u32[]{:S(2)}) %collective-permute-start.1) | collective-permute-done | bytes 131104 | tf_op jit(solution)/shard_map/ppermute | solution.py:248
  81.4 1.5 %collective-permute-start.2 = (f32[16,16,128]{2,1,0:T(8,128)S(1)}, f32[16,16,128]{2,1,0:T(8,128)S(1)}, u32[]{:S(2)}, u32[]{:S(2)}) collective-permute-start(f32[16,16,128]{2,1,0:T(8,128)S(1)} %add.16), channel_id=1, source_target_pairs={{0,16},{16,0},{32,48},{48,32},{64,80},{80,64},{96,112},{112,96},{1... | collective-permute-start | bytes 393224 | tf_op jit(solution)/shard_map/ppermute | solution.py:248
  82.9 4.1 %collective-permute-done.2 = f32[16,16,128]{2,1,0:T(8,128)S(1)} collective-permute-done((f32[16,16,128]{2,1,0:T(8,128)S(1)}, f32[16,16,128]{2,1,0:T(8,128)S(1)}, u32[]{:S(2)}, u32[]{:S(2)}) %collective-permute-start.2) | collective-permute-done | bytes 131104 | tf_op jit(solution)/shard_map/ppermute | solution.py:248
  87.0 1.6 %collective-permute-start.3 = (f32[16,16,128]{2,1,0:T(8,128)S(1)}, f32[16,16,128]{2,1,0:T(8,128)S(1)}, u32[]{:S(2)}, u32[]{:S(2)}) collective-permute-start(f32[16,16,128]{2,1,0:T(8,128)S(1)} %add.17), channel_id=1, source_target_pairs={{0,32},{16,48},{32,0},{48,16},{64,96},{80,112},{96,64},{112,80},{1... | collective-permute-start | bytes 393224 | tf_op jit(solution)/shard_map/ppermute | solution.py:248
  88.6 0.0 all-to-all-done.1.refs_0_
  88.6 1.7 %power.1 = f32[16,24,128]{2,1,0:T(8,128)} custom-call(f32[64,16,128]{2,1,0:T(8,128)S(1)} %all-to-all-done.1.refs_0_), custom_call_target="tpu_custom_call" | custom-call | tf_op jit(solution)/shard_map/power/pallas_call | solution.py:180
  90.3 5.2 %all-to-all-start.2 = ((f32[16,24,128]{2,1,0:T(8,128)}), f32[16,24,128]{2,1,0:T(8,128)S(1)}, u32[]{:S(2)}, u32[]{:S(2)}) async-start(f32[16,24,128]{2,1,0:T(8,128)} %power.1), calls=%async_computation.2 | async-start | bytes 393216 | tf_op jit(solution)/shard_map/all_to_all | solution.py:243
  95.5 0.0 collective-permute-done.3
  95.5 3.5 %collective-permute-start.4 = (f32[16,16,128]{2,1,0:T(8,128)S(1)}, f32[16,16,128]{2,1,0:T(8,128)S(1)}, u32[]{:S(2)}, u32[]{:S(2)}) collective-permute-start(f32[16,16,128]{2,1,0:T(8,128)S(1)} %add.18), channel_id=1, source_target_pairs={{0,64},{16,80},{32,96},{48,112},{64,0},{80,16},{96,32},{112,48},{1... | collective-permute-start | bytes 393224 | tf_op jit(solution)/shard_map/ppermute | solution.py:248
  99.0 3.5 %all-to-all-done.2 = f32[16,24,128]{2,1,0:T(8,128)S(1)} async-done(((f32[16,24,128]{2,1,0:T(8,128)}), f32[16,24,128]{2,1,0:T(8,128)S(1)}, u32[]{:S(2)}, u32[]{:S(2)}) %all-to-all-start.2) | async-done | bytes 196640 | tf_op jit(solution)/shard_map/all_to_all | solution.py:243
  102.6 12.6 %all_to_all.26 = f32[8,16,128]{2,1,0:T(8,128)S(1)} all-to-all(f32[8,16,128]{2,1,0:T(8,128)S(1)} %broadcast_in_dim.2), channel_id=1, replica_groups=mesh['line'=8,'core'=2,'freq'=8] {'freq'}, dimensions={0} | all-to-all | bytes 131072 | tf_op jit(solution)/shard_map/all_to_all | solution.py:243
  115.2 0.0 copy-start.1
  115.2 2.2 %copy-done.1 = bf16[8,1024,256]{2,1,0:T(8,128)(2,1)S(1)} copy-done((bf16[8,1024,256]{2,1,0:T(8,128)(2,1)S(1)}, bf16[8,1024,256]{2,1,0:T(8,128)(2,1)}, u32[]{:S(2)}) %copy-start.1) | copy-done | bytes 4194328
  117.4 2.2 %modes.1 = f32[32,8,256]{2,1,0:T(8,128)} custom-call(s32[2,128]{1,0:T(2,128)S(1)} %bitcast.25, bf16[128,64,256]{2,1,0:T(8,128)(2,1)S(1)} %bitcast.16, f32[128,128]{1,0:T(8,128)S(1)} %bitcast.19), custom_call_target="tpu_custom_call" | custom-call | flops 8388608 | bytes 4194304 | tf_op jit(solution)/shard_map/modes/pallas_call | solution.py:226
  119.6 5.3 %all-to-all-start.4 = ((f32[8,32,256]{2,1,0:T(8,128)}), f32[8,32,256]{2,1,0:T(8,128)S(1)}, u32[]{:S(2)}, u32[]{:S(2)}) async-start(f32[8,32,256]{2,1,0:T(8,128)} %bitcast.11), calls=%async_computation.4 | async-start | bytes 524288 | tf_op jit(solution)/shard_map/all_to_all | solution.py:243
  124.9 0.0 collective-permute-done.4
  124.9 0.4 reshape.53
  125.4 0.9 copy.12
  126.2 0.7 reshape.55
  126.9 0.4 reshape.50
  127.4 0.9 copy.11
  128.2 0.7 slice_reduce_fusion
  128.9 2.7 %all-to-all-done.4 = f32[8,32,256]{2,1,0:T(8,128)S(1)} async-done(((f32[8,32,256]{2,1,0:T(8,128)}), f32[8,32,256]{2,1,0:T(8,128)S(1)}, u32[]{:S(2)}, u32[]{:S(2)}) %all-to-all-start.4) | async-done | bytes 262176 | tf_op jit(solution)/shard_map/all_to_all | solution.py:243
  131.6 0.2 copy.13
  131.8 0.9 reshape.58
  (7 shorter events, 0.1 us)
Async XLA Ops:
  0.6 2.2 %copy-start.2 = (bf16[16,2,32,2048]{3,2,1,0:T(8,128)(2,1)S(1)}, bf16[16,2,32,2048]{3,2,1,0:T(8,128)(2,1)}, u32[]{:S(2)}) copy-start(bf16[16,2,32,2048]{3,2,1,0:T(8,128)(2,1)} %param.3) | copy-start | bytes 12582916
  3.5 57.3 %copy-start.4 = (f32[2048]{0:T(1024)S(1)}, f32[2048]{0:T(1024)}, u32[]{:S(2)}) copy-start(f32[2048]{0:T(1024)} %param.4) | copy-start | bytes 24580
  3.5 57.3 %copy-start.5 = (s32[128,2]{0,1:T(2,128)S(1)}, s32[128,2]{0,1:T(2,128)}, u32[]{:S(2)}) copy-start(s32[128,2]{0,1:T(2,128)} %param.5) | copy-start | bytes 3076
  60.8 4.9 %copy-start = (bf16[8,1024,256]{2,1,0:T(8,128)(2,1)}, bf16[8,1024,256]{2,1,0:T(8,128)(2,1)S(1)}, u32[]{:S(2)}) copy-start(bf16[8,1024,256]{2,1,0:T(8,128)(2,1)S(1)} %all_to_all.25) | copy-start | bytes 12582916
  63.2 2.5 %collective-permute-start = (f32[64,16,128]{2,1,0:T(8,128)S(1)}, f32[64,16,128]{2,1,0:T(8,128)S(1)}, u32[]{:S(2)}, u32[]{:S(2)}) collective-permute-start(f32[64,16,128]{2,1,0:T(8,128)S(1)} %triads_other.1), channel_id=1, source_target_pairs={{0,8},{8,0},{1,9},{9,1},{2,10},{10,2},{3,11},{11,3},{4,12},{12,4},... | collective-permute-start | bytes 1572872 | tf_op jit(solution)/shard_map/ppermute | solution.py:248
  66.6 22.0 %all-to-all-start.1 = ((f32[64,16,128]{2,1,0:T(8,128)}), f32[64,16,128]{2,1,0:T(8,128)S(1)}, u32[]{:S(2)}, u32[]{:S(2)}) async-start(f32[64,16,128]{2,1,0:T(8,128)} %add.15), calls=%async_computation.1 | async-start | bytes 1048576 | tf_op jit(solution)/shard_map/all_to_all | solution.py:243
  74.8 2.2 %copy-start.3 = (bf16[16,2,32,2048]{3,2,1,0:T(8,128)(2,1)S(1)}, bf16[16,2,32,2048]{3,2,1,0:T(8,128)(2,1)}, u32[]{:S(2)}) copy-start(bf16[16,2,32,2048]{3,2,1,0:T(8,128)(2,1)} %param.3) | copy-start | bytes 12582916
  79.9 1.4 %collective-permute-start.1 = (f32[16,16,128]{2,1,0:T(8,128)S(1)}, f32[16,16,128]{2,1,0:T(8,128)S(1)}, u32[]{:S(2)}, u32[]{:S(2)}) collective-permute-start(f32[16,16,128]{2,1,0:T(8,128)S(1)} %density.1), channel_id=1, source_target_pairs={{0,8},{8,0},{1,9},{9,1},{2,10},{10,2},{3,11},{11,3},{4,12},{12,4},... | collective-permute-start | bytes 393224 | tf_op jit(solution)/shard_map/ppermute | solution.py:248
  81.4 5.6 %collective-permute-start.2 = (f32[16,16,128]{2,1,0:T(8,128)S(1)}, f32[16,16,128]{2,1,0:T(8,128)S(1)}, u32[]{:S(2)}, u32[]{:S(2)}) collective-permute-start(f32[16,16,128]{2,1,0:T(8,128)S(1)} %add.16), channel_id=1, source_target_pairs={{0,16},{16,0},{32,48},{48,32},{64,80},{80,64},{96,112},{112,96},{1... | collective-permute-start | bytes 393224 | tf_op jit(solution)/shard_map/ppermute | solution.py:248
  87.0 8.5 %collective-permute-start.3 = (f32[16,16,128]{2,1,0:T(8,128)S(1)}, f32[16,16,128]{2,1,0:T(8,128)S(1)}, u32[]{:S(2)}, u32[]{:S(2)}) collective-permute-start(f32[16,16,128]{2,1,0:T(8,128)S(1)} %add.17), channel_id=1, source_target_pairs={{0,32},{16,48},{32,0},{48,16},{64,96},{80,112},{96,64},{112,80},{1... | collective-permute-start | bytes 393224 | tf_op jit(solution)/shard_map/ppermute | solution.py:248
  90.3 12.3 %all-to-all-start.2 = ((f32[16,24,128]{2,1,0:T(8,128)}), f32[16,24,128]{2,1,0:T(8,128)S(1)}, u32[]{:S(2)}, u32[]{:S(2)}) async-start(f32[16,24,128]{2,1,0:T(8,128)} %power.1), calls=%async_computation.2 | async-start | bytes 393216 | tf_op jit(solution)/shard_map/all_to_all | solution.py:243
  95.5 29.4 %collective-permute-start.4 = (f32[16,16,128]{2,1,0:T(8,128)S(1)}, f32[16,16,128]{2,1,0:T(8,128)S(1)}, u32[]{:S(2)}, u32[]{:S(2)}) collective-permute-start(f32[16,16,128]{2,1,0:T(8,128)S(1)} %add.18), channel_id=1, source_target_pairs={{0,64},{16,80},{32,96},{48,112},{64,0},{80,16},{96,32},{112,48},{1... | collective-permute-start | bytes 393224 | tf_op jit(solution)/shard_map/ppermute | solution.py:248
  115.2 2.2 %copy-start.1 = (bf16[8,1024,256]{2,1,0:T(8,128)(2,1)S(1)}, bf16[8,1024,256]{2,1,0:T(8,128)(2,1)}, u32[]{:S(2)}) copy-start(bf16[8,1024,256]{2,1,0:T(8,128)(2,1)} %copy-done) | copy-start | bytes 12582916
  119.6 12.0 %all-to-all-start.4 = ((f32[8,32,256]{2,1,0:T(8,128)}), f32[8,32,256]{2,1,0:T(8,128)S(1)}, u32[]{:S(2)}, u32[]{:S(2)}) async-start(f32[8,32,256]{2,1,0:T(8,128)} %bitcast.11), calls=%async_computation.4 | async-start | bytes 524288 | tf_op jit(solution)/shard_map/all_to_all | solution.py:243

commit v3 on v2

--- a/solution.py
+++ b/solution.py
@@ -51,13 +51,13 @@
     length, points = rows.shape
     return pl.pallas_call(
         cut_kernel,
-        in_specs=[pl.BlockSpec(memory_space=pl.ANY)],
+        in_specs=[pl.BlockSpec(memory_space=pltpu.HBM)],
         out_specs=VMEM,
         out_shape=pltpu.VMEM((count, length, points // count), rows.dtype),
         scratch_shapes=[pltpu.SemaphoreType.DMA((count,))],
         compiler_params=params(),
         name="cut",
-    )(rows)
+    )(pltpu.with_memory_space_constraint(rows, pltpu.HBM))
 
 
 def density_kernel(spectra_ref, weights_ref, out_ref):
@@ -86,7 +86,7 @@
         ),
         compiler_params=params(24),
         name="density",
-    )(spectra, weights)
+    )(pltpu.with_memory_space_constraint(spectra, pltpu.HBM), weights)
 
 
 def triad_kernel(groups, mine, triads_ref, spectra_ref, weights_ref, out_ref):
@@ -187,10 +187,22 @@
     )(parts)
 
 
-def modes_kernel(triads_ref, spectra_ref, vectors_ref, out_ref, pairs_ref):
-    total = spectra_ref.shape[0]
+def modes_kernel(triads_ref, spectra_ref, vectors_ref, out_ref, pairs_ref, rows_ref, sems):
+    total, height, _ = spectra_ref.shape
     count, lanes = vectors_ref.shape
     blocks = lanes // 4
+
+    def fetch(s, q):
+        t = s * EACH + q
+        m = lax.rem(triads_ref[0, t] + triads_ref[1, t], total)
+        return pltpu.make_async_copy(
+            spectra_ref.at[m], rows_ref.at[s, pl.ds(q * height, height)], sems.at[s, q]
+        )
+
+    for s in range(count // EACH):
+        for q in range(EACH):
+            fetch(s, q).start()
+
     lane = lax.broadcasted_iota(jnp.int32, (1, lanes), 1)
     lower = lane < 2 * blocks
     sign = jnp.where(lax.rem(lax.div(lane, blocks), 2) == 0, 1.0, -1.0)
@@ -203,32 +215,32 @@
     pairs_ref[pl.ds(1, count, stride=2), :] = jnp.where(keep, swapped, 0.0)
     early = lax.broadcasted_iota(jnp.int32, (2 * EACH, 1), 0) < EACH
 
-    def step(s, carry):
-        picked = []
-        for q in range(EACH):
-            t = s * EACH + q
-            m = lax.rem(triads_ref[0, t] + triads_ref[1, t], total)
-            picked.append(spectra_ref[m])
-        right = jnp.concatenate(picked, axis=0)
-        pair = pairs_ref[pl.ds(pl.multiple_of(s * 2 * EACH, 2 * EACH), 2 * EACH), :]
-        left = jnp.concatenate(
-            [jnp.where(early, pair, 0.0), jnp.where(early, 0.0, pair)], axis=1
-        ).astype(jnp.bfloat16)
-        out_ref[s] = jnp.dot(left, right, preferred_element_type=jnp.float32)
-        return carry
-
-    lax.fori_loop(0, count // EACH, step, 0, unroll=16)
+    for first in range(0, count // EACH, 8):
+        for s in range(first, first + 8):
+            for q in range(EACH):
+                fetch(s, q).wait()
+        for s in range(first, first + 8):
+            pair = pairs_ref[pl.ds(s * 2 * EACH, 2 * EACH), :]
+            left = jnp.concatenate(
+                [jnp.where(early, pair, 0.0), jnp.where(early, 0.0, pair)], axis=1
+            ).astype(jnp.bfloat16)
+            out_ref[s] = jnp.dot(left, rows_ref[s], preferred_element_type=jnp.float32)
 
 
 def modes(triads, spectra, vectors):
     count, lanes = vectors.shape
     total, rows, points = spectra.shape
+    steps = count // EACH
     return pl.pallas_call(
         modes_kernel,
-        in_specs=[SMEM, VMEM, VMEM],
+        in_specs=[SMEM, pl.BlockSpec(memory_space=pltpu.HBM), VMEM],
         out_specs=VMEM,
-        out_shape=jax.ShapeDtypeStruct((count // EACH, 2 * EACH, points), jnp.float32),
-        scratch_shapes=[pltpu.VMEM((2 * count, lanes), jnp.float32)],
+        out_shape=jax.ShapeDtypeStruct((steps, 2 * EACH, points), jnp.float32),
+        scratch_shapes=[
+            pltpu.VMEM((2 * count, lanes), jnp.float32),
+            pltpu.VMEM((steps, EACH * rows, points), spectra.dtype),
+            pltpu.SemaphoreType.DMA((steps, EACH)),
+        ],
         cost_estimate=pl.CostEstimate(
             flops=count * rows * points * 4,
             bytes_accessed=spectra.size * 2,
@@ -236,7 +248,7 @@
         ),
         compiler_params=params(),
         name="modes",
-    )(triads, spectra, vectors)
+    )(triads, pltpu.with_memory_space_constraint(spectra, pltpu.HBM), vectors)
 
 
 def exchange(value, axis):
@@ -277,20 +289,28 @@
 
     dens = density_parts(spectra.reshape(f_dev, 2 * blocks, points), late_weights)
     dens = dens + swap(dens, "core", 1)
-    for bit in (1, 2, 4):
-        dens = dens + swap(dens, "line", bit)
+
+    payload = power(parts, 1.0 / math.sqrt(blocks * point_count), lines * cores)
+    payload, dens = lax.optimization_barrier((payload, dens))
+    payload = exchange(payload, ("line", "core"))
+    dens = dens + swap(dens, "line", 1)
+
+    bispectrum = payload[:, : blocks // 2]
+    rows = payload[:, blocks // 2]
+    sent = jnp.broadcast_to(rows[None], (groups, *rows.shape))
+    sent, dens, bispectrum = lax.optimization_barrier((sent, dens, bispectrum))
+    vectors = exchange(sent, "freq")
+    dens = dens + swap(dens, "line", 2)
+
+    fields = modes(triads, turned, vectors.reshape(groups * per_group, -1))
+    fields, dens, rows = lax.optimization_barrier((fields, dens, rows))
+    fields = exchange(fields.reshape(groups, 2 * per_group, share), "freq")
+    dens = dens + swap(dens, "line", 4)
+
+    bispectrum = unfolded(bispectrum)
     density = unfolded(dens * (1.0 / point_count))
-
-    payload = power(parts, 1.0 / math.sqrt(blocks * point_count), lines * cores)
-    payload = exchange(payload, ("line", "core"))
-    bispectrum = unfolded(payload[:, : blocks // 2])
-    rows = payload[:, blocks // 2]
     out_vectors = rows[:, : 2 * blocks].reshape(per_group, 2, blocks)
     energy = rows[:, 2 * blocks]
-
-    vectors = exchange(jnp.broadcast_to(rows[None], (groups, *rows.shape)), "freq")
-    fields = modes(triads, turned, vectors.reshape(groups * per_group, -1))
-    fields = exchange(fields.reshape(groups, 2 * per_group, share), "freq")
     mode_fields = fields.swapaxes(0, 1).reshape(per_group, 2, points)
     return (bispectrum, density, out_vectors, energy, mode_fields)
 

time: 135 us -> 136 us (level)
  local copies, waits for them, and re-layouts: 11.6 us -> 5.02 us
  Pallas kernels: 12.3 us -> 18.5 us
  waiting for transfers between devices: 11.6 us -> 17.5 us
  starting transfers between devices: 25.5 us -> 23.3 us
  blocking collectives: 69.9 us -> 67.9 us
    unnamed x12 -> x6, local copies, waits for them, and re-layouts: 6.57 us -> 0.02 us
    pallas_call x2, Pallas kernels: 2.92 us -> 7.31 us  [the longest x1 5.03 us: modes(): pl.pallas_call(modes_kernel, in_specs=[SMEM, pl.BlockSpec(memory_space=pl...]
    all_to_all x3, waiting for transfers between devices: 6.18 us -> 10.1 us  [exchange(): return lax.all_to_all(value, axis, 0, 0, tiled=True)]
    all_to_all x2, blocking collectives: 69.9 us -> 67.9 us  [exchange(): return lax.all_to_all(value, axis, 0, 0, tiled=True)]
    ppermute x5, waiting for transfers between devices: 5.43 us -> 7.43 us  [swap(): return lax.ppermute(value, axis, [(i, i ^ bit) for i in range(length)])]
    pallas_call x1, Pallas kernels: 2.93 us -> 4.73 us  [density_parts(): pl.pallas_call(density_kernel, grid=(freqs // EACH,), in_specs=[pl.BlockS...]
    all_to_all x3, starting transfers between devices: 18.8 us -> 17.1 us  [exchange(): return lax.all_to_all(value, axis, 0, 0, tiled=True)]
  transfers between devices with their start and end apart: 8 -> 8, of which waited for: 4 -> 4; matrix products, arithmetic and copies ran while one was open for 3% -> 3% of each run, Pallas kernels for 7% -> 9%
where the time goes in v3:
time: 136 us; the launch traced here: 134 us
  blocking collectives  67.9 us (50%)
  starting transfers between devices  23.3 us (17%)
  Pallas kernels  18.5 us (14%)
  waiting for transfers between devices  17.5 us (13%)
  local copies, waits for them, and re-layouts  5.02 us (4%)
    all_to_all x2, blocking collectives, exchange(): return lax.all_to_all(value, axis, 0, 0, tiled=True)  67.9 us
    all_to_all x3, starting transfers between devices, exchange(): return lax.all_to_all(value, axis, 0, 0, tiled=True)  17.1 us
    all_to_all x3, waiting for transfers between devices, exchange(): return lax.all_to_all(value, axis, 0, 0, tiled=True)  10.1 us
    ppermute x5, waiting for transfers between devices, swap(): return lax.ppermute(value, axis, [(i, i ^ bit) for i in range(length)])  7.43 us
    ppermute x5, starting transfers between devices, swap(): return lax.ppermute(value, axis, [(i, i ^ bit) for i in range(length)])  6.28 us
    pallas_call x1, Pallas kernels, modes(): pl.pallas_call(modes_kernel, in_specs=[SMEM, pl.BlockSpec(memory_space=pl...  5.03 us
    pallas_call x2, Pallas kernels, triad_parts(): pl.pallas_call(lambda *refs: triad_kernel(groups, mine, *refs), in_specs=...  4.79 us
    pallas_call x1, Pallas kernels, density_parts(): pl.pallas_call(density_kernel, grid=(freqs // EACH,), in_specs=[pl.BlockS...  4.73 us
  transfers between devices with their start and end apart: 8, of which 4 were waited for; matrix products, arithmetic and copies ran while one was open for 3% of the time, Pallas kernels for 9%

profile of v3, /device:TPU:6, one launch (start us, length us, event | category | flops | bytes accessed | tf_op | source)
XLA Modules:
  0.0 134.0 jit_solution(7574914411228297528)
XLA Ops:
  0.6 2.3 %cut.1 = bf16[8,1024,256]{2,1,0:T(8,128)(2,1)S(1)} custom-call(bf16[1024,2048]{1,0:T(8,128)(2,1)} %bitcast.24), custom_call_target="tpu_custom_call" | custom-call | tf_op jit(solution)/shard_map/cut/pallas_call | solution.py:52
  2.9 0.0 copy-start.1
  2.9 0.0 copy-start.2
  2.9 57.3 %all_to_all.25 = bf16[8,1024,256]{2,1,0:T(8,128)(2,1)S(1)} all-to-all(bf16[8,1024,256]{2,1,0:T(8,128)(2,1)S(1)} %cut.1), channel_id=1, replica_groups=mesh['line'=8,'core'=2,'freq'=8] {'freq'}, dimensions={0} | all-to-all | bytes 8388608 | tf_op jit(solution)/shard_map/all_to_all | solution.py:255
  60.2 0.0 copy-start
  60.2 0.0 copy-done.1
  60.2 0.0 copy-done.2
  60.2 2.4 %triads_other.1 = f32[64,16,128]{2,1,0:T(8,128)S(1)} custom-call(s32[2,128]{1,0:T(2,128)S(1)} %bitcast.21, bf16[128,64,256]{2,1,0:T(8,128)(2,1)S(1)} %bitcast.14, f32[1,2048]{1,0:T(1,128)S(1)} %bitcast.18), custom_call_target="tpu_custom_call" | custom-call | flops 268435456 | bytes 4194304 | tf_op jit(solution)/shard_map/triads_other/pallas_call | solution.py:121
  62.6 0.1 collective-permute-start
  62.7 2.4 %triads_own.1 = f32[64,16,128]{2,1,0:T(8,128)S(1)} custom-call(s32[2,128]{1,0:T(2,128)S(1)} %bitcast.22, bf16[128,64,256]{2,1,0:T(8,128)(2,1)S(1)} %bitcast.15, f32[1,2048]{1,0:T(1,128)S(1)} %bitcast.19), custom_call_target="tpu_custom_call" | custom-call | flops 268435456 | bytes 4194304 | tf_op jit(solution)/shard_map/triads_own/pallas_call | solution.py:121
  65.1 0.0 copy-done
  65.1 0.0 collective-permute-done
  65.1 0.9 add.15
  66.0 8.2 %all-to-all-start.1 = ((f32[64,16,128]{2,1,0:T(8,128)}), f32[64,16,128]{2,1,0:T(8,128)S(1)}, u32[]{:S(2)}, u32[]{:S(2)}) async-start(f32[64,16,128]{2,1,0:T(8,128)} %add.15), calls=%async_computation.1 | async-start | bytes 1048576 | tf_op jit(solution)/shard_map/all_to_all | solution.py:255
  74.2 4.7 %density.1 = f32[16,16,128]{2,1,0:T(8,128)S(1)} custom-call(bf16[16,64,2048]{2,1,0:T(8,128)(2,1)} %bitcast.25, f32[1,2048]{1,0:T(1,128)S(1)} %bitcast.20), custom_call_target="tpu_custom_call" | custom-call | flops 268435456 | bytes 4194304 | tf_op jit(solution)/shard_map/density/pallas_call | solution.py:73
  78.9 0.1 collective-permute-start.1
  79.0 1.3 collective-permute-done.1
  80.4 6.1 %all-to-all-done.1.refs_0_ = f32[64,16,128]{2,1,0:T(8,128)S(1)} async-done(((f32[64,16,128]{2,1,0:T(8,128)}), f32[64,16,128]{2,1,0:T(8,128)S(1)}, u32[]{:S(2)}, u32[]{:S(2)}) %all-to-all-start.1) | async-done | bytes 524320 | tf_op jit(solution)/shard_map/all_to_all | solution.py:255
  86.5 1.7 %power.1 = f32[16,24,128]{2,1,0:T(8,128)} custom-call(f32[64,16,128]{2,1,0:T(8,128)S(1)} %all-to-all-done.1.refs_0_), custom_call_target="tpu_custom_call" | custom-call | tf_op jit(solution)/shard_map/power/pallas_call | solution.py:180
  88.2 3.5 %all-to-all-start.2 = ((f32[16,24,128]{2,1,0:T(8,128)}), f32[16,24,128]{2,1,0:T(8,128)S(1)}, u32[]{:S(2)}, u32[]{:S(2)}) async-start(f32[16,24,128]{2,1,0:T(8,128)} %power.1), calls=%async_computation.2 | async-start | bytes 393216 | tf_op jit(solution)/shard_map/all_to_all | solution.py:255
  91.7 1.8 %collective-permute-start.2 = (f32[16,16,128]{2,1,0:T(8,128)S(1)}, f32[16,16,128]{2,1,0:T(8,128)S(1)}, u32[]{:S(2)}, u32[]{:S(2)}) collective-permute-start(f32[16,16,128]{2,1,0:T(8,128)S(1)} %add.16), channel_id=1, source_target_pairs={{0,16},{16,0},{32,48},{48,32},{64,80},{80,64},{96,112},{112,96},{1... | collective-permute-start | bytes 393224 | tf_op jit(solution)/shard_map/ppermute | solution.py:260
  93.5 6.1 %collective-permute-done.2 = f32[16,16,128]{2,1,0:T(8,128)S(1)} collective-permute-done((f32[16,16,128]{2,1,0:T(8,128)S(1)}, f32[16,16,128]{2,1,0:T(8,128)S(1)}, u32[]{:S(2)}, u32[]{:S(2)}) %collective-permute-start.2) | collective-permute-done | bytes 131104 | tf_op jit(solution)/shard_map/ppermute | solution.py:260
  99.6 0.0 all-to-all-done.2
  99.7 1.6 %collective-permute-start.3 = (f32[16,16,128]{2,1,0:T(8,128)S(1)}, f32[16,16,128]{2,1,0:T(8,128)S(1)}, u32[]{:S(2)}, u32[]{:S(2)}) collective-permute-start(f32[16,16,128]{2,1,0:T(8,128)S(1)} %add.17), channel_id=1, source_target_pairs={{0,32},{16,48},{32,0},{48,16},{64,96},{80,112},{96,64},{112,80},{1... | collective-permute-start | bytes 393224 | tf_op jit(solution)/shard_map/ppermute | solution.py:260
  101.2 10.6 %all_to_all.26 = f32[8,16,128]{2,1,0:T(8,128)S(1)} all-to-all(f32[8,16,128]{2,1,0:T(8,128)S(1)} %broadcast_in_dim.8), channel_id=1, replica_groups=mesh['line'=8,'core'=2,'freq'=8] {'freq'}, dimensions={0} | all-to-all | bytes 131072 | tf_op jit(solution)/shard_map/all_to_all | solution.py:255
  111.8 5.0 %modes.1 = f32[32,8,256]{2,1,0:T(8,128)} custom-call(s32[2,128]{1,0:T(2,128)S(1)} %bitcast.23, bf16[128,64,256]{2,1,0:T(8,128)(2,1)} %bitcast.16, f32[128,128]{1,0:T(8,128)S(1)} %bitcast.17), custom_call_target="tpu_custom_call" | custom-call | flops 8388608 | bytes 4194304 | tf_op jit(solution)/shard_map/modes/pallas_call | solution.py:234
  116.9 0.0 collective-permute-done.3
  116.9 2.7 %collective-permute-start.4 = (f32[16,16,128]{2,1,0:T(8,128)S(1)}, f32[16,16,128]{2,1,0:T(8,128)S(1)}, u32[]{:S(2)}, u32[]{:S(2)}) collective-permute-start(f32[16,16,128]{2,1,0:T(8,128)S(1)} %add.18), channel_id=1, source_target_pairs={{0,64},{16,80},{32,96},{48,112},{64,0},{80,16},{96,32},{112,48},{1... | collective-permute-start | bytes 393224 | tf_op jit(solution)/shard_map/ppermute | solution.py:260
  119.6 0.4 reshape.51
  120.1 0.9 copy.11
  120.9 5.3 %all-to-all-start.4 = ((f32[8,32,256]{2,1,0:T(8,128)}), f32[8,32,256]{2,1,0:T(8,128)S(1)}, u32[]{:S(2)}, u32[]{:S(2)}) async-start(f32[8,32,256]{2,1,0:T(8,128)} %bitcast.11), calls=%async_computation.4 | async-start | bytes 524288 | tf_op jit(solution)/shard_map/all_to_all | solution.py:255
  126.3 0.7 reshape.56
  126.9 0.7 slice_reduce_fusion
  127.6 0.0 collective-permute-done.4
  127.7 0.4 reshape.54
  128.1 0.9 copy.12
  129.0 4.0 %all-to-all-done.4 = f32[8,32,256]{2,1,0:T(8,128)S(1)} async-done(((f32[8,32,256]{2,1,0:T(8,128)}), f32[8,32,256]{2,1,0:T(8,128)S(1)}, u32[]{:S(2)}, u32[]{:S(2)}) %all-to-all-start.4) | async-done | bytes 262176 | tf_op jit(solution)/shard_map/all_to_all | solution.py:255
  132.9 0.2 copy.13
  133.1 0.9 reshape.58
  (7 shorter events, 0.1 us)
Async XLA Ops:
  2.9 57.3 %copy-start.1 = (f32[2048]{0:T(1024)S(1)}, f32[2048]{0:T(1024)}, u32[]{:S(2)}) copy-start(f32[2048]{0:T(1024)} %param.4) | copy-start | bytes 24580
  2.9 57.3 %copy-start.2 = (s32[128,2]{0,1:T(2,128)S(1)}, s32[128,2]{0,1:T(2,128)}, u32[]{:S(2)}) copy-start(s32[128,2]{0,1:T(2,128)} %param.5) | copy-start | bytes 3076
  60.2 4.9 %copy-start = (bf16[8,1024,256]{2,1,0:T(8,128)(2,1)}, bf16[8,1024,256]{2,1,0:T(8,128)(2,1)S(1)}, u32[]{:S(2)}) copy-start(bf16[8,1024,256]{2,1,0:T(8,128)(2,1)S(1)} %all_to_all.25) | copy-start | bytes 12582916
  62.6 2.5 %collective-permute-start = (f32[64,16,128]{2,1,0:T(8,128)S(1)}, f32[64,16,128]{2,1,0:T(8,128)S(1)}, u32[]{:S(2)}, u32[]{:S(2)}) collective-permute-start(f32[64,16,128]{2,1,0:T(8,128)S(1)} %triads_other.1), channel_id=1, source_target_pairs={{0,8},{8,0},{1,9},{9,1},{2,10},{10,2},{3,11},{11,3},{4,12},{12,4},... | collective-permute-start | bytes 1572872 | tf_op jit(solution)/shard_map/ppermute | solution.py:260
  66.0 20.5 %all-to-all-start.1 = ((f32[64,16,128]{2,1,0:T(8,128)}), f32[64,16,128]{2,1,0:T(8,128)S(1)}, u32[]{:S(2)}, u32[]{:S(2)}) async-start(f32[64,16,128]{2,1,0:T(8,128)} %add.15), calls=%async_computation.1 | async-start | bytes 1048576 | tf_op jit(solution)/shard_map/all_to_all | solution.py:255
  78.9 1.4 %collective-permute-start.1 = (f32[16,16,128]{2,1,0:T(8,128)S(1)}, f32[16,16,128]{2,1,0:T(8,128)S(1)}, u32[]{:S(2)}, u32[]{:S(2)}) collective-permute-start(f32[16,16,128]{2,1,0:T(8,128)S(1)} %density.1), channel_id=1, source_target_pairs={{0,8},{8,0},{1,9},{9,1},{2,10},{10,2},{3,11},{11,3},{4,12},{12,4},... | collective-permute-start | bytes 393224 | tf_op jit(solution)/shard_map/ppermute | solution.py:260
  88.2 11.5 %all-to-all-start.2 = ((f32[16,24,128]{2,1,0:T(8,128)}), f32[16,24,128]{2,1,0:T(8,128)S(1)}, u32[]{:S(2)}, u32[]{:S(2)}) async-start(f32[16,24,128]{2,1,0:T(8,128)} %power.1), calls=%async_computation.2 | async-start | bytes 393216 | tf_op jit(solution)/shard_map/all_to_all | solution.py:255
  91.7 7.9 %collective-permute-start.2 = (f32[16,16,128]{2,1,0:T(8,128)S(1)}, f32[16,16,128]{2,1,0:T(8,128)S(1)}, u32[]{:S(2)}, u32[]{:S(2)}) collective-permute-start(f32[16,16,128]{2,1,0:T(8,128)S(1)} %add.16), channel_id=1, source_target_pairs={{0,16},{16,0},{32,48},{48,32},{64,80},{80,64},{96,112},{112,96},{1... | collective-permute-start | bytes 393224 | tf_op jit(solution)/shard_map/ppermute | solution.py:260
  99.7 17.2 %collective-permute-start.3 = (f32[16,16,128]{2,1,0:T(8,128)S(1)}, f32[16,16,128]{2,1,0:T(8,128)S(1)}, u32[]{:S(2)}, u32[]{:S(2)}) collective-permute-start(f32[16,16,128]{2,1,0:T(8,128)S(1)} %add.17), channel_id=1, source_target_pairs={{0,32},{16,48},{32,0},{48,16},{64,96},{80,112},{96,64},{112,80},{1... | collective-permute-start | bytes 393224 | tf_op jit(solution)/shard_map/ppermute | solution.py:260
  116.9 10.7 %collective-permute-start.4 = (f32[16,16,128]{2,1,0:T(8,128)S(1)}, f32[16,16,128]{2,1,0:T(8,128)S(1)}, u32[]{:S(2)}, u32[]{:S(2)}) collective-permute-start(f32[16,16,128]{2,1,0:T(8,128)S(1)} %add.18), channel_id=1, source_target_pairs={{0,64},{16,80},{32,96},{48,112},{64,0},{80,16},{96,32},{112,48},{1... | collective-permute-start | bytes 393224 | tf_op jit(solution)/shard_map/ppermute | solution.py:260
  120.9 12.0 %all-to-all-start.4 = ((f32[8,32,256]{2,1,0:T(8,128)}), f32[8,32,256]{2,1,0:T(8,128)S(1)}, u32[]{:S(2)}, u32[]{:S(2)}) async-start(f32[8,32,256]{2,1,0:T(8,128)} %bitcast.11), calls=%async_computation.4 | async-start | bytes 524288 | tf_op jit(solution)/shard_map/all_to_all | solution.py:255

commit v4 on v2

--- a/solution.py
+++ b/solution.py
@@ -51,47 +51,19 @@
     length, points = rows.shape
     return pl.pallas_call(
         cut_kernel,
-        in_specs=[pl.BlockSpec(memory_space=pl.ANY)],
+        in_specs=[pl.BlockSpec(memory_space=pltpu.HBM)],
         out_specs=VMEM,
         out_shape=pltpu.VMEM((count, length, points // count), rows.dtype),
         scratch_shapes=[pltpu.SemaphoreType.DMA((count,))],
         compiler_params=params(),
         name="cut",
-    )(rows)
-
-
-def density_kernel(spectra_ref, weights_ref, out_ref):
-    half = spectra_ref.shape[1] // 2
-    for f in range(spectra_ref.shape[0]):
-        rows = spectra_ref[f]
-        weighted = (rows.astype(jnp.float32) * weights_ref[...]).astype(jnp.bfloat16)
-        out_ref[f] = folded(gram(weighted[:half], weighted[half:], rows))
-
-
-def density_parts(spectra, weights):
-    freqs, rows, points = spectra.shape
-    return pl.pallas_call(
-        density_kernel,
-        grid=(freqs // EACH,),
-        in_specs=[
-            pl.BlockSpec((EACH, rows, points), lambda f: (f, 0, 0)),
-            pl.BlockSpec((1, points), lambda f: (0, 0)),
-        ],
-        out_specs=pl.BlockSpec((EACH, rows // 4, 2 * rows), lambda f: (f, 0, 0)),
-        out_shape=jax.ShapeDtypeStruct((freqs, rows // 4, 2 * rows), jnp.float32),
-        cost_estimate=pl.CostEstimate(
-            flops=freqs * rows * rows * points * 2,
-            bytes_accessed=spectra.size * 2,
-            transcendentals=0,
-        ),
-        compiler_params=params(24),
-        name="density",
-    )(spectra, weights)
-
-
-def triad_kernel(groups, mine, triads_ref, spectra_ref, weights_ref, out_ref):
+    )(pltpu.with_memory_space_constraint(rows, pltpu.HBM))
+
+
+def sums_kernel(groups, mine, triads_ref, spectra_ref, weights_ref, out_ref):
     total, rows, share = spectra_ref.shape
     half = rows // 2
+    fold = half // 2
     count = out_ref.shape[0]
     per_group = 2 * count // groups
     core = lax.axis_index("core")
@@ -109,33 +81,65 @@
         ar, ai, br, bi = first[:half], first[half:], second[:half], second[half:]
         re = ((ar * br - ai * bi) * weights).astype(jnp.bfloat16)
         im = ((ar * bi + ai * br) * weights).astype(jnp.bfloat16)
-        out_ref[j] = folded(gram(re, im, spectra_ref[m]))
+        out_ref[j, :fold] = folded(gram(re, im, spectra_ref[m]))
+        own = spectra_ref[t]
+        weighted = (own.astype(jnp.float32) * weights).astype(jnp.bfloat16)
+        out_ref[j, fold:] = folded(gram(weighted[:half], weighted[half:], own))
         return carry
 
-    lax.fori_loop(0, count, step, 0, unroll=32)
-
-
-def triad_parts(triads, spectra, weights, groups, mine):
+    lax.fori_loop(0, count, step, 0, unroll=16)
+
+
+def sums(triads, spectra, weights, groups, mine):
     count = triads.shape[1] // 2
     total, rows, points = spectra.shape
     return pl.pallas_call(
-        lambda *refs: triad_kernel(groups, mine, *refs),
+        lambda *refs: sums_kernel(groups, mine, *refs),
         in_specs=[SMEM, VMEM, VMEM],
         out_specs=VMEM,
-        out_shape=jax.ShapeDtypeStruct((count, rows // 4, 2 * rows), jnp.float32),
+        out_shape=jax.ShapeDtypeStruct((count, rows // 2, 2 * rows), jnp.float32),
         cost_estimate=pl.CostEstimate(
-            flops=count * rows * rows * points * 4,
+            flops=count * rows * rows * points * 8,
             bytes_accessed=spectra.size * 2,
             transcendentals=0,
         ),
         compiler_params=params(),
-        name="triads_own" if mine else "triads_other",
+        name="sums_own" if mine else "sums_other",
     )(triads, spectra, weights)
 
 
-def power_kernel(scale, parts_ref, out_ref):
-    total = jnp.sum(parts_ref[...], axis=0) * scale
-    half = total.shape[0]
+def pack_kernel(one_ref, two_ref, out_ref):
+    fold = one_ref.shape[1] // 2
+
+    def step(j, carry):
+        both = one_ref[j] + two_ref[j]
+        high = both[:fold].astype(jnp.bfloat16)
+        rest = both[:fold] - high.astype(jnp.float32)
+        out_ref[j, :fold] = high
+        out_ref[j, fold : 2 * fold] = rest.astype(jnp.bfloat16)
+        out_ref[j, 2 * fold :] = both[fold:].astype(jnp.bfloat16)
+        return carry
+
+    lax.fori_loop(0, one_ref.shape[0], step, 0, unroll=8)
+
+
+def pack(one, two):
+    count, rows, lanes = one.shape
+    return pl.pallas_call(
+        pack_kernel,
+        in_specs=[VMEM, VMEM],
+        out_specs=VMEM,
+        out_shape=jax.ShapeDtypeStruct((count, 3 * rows // 2, lanes), jnp.bfloat16),
+        compiler_params=params(),
+        name="pack",
+    )(one, two)
+
+
+def power_kernel(scales, parts_ref, out_ref):
+    half = parts_ref.shape[1] // 3
+    added = jnp.sum(parts_ref[...].astype(jnp.float32), axis=0)
+    total = (added[:half] + added[half : 2 * half]) * scales[0]
+    density = added[2 * half :] * scales[1]
     blocks = 2 * half
     lane = lax.broadcasted_iota(jnp.int32, (1, 4 * blocks), 1)
     lower = lane < 2 * blocks
@@ -169,19 +173,20 @@
     top = jnp.sum(re * re + im * im, axis=0, keepdims=True)
     energy = top / (blocks * (square(one) + 1.0))
     row = jnp.where(lower, one * sign, energy)
-    tail = jnp.broadcast_to(row, (out_ref.shape[1] - half, 4 * blocks))
+    tail = jnp.broadcast_to(row, (out_ref.shape[1] - 2 * half, 4 * blocks))
     for d in range(out_ref.shape[0]):
         out_ref[d, :half] = total
-        out_ref[d, half:] = tail
-
-
-def power(parts, scale, lines):
+        out_ref[d, half : 2 * half] = density
+        out_ref[d, 2 * half :] = tail
+
+
+def power(parts, scales, lines):
     _, rows, lanes = parts.shape
     return pl.pallas_call(
-        lambda *refs: power_kernel(scale, *refs),
+        lambda *refs: power_kernel(scales, *refs),
         in_specs=[VMEM],
         out_specs=VMEM,
-        out_shape=jax.ShapeDtypeStruct((lines, rows + 8, lanes), jnp.float32),
+        out_shape=jax.ShapeDtypeStruct((lines, 2 * rows // 3 + 8, lanes), jnp.float32),
         compiler_params=params(8),
         name="power",
     )(parts)
@@ -269,28 +274,24 @@
     send = cut(spectra.reshape(f_dev * 2 * blocks, points), groups)
     turned = exchange(send, "freq").reshape(groups * f_dev, 2 * blocks, share)
 
-    other = triad_parts(triads, turned, weights, groups, False)
+    other = sums(triads, turned, weights, groups, False)
     given = swap(other, "core", 1)
-    parts = triad_parts(triads, turned, weights, groups, True) + given
-    late_weights, parts = lax.optimization_barrier((weights, parts))
+    parts = pack(sums(triads, turned, weights, groups, True), given)
     parts = exchange(parts, ("line", "freq"))
 
-    dens = density_parts(spectra.reshape(f_dev, 2 * blocks, points), late_weights)
-    dens = dens + swap(dens, "core", 1)
-    for bit in (1, 2, 4):
-        dens = dens + swap(dens, "line", bit)
-    density = unfolded(dens * (1.0 / point_count))
-
-    payload = power(parts, 1.0 / math.sqrt(blocks * point_count), lines * cores)
+    scales = (1.0 / math.sqrt(blocks * point_count), 1.0 / point_count)
+    payload = power(parts, scales, lines * cores)
     payload = exchange(payload, ("line", "core"))
-    bispectrum = unfolded(payload[:, : blocks // 2])
-    rows = payload[:, blocks // 2]
-    out_vectors = rows[:, : 2 * blocks].reshape(per_group, 2, blocks)
-    energy = rows[:, 2 * blocks]
-
+    fold = blocks // 2
+    rows = payload[:, 2 * fold]
     vectors = exchange(jnp.broadcast_to(rows[None], (groups, *rows.shape)), "freq")
     fields = modes(triads, turned, vectors.reshape(groups * per_group, -1))
     fields = exchange(fields.reshape(groups, 2 * per_group, share), "freq")
+
+    bispectrum = unfolded(payload[:, :fold])
+    density = unfolded(payload[:, fold : 2 * fold])
+    out_vectors = rows[:, : 2 * blocks].reshape(per_group, 2, blocks)
+    energy = rows[:, 2 * blocks]
     mode_fields = fields.swapaxes(0, 1).reshape(per_group, 2, points)
     return (bispectrum, density, out_vectors, energy, mode_fields)
 

time: 135 us -> 132 us (0.978)
  blocking collectives: 69.9 us -> 102 us
  starting transfers between devices: 25.5 us -> 5.37 us
  waiting for transfers between devices: 11.6 us -> 2.68 us
  local copies, waits for them, and re-layouts: 11.6 us -> 5.03 us
    all_to_all x2 -> x4, blocking collectives: 69.9 us -> 102 us  [exchange(): return lax.all_to_all(value, axis, 0, 0, tiled=True)]
    all_to_all x3 -> x1, starting transfers between devices: 18.8 us -> 5.31 us  [exchange(): return lax.all_to_all(value, axis, 0, 0, tiled=True)]
    ppermute x5 -> x1, starting transfers between devices: 6.76 us -> 0.06 us  [swap(): return lax.ppermute(value, axis, [(i, i ^ bit) for i in range(length)])]
    unnamed x12 -> x4, local copies, waits for them, and re-layouts: 6.57 us -> 0.01 us
    ppermute x5 -> x1, waiting for transfers between devices: 5.43 us -> 0.01 us  [swap(): return lax.ppermute(value, axis, [(i, i ^ bit) for i in range(length)])]
    all_to_all x3 -> x1, waiting for transfers between devices: 6.18 us -> 2.67 us  [exchange(): return lax.all_to_all(value, axis, 0, 0, tiled=True)]
  transfers between devices with their start and end apart: 8 -> 2, of which waited for: 4 -> 1; matrix products, arithmetic and copies ran while one was open for 3% -> 3% of each run, Pallas kernels for 7% -> 3%
where the time goes in v4:
time: 132 us; the launch traced here: 129 us
  blocking collectives  102 us (77%)
  Pallas kernels  13.1 us (10%)
  starting transfers between devices  5.37 us (4%)
  local copies, waits for them, and re-layouts  5.03 us (4%)
  waiting for transfers between devices  2.68 us (2%)
    all_to_all x4, blocking collectives, exchange(): return lax.all_to_all(value, axis, 0, 0, tiled=True)  102 us
    pallas_call x2, Pallas kernels, sums(): pl.pallas_call(lambda *refs: sums_kernel(groups, mine, *refs), in_specs=[...  7.28 us
    all_to_all x1, starting transfers between devices, exchange(): return lax.all_to_all(value, axis, 0, 0, tiled=True)  5.31 us
    all_to_all x1, waiting for transfers between devices, exchange(): return lax.all_to_all(value, axis, 0, 0, tiled=True)  2.67 us
  transfers between devices with their start and end apart: 2, of which 1 were waited for; matrix products, arithmetic and copies ran while one was open for 3% of the time, Pallas kernels for 3%

profile of v4, /device:TPU:6, one launch (start us, length us, event | category | flops | bytes accessed | tf_op | source)
XLA Modules:
  0.0 129.3 jit_solution(607149897889856155)
XLA Ops:
  0.6 2.3 %cut.1 = bf16[8,1024,256]{2,1,0:T(8,128)(2,1)S(1)} custom-call(bf16[1024,2048]{1,0:T(8,128)(2,1)} %bitcast.22), custom_call_target="tpu_custom_call" | custom-call | tf_op jit(solution)/shard_map/cut/pallas_call | solution.py:52
  2.9 0.0 copy-start
  2.9 0.0 copy-start.1
  2.9 57.3 %all_to_all.25 = bf16[8,1024,256]{2,1,0:T(8,128)(2,1)S(1)} all-to-all(bf16[8,1024,256]{2,1,0:T(8,128)(2,1)S(1)} %cut.1), channel_id=1, replica_groups=mesh['line'=8,'core'=2,'freq'=8] {'freq'}, dimensions={0} | all-to-all | bytes 8388608 | tf_op jit(solution)/shard_map/all_to_all | solution.py:248
  60.2 0.0 copy-done
  60.2 0.0 copy-done.1
  60.2 3.6 %sums_other.1 = f32[64,32,128]{2,1,0:T(8,128)S(1)} custom-call(s32[2,128]{1,0:T(2,128)S(1)} %bitcast.19, bf16[128,64,256]{2,1,0:T(8,128)(2,1)S(1)} %bitcast.13, f32[1,2048]{1,0:T(1,128)S(1)} %bitcast.17), custom_call_target="tpu_custom_call" | custom-call | flops 536870912 | bytes 4194304 | tf_op jit(solution)/shard_map/sums_other/pallas_call | solution.py:96
  63.9 0.1 collective-permute-start
  63.9 3.6 %sums_own.1.one_ref = f32[64,32,128]{2,1,0:T(8,128)S(1)} custom-call(s32[2,128]{1,0:T(2,128)S(1)} %bitcast.20, bf16[128,64,256]{2,1,0:T(8,128)(2,1)S(1)} %bitcast.14, f32[1,2048]{1,0:T(1,128)S(1)} %bitcast.18), custom_call_target="tpu_custom_call" | custom-call | flops 536870912 | bytes 4194304 | tf_op jit(solution)/shard_map/sums_own/pallas_call | solution.py:96
  67.6 0.0 collective-permute-done.two_ref
  67.6 0.2 pack.1
  67.8 22.9 %all_to_all.26.refs_0_ = bf16[64,48,128]{2,1,0:T(8,128)(2,1)S(1)} all-to-all(bf16[64,48,128]{2,1,0:T(8,128)(2,1)S(1)} %pack.1), channel_id=1, replica_groups=mesh['line'=8,'core'=2,'freq'=8] {'line','freq'}, dimensions={0} | all-to-all | bytes 1572864 | tf_op jit(solution)/shard_map/all_to_all | solution.py:248
  90.8 1.0 power.1
  91.8 10.9 %all_to_all.27 = f32[16,40,128]{2,1,0:T(8,128)S(1)} all-to-all(f32[16,40,128]{2,1,0:T(8,128)S(1)} %power.1), channel_id=1, replica_groups=mesh['line'=8,'core'=2,'freq'=8] {'line','core'}, dimensions={0} | all-to-all | bytes 655360 | tf_op jit(solution)/shard_map/all_to_all | solution.py:248
  102.7 11.3 %all_to_all.28 = f32[8,16,128]{2,1,0:T(8,128)S(1)} all-to-all(f32[8,16,128]{2,1,0:T(8,128)S(1)} %broadcast_in_dim.2), channel_id=1, replica_groups=mesh['line'=8,'core'=2,'freq'=8] {'freq'}, dimensions={0} | all-to-all | bytes 131072 | tf_op jit(solution)/shard_map/all_to_all | solution.py:248
  114.1 2.2 %modes.1 = f32[32,8,256]{2,1,0:T(8,128)} custom-call(s32[2,128]{1,0:T(2,128)S(1)} %bitcast.21, bf16[128,64,256]{2,1,0:T(8,128)(2,1)S(1)} %bitcast.15, f32[128,128]{1,0:T(8,128)S(1)} %bitcast.16), custom_call_target="tpu_custom_call" | custom-call | flops 8388608 | bytes 4194304 | tf_op jit(solution)/shard_map/modes/pallas_call | solution.py:231
  116.3 5.3 %all-to-all-start.4 = ((f32[8,32,256]{2,1,0:T(8,128)}), f32[8,32,256]{2,1,0:T(8,128)S(1)}, u32[]{:S(2)}, u32[]{:S(2)}) async-start(f32[8,32,256]{2,1,0:T(8,128)} %bitcast.10), calls=%async_computation.4 | async-start | bytes 524288 | tf_op jit(solution)/shard_map/all_to_all | solution.py:248
  121.7 0.7 reshape.51
  122.3 0.4 reshape.49
  122.8 0.9 copy.12
  123.6 0.4 reshape.47
  124.1 0.9 copy.11
  124.9 0.7 slice_reduce_fusion
  125.6 2.7 %all-to-all-done.4 = f32[8,32,256]{2,1,0:T(8,128)S(1)} async-done(((f32[8,32,256]{2,1,0:T(8,128)}), f32[8,32,256]{2,1,0:T(8,128)S(1)}, u32[]{:S(2)}, u32[]{:S(2)}) %all-to-all-start.4) | async-done | bytes 262176 | tf_op jit(solution)/shard_map/all_to_all | solution.py:248
  128.3 0.2 copy.13
  128.5 0.9 reshape.54
  (3 shorter events, 0.0 us)
Async XLA Ops:
  2.9 57.3 %copy-start = (f32[2048]{0:T(1024)S(1)}, f32[2048]{0:T(1024)}, u32[]{:S(2)}) copy-start(f32[2048]{0:T(1024)} %param.4) | copy-start | bytes 24580
  2.9 57.3 %copy-start.1 = (s32[128,2]{0,1:T(2,128)S(1)}, s32[128,2]{0,1:T(2,128)}, u32[]{:S(2)}) copy-start(s32[128,2]{0,1:T(2,128)} %param.5) | copy-start | bytes 3076
  63.9 3.7 %collective-permute-start = (f32[64,32,128]{2,1,0:T(8,128)S(1)}, f32[64,32,128]{2,1,0:T(8,128)S(1)}, u32[]{:S(2)}, u32[]{:S(2)}) collective-permute-start(f32[64,32,128]{2,1,0:T(8,128)S(1)} %sums_other.1), channel_id=1, source_target_pairs={{0,8},{8,0},{1,9},{9,1},{2,10},{10,2},{3,11},{11,3},{4,12},{12,4},... | collective-permute-start | bytes 3145736 | tf_op jit(solution)/shard_map/ppermute | solution.py:253
  116.3 12.0 %all-to-all-start.4 = ((f32[8,32,256]{2,1,0:T(8,128)}), f32[8,32,256]{2,1,0:T(8,128)S(1)}, u32[]{:S(2)}, u32[]{:S(2)}) async-start(f32[8,32,256]{2,1,0:T(8,128)} %bitcast.10), calls=%async_computation.4 | async-start | bytes 524288 | tf_op jit(solution)/shard_map/all_to_all | solution.py:248

commit v5 on v4

--- a/solution.py
+++ b/solution.py
@@ -19,13 +19,11 @@
     return pltpu.CompilerParams(vmem_limit_bytes=mib << 20)
 
 
-def gram(left_re, left_im, right):
+def gram(left, right):
     half = right.shape[0] // 2
-    right_re, right_im = right[:half], right[half:]
-    turned = jnp.concatenate([right_im, -right_re], axis=0)
-    return lax.dot_general(
-        left_re, right, NT, preferred_element_type=jnp.float32
-    ) + lax.dot_general(left_im, turned, NT, preferred_element_type=jnp.float32)
+    joined = lax.dot_general(left, right, NT, preferred_element_type=jnp.float32)
+    upper, lower = joined[:half], joined[half:]
+    return upper + jnp.concatenate([lower[:, half:], -lower[:, :half]], axis=1)
 
 
 def folded(matrix):
@@ -81,13 +79,14 @@
         ar, ai, br, bi = first[:half], first[half:], second[:half], second[half:]
         re = ((ar * br - ai * bi) * weights).astype(jnp.bfloat16)
         im = ((ar * bi + ai * br) * weights).astype(jnp.bfloat16)
-        out_ref[j, :fold] = folded(gram(re, im, spectra_ref[m]))
+        product = jnp.concatenate([re, im], axis=0)
+        out_ref[j, :fold] = folded(gram(product, spectra_ref[m]))
         own = spectra_ref[t]
         weighted = (own.astype(jnp.float32) * weights).astype(jnp.bfloat16)
-        out_ref[j, fold:] = folded(gram(weighted[:half], weighted[half:], own))
+        out_ref[j, fold:] = folded(gram(weighted, own))
         return carry
 
-    lax.fori_loop(0, count, step, 0, unroll=16)
+    lax.fori_loop(0, count, step, 0, unroll=32)
 
 
 def sums(triads, spectra, weights, groups, mine):
@@ -219,7 +218,8 @@
         left = jnp.concatenate(
             [jnp.where(early, pair, 0.0), jnp.where(early, 0.0, pair)], axis=1
         ).astype(jnp.bfloat16)
-        out_ref[s] = jnp.dot(left, right, preferred_element_type=jnp.float32)
+        mixed = jnp.dot(left, right, preferred_element_type=jnp.float32)
+        out_ref[s] = mixed.astype(out_ref.dtype)
         return carry
 
     lax.fori_loop(0, count // EACH, step, 0, unroll=16)
@@ -232,7 +232,7 @@
         modes_kernel,
         in_specs=[SMEM, VMEM, VMEM],
         out_specs=VMEM,
-        out_shape=jax.ShapeDtypeStruct((count // EACH, 2 * EACH, points), jnp.float32),
+        out_shape=jax.ShapeDtypeStruct((count // EACH, 2 * EACH, points), jnp.bfloat16),
         scratch_shapes=[pltpu.VMEM((2 * count, lanes), jnp.float32)],
         cost_estimate=pl.CostEstimate(
             flops=count * rows * points * 4,
@@ -244,6 +244,73 @@
     )(triads, spectra, vectors)
 
 
+def spread_kernel(payload_ref, out_ref):
+    rows = payload_ref[:, payload_ref.shape[1] - 1]
+    for d in range(out_ref.shape[0]):
+        out_ref[d] = rows
+
+
+def spread(payload, groups):
+    count, _, lanes = payload.shape
+    return pl.pallas_call(
+        spread_kernel,
+        in_specs=[VMEM],
+        out_specs=VMEM,
+        out_shape=jax.ShapeDtypeStruct((groups, count, lanes), jnp.float32),
+        compiler_params=params(8),
+        name="spread",
+    )(payload)
+
+
+def finish_kernel(fields_ref, payload_ref, bis_ref, dens_ref, vec_ref, energy_ref, modes_ref):
+    count, _, lanes = payload_ref.shape
+    blocks = lanes // 4
+    fold = blocks // 2
+    share = fields_ref.shape[2]
+    for t in range(count):
+        for first, to_ref in ((0, bis_ref), (fold, dens_ref)):
+            packed = payload_ref[t, first : first + fold]
+            for part in range(4):
+                low, ri = part // 2, part % 2
+                piece = packed[:, part * blocks : (part + 1) * blocks]
+                to_ref[t, ri, low * fold : (low + 1) * fold, :] = piece
+    rows = payload_ref[:, payload_ref.shape[1] - 1]
+    for t in range(count):
+        for ri in range(2):
+            vec_ref[t, ri : ri + 1, :] = rows[t : t + 1, ri * blocks : (ri + 1) * blocks]
+    lane = lax.broadcasted_iota(jnp.int32, rows.shape, 1)
+    index = lax.broadcasted_iota(jnp.int32, rows.shape, 0)
+    own = jnp.where(lane == index + 2 * blocks, rows, 0.0)
+    line = pltpu.roll(jnp.sum(own, axis=0, keepdims=True), 2 * blocks, 1)
+    energy_ref[...] = line[:, :count]
+    for g in range(fields_ref.shape[0]):
+        block = fields_ref[g].astype(jnp.float32)
+        for t in range(count):
+            modes_ref[t, :, g * share : (g + 1) * share] = block[2 * t : 2 * t + 2]
+
+
+def finish(fields, payload):
+    count, _, lanes = payload.shape
+    groups, _, share = fields.shape
+    blocks = lanes // 4
+    square = jax.ShapeDtypeStruct((count, 2, blocks, blocks), jnp.float32)
+    bispectrum, density, vectors, energy, mode_fields = pl.pallas_call(
+        finish_kernel,
+        in_specs=[VMEM, VMEM],
+        out_specs=[VMEM] * 5,
+        out_shape=[
+            square,
+            square,
+            jax.ShapeDtypeStruct((count, 2, blocks), jnp.float32),
+            jax.ShapeDtypeStruct((1, count), jnp.float32),
+            jax.ShapeDtypeStruct((count, 2, groups * share), jnp.float32),
+        ],
+        compiler_params=params(8),
+        name="finish",
+    )(fields, payload)
+    return (bispectrum, density, vectors, energy.reshape(count), mode_fields)
+
+
 def exchange(value, axis):
     return lax.all_to_all(value, axis, 0, 0, tiled=True)
 
@@ -251,13 +318,6 @@
 def swap(value, axis, bit):
     length = lax.axis_size(axis)
     return lax.ppermute(value, axis, [(i, i ^ bit) for i in range(length)])
-
-
-def unfolded(packed):
-    n, half, lanes = packed.shape
-    blocks = 2 * half
-    parted = packed.reshape(n, half, 2, 2, blocks)
-    return parted.transpose(0, 3, 2, 1, 4).reshape(n, 2, blocks, blocks)
 
 
 def local(spectra, weights, triads):
@@ -282,18 +342,10 @@
     scales = (1.0 / math.sqrt(blocks * point_count), 1.0 / point_count)
     payload = power(parts, scales, lines * cores)
     payload = exchange(payload, ("line", "core"))
-    fold = blocks // 2
-    rows = payload[:, 2 * fold]
-    vectors = exchange(jnp.broadcast_to(rows[None], (groups, *rows.shape)), "freq")
+    vectors = exchange(spread(payload, groups), "freq")
     fields = modes(triads, turned, vectors.reshape(groups * per_group, -1))
     fields = exchange(fields.reshape(groups, 2 * per_group, share), "freq")
-
-    bispectrum = unfolded(payload[:, :fold])
-    density = unfolded(payload[:, fold : 2 * fold])
-    out_vectors = rows[:, : 2 * blocks].reshape(per_group, 2, blocks)
-    energy = rows[:, 2 * blocks]
-    mode_fields = fields.swapaxes(0, 1).reshape(per_group, 2, points)
-    return (bispectrum, density, out_vectors, energy, mode_fields)
+    return finish(fields, payload)
 
 
 def solution(mesh):

time: 132 us -> 128 us (0.970)
  blocking collectives: 102 us -> 113 us
  starting transfers between devices: 5.37 us -> 0.08 us
  local copies, waits for them, and re-layouts: 5.03 us -> 0.01 us
  waiting for transfers between devices: 2.68 us -> 0.01 us
    all_to_all x4 -> x5, blocking collectives: 102 us -> 113 us  [exchange(): return lax.all_to_all(value, axis, 0, 0, tiled=True)]
    all_to_all x1 -> x0, starting transfers between devices: 5.31 us -> none  [exchange(): return lax.all_to_all(value, axis, 0, 0, tiled=True)]
    all_to_all x1 -> x0, waiting for transfers between devices: 2.67 us -> none  [exchange(): return lax.all_to_all(value, axis, 0, 0, tiled=True)]
    reshape x4 -> x0, local copies, waits for them, and re-layouts: 2.42 us -> none  [the longest x2 0.87 us: unfolded(): parted = packed.reshape(n, half, 2, 2, blocks)]
    transpose x3 -> x0, local copies, waits for them, and re-layouts: 1.87 us -> none  [the longest x2 1.72 us: unfolded(): return parted.transpose(0, 3, 2, 1, 4).reshape(n, 2, blocks, blocks)]
    pallas_call x2, Pallas kernels: 7.28 us -> 5.79 us  [sums(): pl.pallas_call(lambda *refs: sums_kernel(groups, mine, *refs), in_specs=[...]
    pallas_call x0 -> x2, Pallas kernels: none -> 1.35 us  [the longest x1 1.34 us: finish(): pl.pallas_call(finish_kernel, in_specs=[VMEM, VMEM], out_specs=[VMEM] * 5...]
  transfers between devices with their start and end apart: 2 -> 1, of which waited for: 1 -> 0; matrix products, arithmetic and copies ran while one was open for 3% -> 0% of each run, Pallas kernels for 3% -> 2%
where the time goes in v5:
time: 128 us; the launch traced here: 126 us
  blocking collectives  113 us (88%)
  Pallas kernels  12.2 us (10%)
    all_to_all x5, blocking collectives, exchange(): return lax.all_to_all(value, axis, 0, 0, tiled=True)  113 us
    pallas_call x2, Pallas kernels, sums(): pl.pallas_call(lambda *refs: sums_kernel(groups, mine, *refs), in_specs=[...  5.79 us
  transfers between devices with their start and end apart: 1, of which 0 were waited for; matrix products, arithmetic and copies ran while one was open for 0% of the time, Pallas kernels for 2%

profile of v5, /device:TPU:6, one launch (start us, length us, event | category | flops | bytes accessed | tf_op | source)
XLA Modules:
  0.0 126.0 jit_solution(9375401077609651720)
XLA Ops:
  0.6 2.3 %cut.1 = bf16[8,1024,256]{2,1,0:T(8,128)(2,1)S(1)} custom-call(bf16[1024,2048]{1,0:T(8,128)(2,1)} %bitcast.17), custom_call_target="tpu_custom_call" | custom-call | tf_op jit(solution)/shard_map/cut/pallas_call | solution.py:50
  2.9 0.0 copy-start
  2.9 0.0 copy-start.1
  2.9 57.3 %all_to_all.25 = bf16[8,1024,256]{2,1,0:T(8,128)(2,1)S(1)} all-to-all(bf16[8,1024,256]{2,1,0:T(8,128)(2,1)S(1)} %cut.1), channel_id=1, replica_groups=mesh['line'=8,'core'=2,'freq'=8] {'freq'}, dimensions={0} | all-to-all | bytes 8388608 | tf_op jit(solution)/shard_map/all_to_all | solution.py:315
  60.2 0.0 copy-done
  60.2 0.0 copy-done.1
  60.2 2.9 %sums_other.1 = f32[64,32,128]{2,1,0:T(8,128)S(1)} custom-call(s32[2,128]{1,0:T(2,128)S(1)} %bitcast.14, bf16[128,64,256]{2,1,0:T(8,128)(2,1)S(1)} %bitcast.7, f32[1,2048]{1,0:T(1,128)S(1)} %bitcast.12), custom_call_target="tpu_custom_call" | custom-call | flops 536870912 | bytes 4194304 | tf_op jit(solution)/shard_map/sums_other/pallas_call | solution.py:95
  63.1 0.1 collective-permute-start
  63.2 2.9 %sums_own.1.one_ref = f32[64,32,128]{2,1,0:T(8,128)S(1)} custom-call(s32[2,128]{1,0:T(2,128)S(1)} %bitcast.15, bf16[128,64,256]{2,1,0:T(8,128)(2,1)S(1)} %bitcast.8, f32[1,2048]{1,0:T(1,128)S(1)} %bitcast.13), custom_call_target="tpu_custom_call" | custom-call | flops 536870912 | bytes 4194304 | tf_op jit(solution)/shard_map/sums_own/pallas_call | solution.py:95
  66.1 0.0 collective-permute-done.two_ref
  66.1 0.2 pack.1
  66.3 22.9 %all_to_all.26.refs_0_ = bf16[64,48,128]{2,1,0:T(8,128)(2,1)S(1)} all-to-all(bf16[64,48,128]{2,1,0:T(8,128)(2,1)S(1)} %pack.1), channel_id=1, replica_groups=mesh['line'=8,'core'=2,'freq'=8] {'line','freq'}, dimensions={0} | all-to-all | bytes 1572864 | tf_op jit(solution)/shard_map/all_to_all | solution.py:315
  89.3 1.0 power.1
  90.3 10.9 %all_to_all.27.payload_ref = f32[16,40,128]{2,1,0:T(8,128)S(1)} all-to-all(f32[16,40,128]{2,1,0:T(8,128)S(1)} %power.1), channel_id=1, replica_groups=mesh['line'=8,'core'=2,'freq'=8] {'line','core'}, dimensions={0} | all-to-all | bytes 655360 | tf_op jit(solution)/shard_map/all_to_all | solution.py:315
  101.2 11.3 %all_to_all.28 = f32[8,16,128]{2,1,0:T(8,128)S(1)} all-to-all(f32[8,16,128]{2,1,0:T(8,128)S(1)} %spread.1), channel_id=1, replica_groups=mesh['line'=8,'core'=2,'freq'=8] {'freq'}, dimensions={0} | all-to-all | bytes 131072 | tf_op jit(solution)/shard_map/all_to_all | solution.py:315
  112.6 1.5 %modes.1 = bf16[32,8,256]{2,1,0:T(8,128)(2,1)S(1)} custom-call(s32[2,128]{1,0:T(2,128)S(1)} %bitcast.16, bf16[128,64,256]{2,1,0:T(8,128)(2,1)S(1)} %bitcast.9, f32[128,128]{1,0:T(8,128)S(1)} %bitcast.11), custom_call_target="tpu_custom_call" | custom-call | flops 8388608 | bytes 4194304 | tf_op jit(solution)/shard_map/modes/pallas_call | solution.py:231
  114.1 10.5 %all_to_all.29.fields_ref = bf16[8,32,256]{2,1,0:T(8,128)(2,1)S(1)} all-to-all(bf16[8,32,256]{2,1,0:T(8,128)(2,1)S(1)} %bitcast.10), channel_id=1, replica_groups=mesh['line'=8,'core'=2,'freq'=8] {'freq'}, dimensions={0} | all-to-all | bytes 262144 | tf_op jit(solution)/shard_map/all_to_all | solution.py:315
  124.7 1.3 %finish.1 = (f32[16,2,32,32]{3,2,1,0:T(8,128)}, f32[16,2,32,32]{3,2,1,0:T(8,128)}, f32[16,2,32]{2,1,0:T(2,128)}, f32[1,16]{1,0:T(1,128)}, f32[16,2,2048]{2,1,0:T(2,128)}) custom-call(bf16[8,32,256]{2,1,0:T(8,128)(2,1)S(1)} %all_to_all.29.fields_ref, f32[16,40,128]{2,1,0:T(8,128)S(1)} %all_to_all.27.payload_ref), custom_call_target="tpu_custom_call" | custom-call | tf_op jit(solution)/shard_map/finish/pallas_call | solution.py:297
  (1 shorter events, 0.0 us)
Async XLA Ops:
  2.9 57.3 %copy-start = (f32[2048]{0:T(1024)S(1)}, f32[2048]{0:T(1024)}, u32[]{:S(2)}) copy-start(f32[2048]{0:T(1024)} %param.4) | copy-start | bytes 24580
  2.9 57.3 %copy-start.1 = (s32[128,2]{0,1:T(2,128)S(1)}, s32[128,2]{0,1:T(2,128)}, u32[]{:S(2)}) copy-start(s32[128,2]{0,1:T(2,128)} %param.5) | copy-start | bytes 3076
  63.1 3.0 %collective-permute-start = (f32[64,32,128]{2,1,0:T(8,128)S(1)}, f32[64,32,128]{2,1,0:T(8,128)S(1)}, u32[]{:S(2)}, u32[]{:S(2)}) collective-permute-start(f32[64,32,128]{2,1,0:T(8,128)S(1)} %sums_other.1), channel_id=1, source_target_pairs={{0,8},{8,0},{1,9},{9,1},{2,10},{10,2},{3,11},{11,3},{4,12},{12,4},... | collective-permute-start | bytes 3145736 | tf_op jit(solution)/shard_map/ppermute | solution.py:320

commit v6 on v4

--- a/solution.py
+++ b/solution.py
@@ -19,13 +19,11 @@
     return pltpu.CompilerParams(vmem_limit_bytes=mib << 20)
 
 
-def gram(left_re, left_im, right):
+def gram(left, right):
     half = right.shape[0] // 2
-    right_re, right_im = right[:half], right[half:]
-    turned = jnp.concatenate([right_im, -right_re], axis=0)
-    return lax.dot_general(
-        left_re, right, NT, preferred_element_type=jnp.float32
-    ) + lax.dot_general(left_im, turned, NT, preferred_element_type=jnp.float32)
+    joined = lax.dot_general(left, right, NT, preferred_element_type=jnp.float32)
+    upper, lower = joined[:half], joined[half:]
+    return upper + jnp.concatenate([lower[:, half:], -lower[:, :half]], axis=1)
 
 
 def folded(matrix):
@@ -81,13 +79,14 @@
         ar, ai, br, bi = first[:half], first[half:], second[:half], second[half:]
         re = ((ar * br - ai * bi) * weights).astype(jnp.bfloat16)
         im = ((ar * bi + ai * br) * weights).astype(jnp.bfloat16)
-        out_ref[j, :fold] = folded(gram(re, im, spectra_ref[m]))
+        product = jnp.concatenate([re, im], axis=0)
+        out_ref[j, :fold] = folded(gram(product, spectra_ref[m]))
         own = spectra_ref[t]
         weighted = (own.astype(jnp.float32) * weights).astype(jnp.bfloat16)
-        out_ref[j, fold:] = folded(gram(weighted[:half], weighted[half:], own))
+        out_ref[j, fold:] = folded(gram(weighted, own))
         return carry
 
-    lax.fori_loop(0, count, step, 0, unroll=16)
+    lax.fori_loop(0, count, step, 0, unroll=32)
 
 
 def sums(triads, spectra, weights, groups, mine):
@@ -135,7 +134,11 @@
     )(one, two)
 
 
-def power_kernel(scales, parts_ref, out_ref):
+def high_of(value):
+    return value.astype(jnp.bfloat16).astype(jnp.float32)
+
+
+def power_kernel(scales, groups, parts_ref, out_ref, held_ref):
     half = parts_ref.shape[1] // 3
     added = jnp.sum(parts_ref[...].astype(jnp.float32), axis=0)
     total = (added[:half] + added[half : 2 * half]) * scales[0]
@@ -173,29 +176,44 @@
     top = jnp.sum(re * re + im * im, axis=0, keepdims=True)
     energy = top / (blocks * (square(one) + 1.0))
     row = jnp.where(lower, one * sign, energy)
-    tail = jnp.broadcast_to(row, (out_ref.shape[1] - 2 * half, 4 * blocks))
+    row_high, total_high = high_of(row), high_of(total)
+    row_rest, total_rest = row - row_high, total - total_high
+    for g in range(groups):
+        held_ref[8 * g : 8 * g + 1] = row_high
+        held_ref[8 * g + 1 : 8 * g + 2] = row_rest
+        held_ref[8 * g + 2 : 8 * g + 4] = total_high[2 * g : 2 * g + 2]
+        held_ref[8 * g + 4 : 8 * g + 6] = total_rest[2 * g : 2 * g + 2]
+        held_ref[8 * g + 6 : 8 * g + 8] = density[2 * g : 2 * g + 2]
+    slices = [held_ref[8 * g : 8 * g + 8].astype(out_ref.dtype) for g in range(groups)]
     for d in range(out_ref.shape[0]):
-        out_ref[d, :half] = total
-        out_ref[d, half : 2 * half] = density
-        out_ref[d, 2 * half :] = tail
-
-
-def power(parts, scales, lines):
+        out_ref[d] = slices[d % groups]
+
+
+def power(parts, scales, groups, count):
     _, rows, lanes = parts.shape
-    return pl.pallas_call(
-        lambda *refs: power_kernel(scales, *refs),
+    assert rows == 6 * groups
+    return pl.pallas_call(
+        lambda *refs: power_kernel(scales, groups, *refs),
         in_specs=[VMEM],
         out_specs=VMEM,
-        out_shape=jax.ShapeDtypeStruct((lines, 2 * rows // 3 + 8, lanes), jnp.float32),
+        out_shape=jax.ShapeDtypeStruct((count, 8, lanes), jnp.bfloat16),
+        scratch_shapes=[pltpu.VMEM((8 * groups, lanes), jnp.float32)],
         compiler_params=params(8),
         name="power",
     )(parts)
 
 
-def modes_kernel(triads_ref, spectra_ref, vectors_ref, out_ref, pairs_ref):
+def modes_kernel(triads_ref, spectra_ref, slices_ref, out_ref, pairs_ref, wide_ref, vectors_ref):
     total = spectra_ref.shape[0]
-    count, lanes = vectors_ref.shape
+    count, height, lanes = slices_ref.shape
+    groups = out_ref.shape[0]
+    per_group = count // groups
     blocks = lanes // 4
+    wide_ref[...] = slices_ref[...].astype(jnp.float32).reshape(count * height, lanes)
+    for g in range(groups):
+        vectors_ref[g * per_group : (g + 1) * per_group] = wide_ref[
+            pl.ds(g * height, per_group, stride=groups * height), :
+        ]
     lane = lax.broadcasted_iota(jnp.int32, (1, lanes), 1)
     lower = lane < 2 * blocks
     sign = jnp.where(lax.rem(lax.div(lane, blocks), 2) == 0, 1.0, -1.0)
@@ -207,33 +225,45 @@
     pairs_ref[pl.ds(0, count, stride=2), :] = jnp.where(keep, rows * sign, 0.0)
     pairs_ref[pl.ds(1, count, stride=2), :] = jnp.where(keep, swapped, 0.0)
     early = lax.broadcasted_iota(jnp.int32, (2 * EACH, 1), 0) < EACH
-
-    def step(s, carry):
-        picked = []
-        for q in range(EACH):
-            t = s * EACH + q
-            m = lax.rem(triads_ref[0, t] + triads_ref[1, t], total)
-            picked.append(spectra_ref[m])
-        right = jnp.concatenate(picked, axis=0)
-        pair = pairs_ref[pl.ds(pl.multiple_of(s * 2 * EACH, 2 * EACH), 2 * EACH), :]
-        left = jnp.concatenate(
-            [jnp.where(early, pair, 0.0), jnp.where(early, 0.0, pair)], axis=1
-        ).astype(jnp.bfloat16)
-        out_ref[s] = jnp.dot(left, right, preferred_element_type=jnp.float32)
-        return carry
-
-    lax.fori_loop(0, count // EACH, step, 0, unroll=16)
-
-
-def modes(triads, spectra, vectors):
-    count, lanes = vectors.shape
+    steps = per_group // EACH
+    after = 2 * steps * 2 * EACH
+    for g in range(groups):
+        for s in range(steps):
+            picked = []
+            for q in range(EACH):
+                t = g * per_group + s * EACH + q
+                m = lax.rem(triads_ref[0, t] + triads_ref[1, t], total)
+                picked.append(spectra_ref[m])
+            right = jnp.concatenate(picked, axis=0)
+            pair = pairs_ref[pl.ds(2 * (g * per_group + s * EACH), 2 * EACH), :]
+            left = jnp.concatenate(
+                [jnp.where(early, pair, 0.0), jnp.where(early, 0.0, pair)], axis=1
+            ).astype(jnp.bfloat16)
+            mixed = jnp.dot(left, right, preferred_element_type=jnp.float32)
+            mixed = mixed.astype(out_ref.dtype)
+            for h in range(2):
+                at = (h * steps + s) * 2 * EACH
+                out_ref[g, at : at + 2 * EACH] = mixed[:, h * lanes : (h + 1) * lanes]
+        for i in range(per_group):
+            at = after + height * i
+            out_ref[g, at : at + height] = slices_ref[i * groups + g]
+
+
+def modes(triads, spectra, slices, groups):
+    count, height, lanes = slices.shape
     total, rows, points = spectra.shape
+    assert points == 2 * lanes
+    per_group = count // groups
     return pl.pallas_call(
         modes_kernel,
         in_specs=[SMEM, VMEM, VMEM],
         out_specs=VMEM,
-        out_shape=jax.ShapeDtypeStruct((count // EACH, 2 * EACH, points), jnp.float32),
-        scratch_shapes=[pltpu.VMEM((2 * count, lanes), jnp.float32)],
+        out_shape=jax.ShapeDtypeStruct((groups, (4 + height) * per_group, lanes), jnp.bfloat16),
+        scratch_shapes=[
+            pltpu.VMEM((2 * count, lanes), jnp.float32),
+            pltpu.VMEM((count * height, lanes), jnp.float32),
+            pltpu.VMEM((count, lanes), jnp.float32),
+        ],
         cost_estimate=pl.CostEstimate(
             flops=count * rows * points * 4,
             bytes_accessed=spectra.size * 2,
@@ -241,7 +271,78 @@
         ),
         compiler_params=params(),
         name="modes",
-    )(triads, spectra, vectors)
+    )(triads, spectra, slices)
+
+
+def finish_kernel(got_ref, bis_ref, dens_ref, vec_ref, energy_ref, modes_ref, wide_ref):
+    groups, _, lanes = got_ref.shape
+    count = modes_ref.shape[0]
+    blocks = lanes // 4
+    fold = blocks // 2
+    first = 4 * count
+
+    def spread(value, row, to_ref):
+        for part in range(4):
+            low, ri = part // 2, part % 2
+            at = ri * blocks + low * fold + row
+            piece = value[:, part * blocks : (part + 1) * blocks]
+            to_ref[pl.ds(at, count, stride=2 * blocks), :] = piece
+
+    for g in range(groups):
+        wide_ref[...] = got_ref[g, first:].astype(jnp.float32)
+
+        def every(k):
+            return wide_ref[pl.ds(k, count, stride=8), :]
+
+        for r in range(2):
+            spread(every(2 + r) + every(4 + r), 2 * g + r, bis_ref)
+            spread(every(6 + r), 2 * g + r, dens_ref)
+        if g == 0:
+            rows = every(0) + every(1)
+            for t in range(count):
+                for ri in range(2):
+                    part = rows[t : t + 1, ri * blocks : (ri + 1) * blocks]
+                    vec_ref[t, ri : ri + 1, :] = part
+            lane = lax.broadcasted_iota(jnp.int32, rows.shape, 1)
+            index = lax.broadcasted_iota(jnp.int32, rows.shape, 0)
+            own = jnp.where(lane == index + 2 * blocks, rows, 0.0)
+            line = pltpu.roll(jnp.sum(own, axis=0, keepdims=True), 2 * blocks, 1)
+            energy_ref[...] = line[:, :count]
+        for h in range(2):
+            block = got_ref[g, h * 2 * count : (h + 1) * 2 * count].astype(jnp.float32)
+            at = (2 * g + h) * lanes
+            for t in range(count):
+                modes_ref[t, :, at : at + lanes] = block[2 * t : 2 * t + 2]
+
+
+def finish(got):
+    groups, rows, lanes = got.shape
+    count = rows // 12
+    blocks = lanes // 4
+    square = jax.ShapeDtypeStruct((count * 2 * blocks, blocks), jnp.float32)
+    bispectrum, density, vectors, energy, mode_fields = pl.pallas_call(
+        finish_kernel,
+        in_specs=[VMEM],
+        out_specs=[VMEM] * 5,
+        out_shape=[
+            square,
+            square,
+            jax.ShapeDtypeStruct((count, 2, blocks), jnp.float32),
+            jax.ShapeDtypeStruct((1, count), jnp.float32),
+            jax.ShapeDtypeStruct((count, 2, 2 * groups * lanes), jnp.float32),
+        ],
+        scratch_shapes=[pltpu.VMEM((8 * count, lanes), jnp.float32)],
+        compiler_params=params(8),
+        name="finish",
+    )(got)
+    whole = (count, 2, blocks, blocks)
+    return (
+        bispectrum.reshape(whole),
+        density.reshape(whole),
+        vectors,
+        energy.reshape(count),
+        mode_fields,
+    )
 
 
 def exchange(value, axis):
@@ -251,13 +352,6 @@
 def swap(value, axis, bit):
     length = lax.axis_size(axis)
     return lax.ppermute(value, axis, [(i, i ^ bit) for i in range(length)])
-
-
-def unfolded(packed):
-    n, half, lanes = packed.shape
-    blocks = 2 * half
-    parted = packed.reshape(n, half, 2, 2, blocks)
-    return parted.transpose(0, 3, 2, 1, 4).reshape(n, 2, blocks, blocks)
 
 
 def local(spectra, weights, triads):
@@ -280,20 +374,10 @@
     parts = exchange(parts, ("line", "freq"))
 
     scales = (1.0 / math.sqrt(blocks * point_count), 1.0 / point_count)
-    payload = power(parts, scales, lines * cores)
-    payload = exchange(payload, ("line", "core"))
-    fold = blocks // 2
-    rows = payload[:, 2 * fold]
-    vectors = exchange(jnp.broadcast_to(rows[None], (groups, *rows.shape)), "freq")
-    fields = modes(triads, turned, vectors.reshape(groups * per_group, -1))
-    fields = exchange(fields.reshape(groups, 2 * per_group, share), "freq")
-
-    bispectrum = unfolded(payload[:, :fold])
-    density = unfolded(payload[:, fold : 2 * fold])
-    out_vectors = rows[:, : 2 * blocks].reshape(per_group, 2, blocks)
-    energy = rows[:, 2 * blocks]
-    mode_fields = fields.swapaxes(0, 1).reshape(per_group, 2, points)
-    return (bispectrum, density, out_vectors, energy, mode_fields)
+    slices = power(parts, scales, groups, lines * cores * groups)
+    slices = exchange(slices, ("line", "core", "freq"))
+    got = exchange(modes(triads, turned, slices, groups), "freq")
+    return finish(got)
 
 
 def solution(mesh):

time: 132 us -> 124 us (0.939)
  blocking collectives: 102 us -> 108 us
  starting transfers between devices: 5.37 us -> 0.08 us
  local copies, waits for them, and re-layouts: 5.03 us -> 0.01 us
  waiting for transfers between devices: 2.68 us -> 0.01 us
    all_to_all x4, blocking collectives: 102 us -> 108 us  [exchange(): return lax.all_to_all(value, axis, 0, 0, tiled=True)]
    all_to_all x1 -> x0, starting transfers between devices: 5.31 us -> none  [exchange(): return lax.all_to_all(value, axis, 0, 0, tiled=True)]
    all_to_all x1 -> x0, waiting for transfers between devices: 2.67 us -> none  [exchange(): return lax.all_to_all(value, axis, 0, 0, tiled=True)]
    reshape x4 -> x0, local copies, waits for them, and re-layouts: 2.42 us -> none  [the longest x2 0.87 us: unfolded(): parted = packed.reshape(n, half, 2, 2, blocks)]
    pallas_call x1 -> x2, Pallas kernels: 1.03 us -> 3.08 us  [the longest x1 2.02 us: finish(): pl.pallas_call(finish_kernel, in_specs=[VMEM], out_specs=[VMEM] * 5, out_...]
    transpose x3 -> x0, local copies, waits for them, and re-layouts: 1.87 us -> none  [the longest x2 1.72 us: unfolded(): return parted.transpose(0, 3, 2, 1, 4).reshape(n, 2, blocks, blocks)]
    pallas_call x2, Pallas kernels: 7.28 us -> 5.79 us  [sums(): pl.pallas_call(lambda *refs: sums_kernel(groups, mine, *refs), in_specs=[...]
  transfers between devices with their start and end apart: 2 -> 1, of which waited for: 1 -> 0; matrix products, arithmetic and copies ran while one was open for 3% -> 0% of each run, Pallas kernels for 3% -> 2%
where the time goes in v6:
time: 124 us; the launch traced here: 122 us
  blocking collectives  108 us (87%)
  Pallas kernels  12.7 us (10%)
    all_to_all x4, blocking collectives, exchange(): return lax.all_to_all(value, axis, 0, 0, tiled=True)  108 us
    pallas_call x2, Pallas kernels, sums(): pl.pallas_call(lambda *refs: sums_kernel(groups, mine, *refs), in_specs=[...  5.79 us
  transfers between devices with their start and end apart: 1, of which 0 were waited for; matrix products, arithmetic and copies ran while one was open for 0% of the time, Pallas kernels for 2%

profile of v6, /device:TPU:6, one launch (start us, length us, event | category | flops | bytes accessed | tf_op | source)
XLA Modules:
  0.0 121.8 jit_solution(15042269339396156365)
XLA Ops:
  0.6 2.3 %cut.1 = bf16[8,1024,256]{2,1,0:T(8,128)(2,1)S(1)} custom-call(bf16[1024,2048]{1,0:T(8,128)(2,1)} %bitcast.15), custom_call_target="tpu_custom_call" | custom-call | tf_op jit(solution)/shard_map/cut/pallas_call | solution.py:50
  2.9 0.0 copy-start
  2.9 0.0 copy-start.1
  2.9 57.3 %all_to_all.20 = bf16[8,1024,256]{2,1,0:T(8,128)(2,1)S(1)} all-to-all(bf16[8,1024,256]{2,1,0:T(8,128)(2,1)S(1)} %cut.1), channel_id=1, replica_groups=mesh['line'=8,'core'=2,'freq'=8] {'freq'}, dimensions={0} | all-to-all | bytes 8388608 | tf_op jit(solution)/shard_map/all_to_all | solution.py:349
  60.2 0.0 copy-done
  60.2 0.0 copy-done.1
  60.2 2.9 %sums_other.1 = f32[64,32,128]{2,1,0:T(8,128)S(1)} custom-call(s32[2,128]{1,0:T(2,128)S(1)} %bitcast.12, bf16[128,64,256]{2,1,0:T(8,128)(2,1)S(1)} %bitcast.7, f32[1,2048]{1,0:T(1,128)S(1)} %bitcast.10), custom_call_target="tpu_custom_call" | custom-call | flops 536870912 | bytes 4194304 | tf_op jit(solution)/shard_map/sums_other/pallas_call | solution.py:95
  63.1 0.1 collective-permute-start
  63.2 2.9 %sums_own.1.one_ref = f32[64,32,128]{2,1,0:T(8,128)S(1)} custom-call(s32[2,128]{1,0:T(2,128)S(1)} %bitcast.13, bf16[128,64,256]{2,1,0:T(8,128)(2,1)S(1)} %bitcast.8, f32[1,2048]{1,0:T(1,128)S(1)} %bitcast.11), custom_call_target="tpu_custom_call" | custom-call | flops 536870912 | bytes 4194304 | tf_op jit(solution)/shard_map/sums_own/pallas_call | solution.py:95
  66.1 0.0 collective-permute-done.two_ref
  66.1 0.2 pack.1
  66.3 22.9 %all_to_all.21.refs_0_ = bf16[64,48,128]{2,1,0:T(8,128)(2,1)S(1)} all-to-all(bf16[64,48,128]{2,1,0:T(8,128)(2,1)S(1)} %pack.1), channel_id=1, replica_groups=mesh['line'=8,'core'=2,'freq'=8] {'line','freq'}, dimensions={0} | all-to-all | bytes 1572864 | tf_op jit(solution)/shard_map/all_to_all | solution.py:349
  89.3 1.1 power.1
  90.3 14.5 %all_to_all.22.slices_ref = bf16[128,8,128]{2,1,0:T(8,128)(2,1)S(1)} all-to-all(bf16[128,8,128]{2,1,0:T(8,128)(2,1)S(1)} %power.1), channel_id=1, replica_groups=mesh['line'=8,'core'=2,'freq'=8] {'line','core','freq'}, dimensions={0} | all-to-all | bytes 524288 | tf_op jit(solution)/shard_map/all_to_all | solution.py:349
  104.8 1.4 %modes.1 = bf16[8,192,128]{2,1,0:T(8,128)(2,1)S(1)} custom-call(s32[2,128]{1,0:T(2,128)S(1)} %bitcast.14, bf16[128,64,256]{2,1,0:T(8,128)(2,1)S(1)} %bitcast.9, bf16[128,8,128]{2,1,0:T(8,128)(2,1)S(1)} %all_to_all.22.slices_ref), custom_call_target="tpu_custom_call" | custom-call | flops 8388608 | bytes 4194304 | tf_op jit(solution)/shard_map/modes/pallas_call | solution.py:257
  106.2 13.6 %all_to_all.23.got_ref = bf16[8,192,128]{2,1,0:T(8,128)(2,1)S(1)} all-to-all(bf16[8,192,128]{2,1,0:T(8,128)(2,1)S(1)} %modes.1), channel_id=1, replica_groups=mesh['line'=8,'core'=2,'freq'=8] {'freq'}, dimensions={0} | all-to-all | bytes 786432 | tf_op jit(solution)/shard_map/all_to_all | solution.py:349
  119.8 2.0 %finish.1 = (f32[1024,32]{1,0:T(8,128)}, f32[1024,32]{1,0:T(8,128)}, f32[16,2,32]{2,1,0:T(2,128)}, f32[1,16]{1,0:T(1,128)}, f32[16,2,2048]{2,1,0:T(2,128)}) custom-call(bf16[8,192,128]{2,1,0:T(8,128)(2,1)S(1)} %all_to_all.23.got_ref), custom_call_target="tpu_custom_call" | custom-call | tf_op jit(solution)/shard_map/finish/pallas_call | solution.py:323
Async XLA Ops:
  2.9 57.3 %copy-start = (f32[2048]{0:T(1024)S(1)}, f32[2048]{0:T(1024)}, u32[]{:S(2)}) copy-start(f32[2048]{0:T(1024)} %param.4) | copy-start | bytes 24580
  2.9 57.3 %copy-start.1 = (s32[128,2]{0,1:T(2,128)S(1)}, s32[128,2]{0,1:T(2,128)}, u32[]{:S(2)}) copy-start(s32[128,2]{0,1:T(2,128)} %param.5) | copy-start | bytes 3076
  63.1 3.0 %collective-permute-start = (f32[64,32,128]{2,1,0:T(8,128)S(1)}, f32[64,32,128]{2,1,0:T(8,128)S(1)}, u32[]{:S(2)}, u32[]{:S(2)}) collective-permute-start(f32[64,32,128]{2,1,0:T(8,128)S(1)} %sums_other.1), channel_id=1, source_target_pairs={{0,8},{8,0},{1,9},{9,1},{2,10},{10,2},{3,11},{11,3},{4,12},{12,4},... | collective-permute-start | bytes 3145736 | tf_op jit(solution)/shard_map/ppermute | solution.py:354

commit v7 on v6

--- a/solution.py
+++ b/solution.py
@@ -244,9 +244,10 @@
             for h in range(2):
                 at = (h * steps + s) * 2 * EACH
                 out_ref[g, at : at + 2 * EACH] = mixed[:, h * lanes : (h + 1) * lanes]
-        for i in range(per_group):
-            at = after + height * i
-            out_ref[g, at : at + height] = slices_ref[i * groups + g]
+        for k in range(2, height):
+            at = after + (k - 2) * per_group
+            part = wide_ref[pl.ds(g * height + k, per_group, stride=groups * height), :]
+            out_ref[g, at : at + per_group] = part.astype(out_ref.dtype)
 
 
 def modes(triads, spectra, slices, groups):
@@ -258,7 +259,7 @@
         modes_kernel,
         in_specs=[SMEM, VMEM, VMEM],
         out_specs=VMEM,
-        out_shape=jax.ShapeDtypeStruct((groups, (4 + height) * per_group, lanes), jnp.bfloat16),
+        out_shape=jax.ShapeDtypeStruct((groups, (2 + height) * per_group, lanes), jnp.bfloat16),
         scratch_shapes=[
             pltpu.VMEM((2 * count, lanes), jnp.float32),
             pltpu.VMEM((count * height, lanes), jnp.float32),
@@ -274,7 +275,9 @@
     )(triads, spectra, slices)
 
 
-def finish_kernel(got_ref, bis_ref, dens_ref, vec_ref, energy_ref, modes_ref, wide_ref):
+def finish_kernel(
+    got_ref, slices_ref, bis_ref, dens_ref, vec_ref, energy_ref, modes_ref, bis, dens, fields, held, sems
+):
     groups, _, lanes = got_ref.shape
     count = modes_ref.shape[0]
     blocks = lanes // 4
@@ -289,52 +292,73 @@
             to_ref[pl.ds(at, count, stride=2 * blocks), :] = piece
 
     for g in range(groups):
-        wide_ref[...] = got_ref[g, first:].astype(jnp.float32)
-
-        def every(k):
-            return wide_ref[pl.ds(k, count, stride=8), :]
-
+        parts = [
+            got_ref[g, first + k * count : first + (k + 1) * count].astype(jnp.float32)
+            for k in range(6)
+        ]
         for r in range(2):
-            spread(every(2 + r) + every(4 + r), 2 * g + r, bis_ref)
-            spread(every(6 + r), 2 * g + r, dens_ref)
-        if g == 0:
-            rows = every(0) + every(1)
-            for t in range(count):
-                for ri in range(2):
-                    part = rows[t : t + 1, ri * blocks : (ri + 1) * blocks]
-                    vec_ref[t, ri : ri + 1, :] = part
-            lane = lax.broadcasted_iota(jnp.int32, rows.shape, 1)
-            index = lax.broadcasted_iota(jnp.int32, rows.shape, 0)
-            own = jnp.where(lane == index + 2 * blocks, rows, 0.0)
-            line = pltpu.roll(jnp.sum(own, axis=0, keepdims=True), 2 * blocks, 1)
-            energy_ref[...] = line[:, :count]
+            spread(parts[r] + parts[2 + r], 2 * g + r, bis)
+            spread(parts[4 + r], 2 * g + r, dens)
+    copies = [
+        pltpu.make_async_copy(bis, bis_ref, sems.at[0]),
+        pltpu.make_async_copy(dens, dens_ref, sems.at[1]),
+        pltpu.make_async_copy(fields, modes_ref, sems.at[2]),
+    ]
+    copies[0].start()
+    copies[1].start()
+    for g in range(groups):
         for h in range(2):
             block = got_ref[g, h * 2 * count : (h + 1) * 2 * count].astype(jnp.float32)
             at = (2 * g + h) * lanes
             for t in range(count):
-                modes_ref[t, :, at : at + lanes] = block[2 * t : 2 * t + 2]
-
-
-def finish(got):
+                fields[t, :, at : at + lanes] = block[2 * t : 2 * t + 2]
+    copies[2].start()
+
+    group = lax.axis_index("freq")
+    for t in range(count):
+        own = slices_ref[t * groups + group].astype(jnp.float32)
+        held[t : t + 1] = own[0:1] + own[1:2]
+    rows = held[...]
+    for t in range(count):
+        for ri in range(2):
+            vec_ref[t, ri : ri + 1, :] = rows[t : t + 1, ri * blocks : (ri + 1) * blocks]
+    lane = lax.broadcasted_iota(jnp.int32, rows.shape, 1)
+    index = lax.broadcasted_iota(jnp.int32, rows.shape, 0)
+    own = jnp.where(lane == index + 2 * blocks, rows, 0.0)
+    line = pltpu.roll(jnp.sum(own, axis=0, keepdims=True), 2 * blocks, 1)
+    energy_ref[...] = line[:, :count]
+    for copy in copies:
+        copy.wait()
+
+
+def finish(got, slices):
     groups, rows, lanes = got.shape
-    count = rows // 12
+    count = rows // 10
     blocks = lanes // 4
-    square = jax.ShapeDtypeStruct((count * 2 * blocks, blocks), jnp.float32)
+    square = (count * 2 * blocks, blocks)
+    wide = (count, 2, 2 * groups * lanes)
+    there = pl.BlockSpec(memory_space=pltpu.HBM)
     bispectrum, density, vectors, energy, mode_fields = pl.pallas_call(
         finish_kernel,
-        in_specs=[VMEM],
-        out_specs=[VMEM] * 5,
+        in_specs=[VMEM, VMEM],
+        out_specs=[there, there, VMEM, VMEM, there],
         out_shape=[
-            square,
-            square,
+            jax.ShapeDtypeStruct(square, jnp.float32),
+            jax.ShapeDtypeStruct(square, jnp.float32),
             jax.ShapeDtypeStruct((count, 2, blocks), jnp.float32),
             jax.ShapeDtypeStruct((1, count), jnp.float32),
-            jax.ShapeDtypeStruct((count, 2, 2 * groups * lanes), jnp.float32),
+            jax.ShapeDtypeStruct(wide, jnp.float32),
         ],
-        scratch_shapes=[pltpu.VMEM((8 * count, lanes), jnp.float32)],
+        scratch_shapes=[
+            pltpu.VMEM(square, jnp.float32),
+            pltpu.VMEM(square, jnp.float32),
+            pltpu.VMEM(wide, jnp.float32),
+            pltpu.VMEM((count, lanes), jnp.float32),
+            pltpu.SemaphoreType.DMA((3,)),
+        ],
         compiler_params=params(8),
         name="finish",
-    )(got)
+    )(got, slices)
     whole = (count, 2, blocks, blocks)
     return (
         bispectrum.reshape(whole),
@@ -377,7 +401,7 @@
     slices = power(parts, scales, groups, lines * cores * groups)
     slices = exchange(slices, ("line", "core", "freq"))
     got = exchange(modes(triads, turned, slices, groups), "freq")
-    return finish(got)
+    return finish(got, slices)
 
 
 def solution(mesh):

time: 124 us -> 124 us (level)
  no operation moved by 1% of the time
where the time goes in v7:
time: 124 us; the launch traced here: 122 us
  blocking collectives  108 us (87%)
  Pallas kernels  13.3 us (11%)
    all_to_all x4, blocking collectives, exchange(): return lax.all_to_all(value, axis, 0, 0, tiled=True)  108 us
    pallas_call x2, Pallas kernels, sums(): pl.pallas_call(lambda *refs: sums_kernel(groups, mine, *refs), in_specs=[...  5.79 us
    pallas_call x1, Pallas kernels, finish(): pl.pallas_call(finish_kernel, in_specs=[VMEM, VMEM], out_specs=[there, th...  2.6 us
  transfers between devices with their start and end apart: 1, of which 0 were waited for; matrix products, arithmetic and copies ran while one was open for 0% of the time, Pallas kernels for 2%

profile of v7, /device:TPU:6, one launch (start us, length us, event | category | flops | bytes accessed | tf_op | source)
XLA Modules:
  0.0 121.8 jit_solution(6187775922262187249)
XLA Ops:
  0.6 2.3 %cut.1 = bf16[8,1024,256]{2,1,0:T(8,128)(2,1)S(1)} custom-call(bf16[1024,2048]{1,0:T(8,128)(2,1)} %bitcast.15), custom_call_target="tpu_custom_call" | custom-call | tf_op jit(solution)/shard_map/cut/pallas_call | solution.py:50
  2.9 0.0 copy-start
  2.9 0.0 copy-start.1
  2.9 57.3 %all_to_all.20 = bf16[8,1024,256]{2,1,0:T(8,128)(2,1)S(1)} all-to-all(bf16[8,1024,256]{2,1,0:T(8,128)(2,1)S(1)} %cut.1), channel_id=1, replica_groups=mesh['line'=8,'core'=2,'freq'=8] {'freq'}, dimensions={0} | all-to-all | bytes 8388608 | tf_op jit(solution)/shard_map/all_to_all | solution.py:373
  60.2 0.0 copy-done
  60.2 0.0 copy-done.1
  60.2 2.9 %sums_other.1 = f32[64,32,128]{2,1,0:T(8,128)S(1)} custom-call(s32[2,128]{1,0:T(2,128)S(1)} %bitcast.12, bf16[128,64,256]{2,1,0:T(8,128)(2,1)S(1)} %bitcast.7, f32[1,2048]{1,0:T(1,128)S(1)} %bitcast.10), custom_call_target="tpu_custom_call" | custom-call | flops 536870912 | bytes 4194304 | tf_op jit(solution)/shard_map/sums_other/pallas_call | solution.py:95
  63.1 0.1 collective-permute-start
  63.2 2.9 %sums_own.1.one_ref = f32[64,32,128]{2,1,0:T(8,128)S(1)} custom-call(s32[2,128]{1,0:T(2,128)S(1)} %bitcast.13, bf16[128,64,256]{2,1,0:T(8,128)(2,1)S(1)} %bitcast.8, f32[1,2048]{1,0:T(1,128)S(1)} %bitcast.11), custom_call_target="tpu_custom_call" | custom-call | flops 536870912 | bytes 4194304 | tf_op jit(solution)/shard_map/sums_own/pallas_call | solution.py:95
  66.1 0.0 collective-permute-done.two_ref
  66.1 0.2 pack.1
  66.3 22.9 %all_to_all.21.refs_0_ = bf16[64,48,128]{2,1,0:T(8,128)(2,1)S(1)} all-to-all(bf16[64,48,128]{2,1,0:T(8,128)(2,1)S(1)} %pack.1), channel_id=1, replica_groups=mesh['line'=8,'core'=2,'freq'=8] {'line','freq'}, dimensions={0} | all-to-all | bytes 1572864 | tf_op jit(solution)/shard_map/all_to_all | solution.py:373
  89.3 1.1 power.1
  90.3 14.5 %all_to_all.22.slices_ref = bf16[128,8,128]{2,1,0:T(8,128)(2,1)S(1)} all-to-all(bf16[128,8,128]{2,1,0:T(8,128)(2,1)S(1)} %power.1), channel_id=1, replica_groups=mesh['line'=8,'core'=2,'freq'=8] {'line','core','freq'}, dimensions={0} | all-to-all | bytes 524288 | tf_op jit(solution)/shard_map/all_to_all | solution.py:373
  104.8 1.4 %modes.1 = bf16[8,160,128]{2,1,0:T(8,128)(2,1)S(1)} custom-call(s32[2,128]{1,0:T(2,128)S(1)} %bitcast.14, bf16[128,64,256]{2,1,0:T(8,128)(2,1)S(1)} %bitcast.9, bf16[128,8,128]{2,1,0:T(8,128)(2,1)S(1)} %all_to_all.22.slices_ref), custom_call_target="tpu_custom_call" | custom-call | flops 8388608 | bytes 4194304 | tf_op jit(solution)/shard_map/modes/pallas_call | solution.py:258
  106.2 13.0 %all_to_all.23.got_ref = bf16[8,160,128]{2,1,0:T(8,128)(2,1)S(1)} all-to-all(bf16[8,160,128]{2,1,0:T(8,128)(2,1)S(1)} %modes.1), channel_id=1, replica_groups=mesh['line'=8,'core'=2,'freq'=8] {'freq'}, dimensions={0} | all-to-all | bytes 655360 | tf_op jit(solution)/shard_map/all_to_all | solution.py:373
  119.2 2.6 %finish.1 = (f32[1024,32]{1,0:T(8,128)}, f32[1024,32]{1,0:T(8,128)}, f32[16,2,32]{2,1,0:T(2,128)}, f32[1,16]{1,0:T(1,128)}, f32[16,2,2048]{2,1,0:T(2,128)}) custom-call(bf16[8,160,128]{2,1,0:T(8,128)(2,1)S(1)} %all_to_all.23.got_ref, bf16[128,8,128]{2,1,0:T(8,128)(2,1)S(1)} %all_to_all.22.slices_ref), custom_call_target="tpu_custom_call" | custom-call | tf_op jit(solution)/shard_map/finish/pallas_call | solution.py:341
Async XLA Ops:
  2.9 57.3 %copy-start = (f32[2048]{0:T(1024)S(1)}, f32[2048]{0:T(1024)}, u32[]{:S(2)}) copy-start(f32[2048]{0:T(1024)} %param.4) | copy-start | bytes 24580
  2.9 57.3 %copy-start.1 = (s32[128,2]{0,1:T(2,128)S(1)}, s32[128,2]{0,1:T(2,128)}, u32[]{:S(2)}) copy-start(s32[128,2]{0,1:T(2,128)} %param.5) | copy-start | bytes 3076
  63.1 3.0 %collective-permute-start = (f32[64,32,128]{2,1,0:T(8,128)S(1)}, f32[64,32,128]{2,1,0:T(8,128)S(1)}, u32[]{:S(2)}, u32[]{:S(2)}) collective-permute-start(f32[64,32,128]{2,1,0:T(8,128)S(1)} %sums_other.1), channel_id=1, source_target_pairs={{0,8},{8,0},{1,9},{9,1},{2,10},{10,2},{3,11},{11,3},{4,12},{12,4},... | collective-permute-start | bytes 3145736 | tf_op jit(solution)/shard_map/ppermute | solution.py:378

commit v8 on v7

--- a/solution.py
+++ b/solution.py
@@ -10,6 +10,7 @@
 
 ITERS = 3
 EACH = 4
+STEP = 24
 NT = (((1,), (1,)), ((), ()))
 VMEM = pl.BlockSpec(memory_space=pltpu.VMEM)
 SMEM = pl.BlockSpec(memory_space=pltpu.SMEM)
@@ -276,7 +277,7 @@
 
 
 def finish_kernel(
-    got_ref, slices_ref, bis_ref, dens_ref, vec_ref, energy_ref, modes_ref, bis, dens, fields, held, sems
+    got_ref, slices_ref, bis_ref, dens_ref, vec_ref, energy_ref, modes_ref, bis, dens, held
 ):
     groups, _, lanes = got_ref.shape
     count = modes_ref.shape[0]
@@ -284,35 +285,27 @@
     fold = blocks // 2
     first = 4 * count
 
-    def spread(value, row, to_ref):
-        for part in range(4):
-            low, ri = part // 2, part % 2
-            at = ri * blocks + low * fold + row
-            piece = value[:, part * blocks : (part + 1) * blocks]
-            to_ref[pl.ds(at, count, stride=2 * blocks), :] = piece
-
     for g in range(groups):
         parts = [
             got_ref[g, first + k * count : first + (k + 1) * count].astype(jnp.float32)
             for k in range(6)
         ]
         for r in range(2):
-            spread(parts[r] + parts[2 + r], 2 * g + r, bis)
-            spread(parts[4 + r], 2 * g + r, dens)
-    copies = [
-        pltpu.make_async_copy(bis, bis_ref, sems.at[0]),
-        pltpu.make_async_copy(dens, dens_ref, sems.at[1]),
-        pltpu.make_async_copy(fields, modes_ref, sems.at[2]),
-    ]
-    copies[0].start()
-    copies[1].start()
-    for g in range(groups):
+            rows = pl.ds(2 * g + r, count, stride=STEP)
+            bis[rows, :] = parts[r] + parts[2 + r]
+            dens[rows, :] = parts[4 + r]
         for h in range(2):
             block = got_ref[g, h * 2 * count : (h + 1) * 2 * count].astype(jnp.float32)
             at = (2 * g + h) * lanes
             for t in range(count):
-                fields[t, :, at : at + lanes] = block[2 * t : 2 * t + 2]
-    copies[2].start()
+                modes_ref[t, :, at : at + lanes] = block[2 * t : 2 * t + 2]
+    for t in range(count):
+        for packed, to_ref in ((bis, bis_ref), (dens, dens_ref)):
+            square = packed[STEP * t : STEP * t + fold]
+            for part in range(4):
+                low, ri = part // 2, part % 2
+                piece = square[:, part * blocks : (part + 1) * blocks]
+                to_ref[t, ri, low * fold : (low + 1) * fold, :] = piece
 
     group = lax.axis_index("freq")
     for t in range(count):
@@ -327,46 +320,33 @@
     own = jnp.where(lane == index + 2 * blocks, rows, 0.0)
     line = pltpu.roll(jnp.sum(own, axis=0, keepdims=True), 2 * blocks, 1)
     energy_ref[...] = line[:, :count]
-    for copy in copies:
-        copy.wait()
 
 
 def finish(got, slices):
     groups, rows, lanes = got.shape
     count = rows // 10
     blocks = lanes // 4
-    square = (count * 2 * blocks, blocks)
-    wide = (count, 2, 2 * groups * lanes)
-    there = pl.BlockSpec(memory_space=pltpu.HBM)
+    square = jax.ShapeDtypeStruct((count, 2, blocks, blocks), jnp.float32)
     bispectrum, density, vectors, energy, mode_fields = pl.pallas_call(
         finish_kernel,
         in_specs=[VMEM, VMEM],
-        out_specs=[there, there, VMEM, VMEM, there],
+        out_specs=[VMEM] * 5,
         out_shape=[
-            jax.ShapeDtypeStruct(square, jnp.float32),
-            jax.ShapeDtypeStruct(square, jnp.float32),
+            square,
+            square,
             jax.ShapeDtypeStruct((count, 2, blocks), jnp.float32),
             jax.ShapeDtypeStruct((1, count), jnp.float32),
-            jax.ShapeDtypeStruct(wide, jnp.float32),
+            jax.ShapeDtypeStruct((count, 2, 2 * groups * lanes), jnp.float32),
         ],
         scratch_shapes=[
-            pltpu.VMEM(square, jnp.float32),
-            pltpu.VMEM(square, jnp.float32),
-            pltpu.VMEM(wide, jnp.float32),
+            pltpu.VMEM((count * STEP, lanes), jnp.float32),
+            pltpu.VMEM((count * STEP, lanes), jnp.float32),
             pltpu.VMEM((count, lanes), jnp.float32),
-            pltpu.SemaphoreType.DMA((3,)),
         ],
         compiler_params=params(8),
         name="finish",
     )(got, slices)
-    whole = (count, 2, blocks, blocks)
-    return (
-        bispectrum.reshape(whole),
-        density.reshape(whole),
-        vectors,
-        energy.reshape(count),
-        mode_fields,
-    )
+    return (bispectrum, density, vectors, energy.reshape(count), mode_fields)
 
 
 def exchange(value, axis):

time: 124 us -> 122 us (0.984)
    pallas_call x1, Pallas kernels: 2.6 us -> 1.35 us  [finish(): pl.pallas_call(finish_kernel, in_specs=[VMEM, VMEM], out_specs=[VMEM] * 5...]
where the time goes in v8:
time: 122 us; the launch traced here: 121 us
  blocking collectives  108 us (89%)
  Pallas kernels  12.1 us (10%)
    all_to_all x4, blocking collectives, exchange(): return lax.all_to_all(value, axis, 0, 0, tiled=True)  108 us
    pallas_call x2, Pallas kernels, sums(): pl.pallas_call(lambda *refs: sums_kernel(groups, mine, *refs), in_specs=[...  5.79 us
  transfers between devices with their start and end apart: 1, of which 0 were waited for; matrix products, arithmetic and copies ran while one was open for 0% of the time, Pallas kernels for 2%

profile of v8, /device:TPU:6, one launch (start us, length us, event | category | flops | bytes accessed | tf_op | source)
XLA Modules:
  0.0 120.6 jit_solution(5194680960140007807)
XLA Ops:
  0.6 2.3 %cut.1 = bf16[8,1024,256]{2,1,0:T(8,128)(2,1)S(1)} custom-call(bf16[1024,2048]{1,0:T(8,128)(2,1)} %bitcast.13), custom_call_target="tpu_custom_call" | custom-call | tf_op jit(solution)/shard_map/cut/pallas_call | solution.py:51
  2.9 0.0 copy-start
  2.9 0.0 copy-start.1
  2.9 57.3 %all_to_all.20 = bf16[8,1024,256]{2,1,0:T(8,128)(2,1)S(1)} all-to-all(bf16[8,1024,256]{2,1,0:T(8,128)(2,1)S(1)} %cut.1), channel_id=1, replica_groups=mesh['line'=8,'core'=2,'freq'=8] {'freq'}, dimensions={0} | all-to-all | bytes 8388608 | tf_op jit(solution)/shard_map/all_to_all | solution.py:353
  60.2 0.0 copy-done
  60.2 0.0 copy-done.1
  60.2 2.9 %sums_other.1 = f32[64,32,128]{2,1,0:T(8,128)S(1)} custom-call(s32[2,128]{1,0:T(2,128)S(1)} %bitcast.10, bf16[128,64,256]{2,1,0:T(8,128)(2,1)S(1)} %bitcast.5, f32[1,2048]{1,0:T(1,128)S(1)} %bitcast.8), custom_call_target="tpu_custom_call" | custom-call | flops 536870912 | bytes 4194304 | tf_op jit(solution)/shard_map/sums_other/pallas_call | solution.py:96
  63.1 0.1 collective-permute-start
  63.2 2.9 %sums_own.1.one_ref = f32[64,32,128]{2,1,0:T(8,128)S(1)} custom-call(s32[2,128]{1,0:T(2,128)S(1)} %bitcast.11, bf16[128,64,256]{2,1,0:T(8,128)(2,1)S(1)} %bitcast.6, f32[1,2048]{1,0:T(1,128)S(1)} %bitcast.9), custom_call_target="tpu_custom_call" | custom-call | flops 536870912 | bytes 4194304 | tf_op jit(solution)/shard_map/sums_own/pallas_call | solution.py:96
  66.1 0.0 collective-permute-done.two_ref
  66.1 0.2 pack.1
  66.3 22.9 %all_to_all.21.refs_0_ = bf16[64,48,128]{2,1,0:T(8,128)(2,1)S(1)} all-to-all(bf16[64,48,128]{2,1,0:T(8,128)(2,1)S(1)} %pack.1), channel_id=1, replica_groups=mesh['line'=8,'core'=2,'freq'=8] {'line','freq'}, dimensions={0} | all-to-all | bytes 1572864 | tf_op jit(solution)/shard_map/all_to_all | solution.py:353
  89.3 1.1 power.1
  90.3 14.5 %all_to_all.22.slices_ref = bf16[128,8,128]{2,1,0:T(8,128)(2,1)S(1)} all-to-all(bf16[128,8,128]{2,1,0:T(8,128)(2,1)S(1)} %power.1), channel_id=1, replica_groups=mesh['line'=8,'core'=2,'freq'=8] {'line','core','freq'}, dimensions={0} | all-to-all | bytes 524288 | tf_op jit(solution)/shard_map/all_to_all | solution.py:353
  104.8 1.4 %modes.1 = bf16[8,160,128]{2,1,0:T(8,128)(2,1)S(1)} custom-call(s32[2,128]{1,0:T(2,128)S(1)} %bitcast.12, bf16[128,64,256]{2,1,0:T(8,128)(2,1)S(1)} %bitcast.7, bf16[128,8,128]{2,1,0:T(8,128)(2,1)S(1)} %all_to_all.22.slices_ref), custom_call_target="tpu_custom_call" | custom-call | flops 8388608 | bytes 4194304 | tf_op jit(solution)/shard_map/modes/pallas_call | solution.py:259
  106.2 13.0 %all_to_all.23.got_ref = bf16[8,160,128]{2,1,0:T(8,128)(2,1)S(1)} all-to-all(bf16[8,160,128]{2,1,0:T(8,128)(2,1)S(1)} %modes.1), channel_id=1, replica_groups=mesh['line'=8,'core'=2,'freq'=8] {'freq'}, dimensions={0} | all-to-all | bytes 655360 | tf_op jit(solution)/shard_map/all_to_all | solution.py:353
  119.2 1.4 %finish.1 = (f32[16,2,32,32]{3,2,1,0:T(8,128)}, f32[16,2,32,32]{3,2,1,0:T(8,128)}, f32[16,2,32]{2,1,0:T(2,128)}, f32[1,16]{1,0:T(1,128)}, f32[16,2,2048]{2,1,0:T(2,128)}) custom-call(bf16[8,160,128]{2,1,0:T(8,128)(2,1)S(1)} %all_to_all.23.got_ref, bf16[128,8,128]{2,1,0:T(8,128)(2,1)S(1)} %all_to_all.22.slices_ref), custom_call_target="tpu_custom_call" | custom-call | tf_op jit(solution)/shard_map/finish/pallas_call | solution.py:330
Async XLA Ops:
  2.9 57.3 %copy-start = (f32[2048]{0:T(1024)S(1)}, f32[2048]{0:T(1024)}, u32[]{:S(2)}) copy-start(f32[2048]{0:T(1024)} %param.4) | copy-start | bytes 24580
  2.9 57.3 %copy-start.1 = (s32[128,2]{0,1:T(2,128)S(1)}, s32[128,2]{0,1:T(2,128)}, u32[]{:S(2)}) copy-start(s32[128,2]{0,1:T(2,128)} %param.5) | copy-start | bytes 3076
  63.1 3.0 %collective-permute-start = (f32[64,32,128]{2,1,0:T(8,128)S(1)}, f32[64,32,128]{2,1,0:T(8,128)S(1)}, u32[]{:S(2)}, u32[]{:S(2)}) collective-permute-start(f32[64,32,128]{2,1,0:T(8,128)S(1)} %sums_other.1), channel_id=1, source_target_pairs={{0,8},{8,0},{1,9},{9,1},{2,10},{10,2},{3,11},{11,3},{4,12},{12,4},... | collective-permute-start | bytes 3145736 | tf_op jit(solution)/shard_map/ppermute | solution.py:358

commit v9 on v8

--- a/solution.py
+++ b/solution.py
@@ -27,9 +27,16 @@
     return upper + jnp.concatenate([lower[:, half:], -lower[:, :half]], axis=1)
 
 
-def folded(matrix):
-    half = matrix.shape[0] // 2
-    return jnp.concatenate([matrix[:half], matrix[half:]], axis=1)
+def gram_of_itself(left, right):
+    half = right.shape[0] // 2
+    joined = lax.dot_general(left, right, NT, preferred_element_type=jnp.float32)
+    upper, lower = joined[:half], joined[half:]
+    return (upper[:, :half] - lower[:, :half]) + (upper[:, half:] + lower[:, half:])
+
+
+def folded(matrix, count):
+    rows = matrix.shape[0] // count
+    return jnp.concatenate([matrix[k * rows : (k + 1) * rows] for k in range(count)], axis=1)
 
 
 def cut_kernel(rows_ref, out_ref, sems):
@@ -81,10 +88,10 @@
         re = ((ar * br - ai * bi) * weights).astype(jnp.bfloat16)
         im = ((ar * bi + ai * br) * weights).astype(jnp.bfloat16)
         product = jnp.concatenate([re, im], axis=0)
-        out_ref[j, :fold] = folded(gram(product, spectra_ref[m]))
+        out_ref[j, :fold] = folded(gram(product, spectra_ref[m]), 2)
         own = spectra_ref[t]
         weighted = (own.astype(jnp.float32) * weights).astype(jnp.bfloat16)
-        out_ref[j, fold:] = folded(gram(weighted, own))
+        out_ref[j, fold:] = folded(gram_of_itself(weighted, own), 4)
         return carry
 
     lax.fori_loop(0, count, step, 0, unroll=32)
@@ -97,7 +104,7 @@
         lambda *refs: sums_kernel(groups, mine, *refs),
         in_specs=[SMEM, VMEM, VMEM],
         out_specs=VMEM,
-        out_shape=jax.ShapeDtypeStruct((count, rows // 2, 2 * rows), jnp.float32),
+        out_shape=jax.ShapeDtypeStruct((count, 3 * rows // 8, 2 * rows), jnp.float32),
         cost_estimate=pl.CostEstimate(
             flops=count * rows * rows * points * 8,
             bytes_accessed=spectra.size * 2,
@@ -109,7 +116,7 @@
 
 
 def pack_kernel(one_ref, two_ref, out_ref):
-    fold = one_ref.shape[1] // 2
+    fold = 2 * one_ref.shape[1] // 3
 
     def step(j, carry):
         both = one_ref[j] + two_ref[j]
@@ -129,18 +136,14 @@
         pack_kernel,
         in_specs=[VMEM, VMEM],
         out_specs=VMEM,
-        out_shape=jax.ShapeDtypeStruct((count, 3 * rows // 2, lanes), jnp.bfloat16),
+        out_shape=jax.ShapeDtypeStruct((count, 5 * rows // 3, lanes), jnp.bfloat16),
         compiler_params=params(),
         name="pack",
     )(one, two)
 
 
-def high_of(value):
-    return value.astype(jnp.bfloat16).astype(jnp.float32)
-
-
 def power_kernel(scales, groups, parts_ref, out_ref, held_ref):
-    half = parts_ref.shape[1] // 3
+    half = 2 * parts_ref.shape[1] // 5
     added = jnp.sum(parts_ref[...].astype(jnp.float32), axis=0)
     total = (added[:half] + added[half : 2 * half]) * scales[0]
     density = added[2 * half :] * scales[1]
@@ -177,27 +180,23 @@
     top = jnp.sum(re * re + im * im, axis=0, keepdims=True)
     energy = top / (blocks * (square(one) + 1.0))
     row = jnp.where(lower, one * sign, energy)
-    row_high, total_high = high_of(row), high_of(total)
-    row_rest, total_rest = row - row_high, total - total_high
     for g in range(groups):
-        held_ref[8 * g : 8 * g + 1] = row_high
-        held_ref[8 * g + 1 : 8 * g + 2] = row_rest
-        held_ref[8 * g + 2 : 8 * g + 4] = total_high[2 * g : 2 * g + 2]
-        held_ref[8 * g + 4 : 8 * g + 6] = total_rest[2 * g : 2 * g + 2]
-        held_ref[8 * g + 6 : 8 * g + 8] = density[2 * g : 2 * g + 2]
-    slices = [held_ref[8 * g : 8 * g + 8].astype(out_ref.dtype) for g in range(groups)]
+        held_ref[8 * g : 8 * g + 1] = row
+        held_ref[8 * g + 1 : 8 * g + 3] = total[2 * g : 2 * g + 2]
+        held_ref[8 * g + 3 : 8 * g + 4] = density[g : g + 1]
+    slices = [held_ref[8 * g : 8 * g + 4].astype(out_ref.dtype) for g in range(groups)]
     for d in range(out_ref.shape[0]):
         out_ref[d] = slices[d % groups]
 
 
 def power(parts, scales, groups, count):
     _, rows, lanes = parts.shape
-    assert rows == 6 * groups
+    assert rows == 5 * groups
     return pl.pallas_call(
         lambda *refs: power_kernel(scales, groups, *refs),
         in_specs=[VMEM],
         out_specs=VMEM,
-        out_shape=jax.ShapeDtypeStruct((count, 8, lanes), jnp.bfloat16),
+        out_shape=jax.ShapeDtypeStruct((count, 4, lanes), jnp.bfloat16),
         scratch_shapes=[pltpu.VMEM((8 * groups, lanes), jnp.float32)],
         compiler_params=params(8),
         name="power",
@@ -210,10 +209,11 @@
     groups = out_ref.shape[0]
     per_group = count // groups
     blocks = lanes // 4
-    wide_ref[...] = slices_ref[...].astype(jnp.float32).reshape(count * height, lanes)
+    for d in range(count):
+        wide_ref[8 * d : 8 * d + height] = slices_ref[d].astype(jnp.float32)
     for g in range(groups):
         vectors_ref[g * per_group : (g + 1) * per_group] = wide_ref[
-            pl.ds(g * height, per_group, stride=groups * height), :
+            pl.ds(8 * g, per_group, stride=8 * groups), :
         ]
     lane = lax.broadcasted_iota(jnp.int32, (1, lanes), 1)
     lower = lane < 2 * blocks
@@ -245,9 +245,9 @@
             for h in range(2):
                 at = (h * steps + s) * 2 * EACH
                 out_ref[g, at : at + 2 * EACH] = mixed[:, h * lanes : (h + 1) * lanes]
-        for k in range(2, height):
-            at = after + (k - 2) * per_group
-            part = wide_ref[pl.ds(g * height + k, per_group, stride=groups * height), :]
+        for k in range(1, height):
+            at = after + (k - 1) * per_group
+            part = wide_ref[pl.ds(8 * g + k, per_group, stride=8 * groups), :]
             out_ref[g, at : at + per_group] = part.astype(out_ref.dtype)
 
 
@@ -260,10 +260,10 @@
         modes_kernel,
         in_specs=[SMEM, VMEM, VMEM],
         out_specs=VMEM,
-        out_shape=jax.ShapeDtypeStruct((groups, (2 + height) * per_group, lanes), jnp.bfloat16),
+        out_shape=jax.ShapeDtypeStruct((groups, (3 + height) * per_group, lanes), jnp.bfloat16),
         scratch_shapes=[
             pltpu.VMEM((2 * count, lanes), jnp.float32),
-            pltpu.VMEM((count * height, lanes), jnp.float32),
+            pltpu.VMEM((8 * count, lanes), jnp.float32),
             pltpu.VMEM((count, lanes), jnp.float32),
         ],
         cost_estimate=pl.CostEstimate(
@@ -288,29 +288,41 @@
     for g in range(groups):
         parts = [
             got_ref[g, first + k * count : first + (k + 1) * count].astype(jnp.float32)
-            for k in range(6)
+            for k in range(3)
         ]
         for r in range(2):
-            rows = pl.ds(2 * g + r, count, stride=STEP)
-            bis[rows, :] = parts[r] + parts[2 + r]
-            dens[rows, :] = parts[4 + r]
+            bis[pl.ds(2 * g + r, count, stride=STEP), :] = parts[r]
+        dens[pl.ds(g, count, stride=groups), :] = parts[2]
         for h in range(2):
             block = got_ref[g, h * 2 * count : (h + 1) * 2 * count].astype(jnp.float32)
             at = (2 * g + h) * lanes
             for t in range(count):
                 modes_ref[t, :, at : at + lanes] = block[2 * t : 2 * t + 2]
     for t in range(count):
-        for packed, to_ref in ((bis, bis_ref), (dens, dens_ref)):
-            square = packed[STEP * t : STEP * t + fold]
-            for part in range(4):
-                low, ri = part // 2, part % 2
-                piece = square[:, part * blocks : (part + 1) * blocks]
-                to_ref[t, ri, low * fold : (low + 1) * fold, :] = piece
+        square = bis[STEP * t : STEP * t + fold]
+        for part in range(4):
+            low, ri = part // 2, part % 2
+            piece = square[:, part * blocks : (part + 1) * blocks]
+            bis_ref[t, ri, low * fold : (low + 1) * fold, :] = piece
+    for t in range(0, count, 4):
+        runs = []
+        for q in range(4):
+            pieces = [
+                dens[groups * (t + k) : groups * (t + k + 1), q * blocks : (q + 1) * blocks]
+                for k in range(4)
+            ]
+            runs.append(jnp.concatenate(pieces, axis=1))
+        four = jnp.concatenate(runs, axis=0)
+        turned = four.T
+        for k in range(4):
+            square = four[:, k * blocks : (k + 1) * blocks]
+            other = turned[k * blocks : (k + 1) * blocks, :]
+            dens_ref[t + k, 0] = 0.5 * (square + other)
+            dens_ref[t + k, 1] = 0.5 * (square - other)
 
     group = lax.axis_index("freq")
     for t in range(count):
-        own = slices_ref[t * groups + group].astype(jnp.float32)
-        held[t : t + 1] = own[0:1] + own[1:2]
+        held[t : t + 1] = slices_ref[t * groups + group].astype(jnp.float32)[0:1]
     rows = held[...]
     for t in range(count):
         for ri in range(2):
@@ -324,7 +336,7 @@
 
 def finish(got, slices):
     groups, rows, lanes = got.shape
-    count = rows // 10
+    count = rows // 7
     blocks = lanes // 4
     square = jax.ShapeDtypeStruct((count, 2, blocks, blocks), jnp.float32)
     bispectrum, density, vectors, energy, mode_fields = pl.pallas_call(
@@ -340,7 +352,7 @@
         ],
         scratch_shapes=[
             pltpu.VMEM((count * STEP, lanes), jnp.float32),
-            pltpu.VMEM((count * STEP, lanes), jnp.float32),
+            pltpu.VMEM((count * groups, lanes), jnp.float32),
             pltpu.VMEM((count, lanes), jnp.float32),
         ],
         compiler_params=params(8),

time: 122 us -> 119 us (0.975)
  blocking collectives: 108 us -> 104 us
    all_to_all x4, blocking collectives: 108 us -> 104 us  [exchange(): return lax.all_to_all(value, axis, 0, 0, tiled=True)]
where the time goes in v9:
time: 119 us; the launch traced here: 117 us
  blocking collectives  104 us (87%)
  Pallas kernels  12.5 us (11%)
    all_to_all x4, blocking collectives, exchange(): return lax.all_to_all(value, axis, 0, 0, tiled=True)  104 us
    pallas_call x2, Pallas kernels, sums(): pl.pallas_call(lambda *refs: sums_kernel(groups, mine, *refs), in_specs=[...  5.86 us
  transfers between devices with their start and end apart: 1, of which 0 were waited for; matrix products, arithmetic and copies ran while one was open for 0% of the time, Pallas kernels for 2%

profile of v9, /device:TPU:6, one launch (start us, length us, event | category | flops | bytes accessed | tf_op | source)
XLA Modules:
  0.0 117.5 jit_solution(12671972218582817311)
XLA Ops:
  0.6 2.3 %cut.1 = bf16[8,1024,256]{2,1,0:T(8,128)(2,1)S(1)} custom-call(bf16[1024,2048]{1,0:T(8,128)(2,1)} %bitcast.13), custom_call_target="tpu_custom_call" | custom-call | tf_op jit(solution)/shard_map/cut/pallas_call | solution.py:58
  2.9 0.0 copy-start
  2.9 0.0 copy-start.1
  2.9 57.3 %all_to_all.20 = bf16[8,1024,256]{2,1,0:T(8,128)(2,1)S(1)} all-to-all(bf16[8,1024,256]{2,1,0:T(8,128)(2,1)S(1)} %cut.1), channel_id=1, replica_groups=mesh['line'=8,'core'=2,'freq'=8] {'freq'}, dimensions={0} | all-to-all | bytes 8388608 | tf_op jit(solution)/shard_map/all_to_all | solution.py:365
  60.2 0.0 copy-done
  60.2 0.0 copy-done.1
  60.2 2.9 %sums_other.1 = f32[64,24,128]{2,1,0:T(8,128)S(1)} custom-call(s32[2,128]{1,0:T(2,128)S(1)} %bitcast.10, bf16[128,64,256]{2,1,0:T(8,128)(2,1)S(1)} %bitcast.5, f32[1,2048]{1,0:T(1,128)S(1)} %bitcast.8), custom_call_target="tpu_custom_call" | custom-call | flops 536870912 | bytes 4194304 | tf_op jit(solution)/shard_map/sums_other/pallas_call | solution.py:103
  63.2 0.1 collective-permute-start
  63.2 2.9 %sums_own.1.one_ref = f32[64,24,128]{2,1,0:T(8,128)S(1)} custom-call(s32[2,128]{1,0:T(2,128)S(1)} %bitcast.11, bf16[128,64,256]{2,1,0:T(8,128)(2,1)S(1)} %bitcast.6, f32[1,2048]{1,0:T(1,128)S(1)} %bitcast.9), custom_call_target="tpu_custom_call" | custom-call | flops 536870912 | bytes 4194304 | tf_op jit(solution)/shard_map/sums_own/pallas_call | solution.py:103
  66.2 0.0 collective-permute-done.two_ref
  66.2 0.2 pack.1
  66.3 21.6 %all_to_all.21.refs_0_ = bf16[64,40,128]{2,1,0:T(8,128)(2,1)S(1)} all-to-all(bf16[64,40,128]{2,1,0:T(8,128)(2,1)S(1)} %pack.1), channel_id=1, replica_groups=mesh['line'=8,'core'=2,'freq'=8] {'line','freq'}, dimensions={0} | all-to-all | bytes 1310720 | tf_op jit(solution)/shard_map/all_to_all | solution.py:365
  88.0 1.1 power.1
  89.0 13.4 %all_to_all.22.slices_ref = bf16[128,4,128]{2,1,0:T(4,128)(2,1)S(1)} all-to-all(bf16[128,4,128]{2,1,0:T(4,128)(2,1)S(1)} %power.1), channel_id=1, replica_groups=mesh['line'=8,'core'=2,'freq'=8] {'line','core','freq'}, dimensions={0} | all-to-all | bytes 262144 | tf_op jit(solution)/shard_map/all_to_all | solution.py:365
  102.5 1.4 %modes.1 = bf16[8,112,128]{2,1,0:T(8,128)(2,1)S(1)} custom-call(s32[2,128]{1,0:T(2,128)S(1)} %bitcast.12, bf16[128,64,256]{2,1,0:T(8,128)(2,1)S(1)} %bitcast.7, bf16[128,4,128]{2,1,0:T(4,128)(2,1)S(1)} %all_to_all.22.slices_ref), custom_call_target="tpu_custom_call" | custom-call | flops 8388608 | bytes 4194304 | tf_op jit(solution)/shard_map/modes/pallas_call | solution.py:259
  103.8 11.8 %all_to_all.23.got_ref = bf16[8,112,128]{2,1,0:T(8,128)(2,1)S(1)} all-to-all(bf16[8,112,128]{2,1,0:T(8,128)(2,1)S(1)} %modes.1), channel_id=1, replica_groups=mesh['line'=8,'core'=2,'freq'=8] {'freq'}, dimensions={0} | all-to-all | bytes 458752 | tf_op jit(solution)/shard_map/all_to_all | solution.py:365
  115.7 1.8 %finish.1 = (f32[16,2,32,32]{3,2,1,0:T(8,128)}, f32[16,2,32,32]{3,2,1,0:T(8,128)}, f32[16,2,32]{2,1,0:T(2,128)}, f32[1,16]{1,0:T(1,128)}, f32[16,2,2048]{2,1,0:T(2,128)}) custom-call(bf16[8,112,128]{2,1,0:T(8,128)(2,1)S(1)} %all_to_all.23.got_ref, bf16[128,4,128]{2,1,0:T(4,128)(2,1)S(1)} %all_to_all.22.slices_ref), custom_call_target="tpu_custom_call" | custom-call | tf_op jit(solution)/shard_map/finish/pallas_call | solution.py:342
Async XLA Ops:
  2.9 57.3 %copy-start = (f32[2048]{0:T(1024)S(1)}, f32[2048]{0:T(1024)}, u32[]{:S(2)}) copy-start(f32[2048]{0:T(1024)} %param.4) | copy-start | bytes 24580
  2.9 57.3 %copy-start.1 = (s32[128,2]{0,1:T(2,128)S(1)}, s32[128,2]{0,1:T(2,128)}, u32[]{:S(2)}) copy-start(s32[128,2]{0,1:T(2,128)} %param.5) | copy-start | bytes 3076
  63.2 3.0 %collective-permute-start = (f32[64,24,128]{2,1,0:T(8,128)S(1)}, f32[64,24,128]{2,1,0:T(8,128)S(1)}, u32[]{:S(2)}, u32[]{:S(2)}) collective-permute-start(f32[64,24,128]{2,1,0:T(8,128)S(1)} %sums_other.1), channel_id=1, source_target_pairs={{0,8},{8,0},{1,9},{9,1},{2,10},{10,2},{3,11},{11,3},{4,12},{12,4},... | collective-permute-start | bytes 2359304 | tf_op jit(solution)/shard_map/ppermute | solution.py:370
